TPU v7x, 32 devices: a whole 2x2x4 slice. The times are simulated.
32 devices in a mesh: dp: 8 (over z, x), ctx: 4 (over y, core).
Axes of the slice: x: 2, y: 2, z: 4, core: 2. Of those that a mesh axis runs over, the one named last changes fastest.
Arguments:
- tokens: bfloat16 [8192, 1536], P(('dp', 'ctx')), may hold values from -6 to 6
- norm_attn: float32 [1536], P(('dp', 'ctx')), may hold values from 0.5 to 1.5
- w_qkv: bfloat16 [3072, 1536], P(('dp', 'ctx')), may hold values from -1 to 1
- w_out: bfloat16 [1536, 1536], P(('dp', 'ctx')), may hold values from -0.875 to 0.875
- norm_mlp: float32 [1536], P(('dp', 'ctx')), may hold values from 0.5 to 1.5
- w_gate_up: bfloat16 [8192, 1536], P(('dp', 'ctx')), may hold values from -0.15625 to 0.15625
- w_down: bfloat16 [1536, 4096], P(('dp', 'ctx')), may hold values from -0.09375 to 0.09375
- cotangent: bfloat16 [8192, 1536], P(('dp', 'ctx')), may hold values from -6 to 6
- seq_lengths: int32 [8, 2], P('dp'), may hold values from 1 to 768, 1024 in all within a row
- block_slot: int32 [8, 8], P('dp'), may hold values from 0 to 7, each once within a row
Outputs:
- result: bfloat16 [8192, 1536], P(('dp', 'ctx'))
- grad_input: float32 [8192, 1536], P(('dp', 'ctx'))
- grad_norm_attn: float32 [1536], P(('dp', 'ctx'))
- grad_qkv: float32 [3072, 1536], P(('dp', 'ctx'))
- grad_out: float32 [1536, 1536], P(('dp', 'ctx'))
- grad_norm_mlp: float32 [1536], P(('dp', 'ctx'))
- grad_gate_up: float32 [8192, 1536], P(('dp', 'ctx'))
- grad_down: float32 [1536, 4096], P(('dp', 'ctx'))
Inputs may be any that keep to these rules, and one draw needn't show every extreme that they name: `seq_lengths`: each row sums to 1024. `block_slot`: each row names every number once; ctx device c of group g holds the blocks of positions c * 2 to (c + 1) * 2 - 1 of that row.
All inputs are finite; a program needn't handle non-finite values.
Results may differ from a plain program's by a relative error of at most 0.025.
Values may be sent and summed in bfloat16 or wider, within the bound.
A program may use at most 320 MiB of HBM per device.

v0:
```python
import math

import jax
import jax.numpy as jnp
from jax import lax
from jax.sharding import PartitionSpec as P

QUERY_HEADS = 16
KEY_VALUE_HEADS = 8
HEAD_SIZE = 96
FF = 4096
BLK = 128
QUERY_FEATURES = 1536
KEY_FEATURES = 768


EPSILON = 1e-05
THETA = 100000.0
MASK_FILL = -1e30


def rope_tables(rope_pos):
    half_dim = HEAD_SIZE // 2
    exponent = jnp.arange(half_dim, dtype=jnp.float32) * (2.0 / HEAD_SIZE)
    frequency = jnp.power(jnp.float32(THETA), -exponent)
    angles = rope_pos.astype(jnp.float32)[:, None] * frequency[None, :]
    return (jnp.cos(angles)[:, None, :], jnp.sin(angles)[:, None, :])


def apply_rotation(values, cosine_table, sine_values):
    half_dim = HEAD_SIZE // 2
    first_half = values[..., :half_dim]
    second_half = values[..., half_dim:]
    return jnp.concatenate(
        [
            first_half * cosine_table - second_half * sine_values,
            second_half * cosine_table + first_half * sine_values,
        ],
        -1,
    )


def rotate_back(gradient, cosine_table, sine_values):
    half_dim = HEAD_SIZE // 2
    first_half = gradient[..., :half_dim]
    second_half = gradient[..., half_dim:]
    return jnp.concatenate(
        [
            first_half * cosine_table + second_half * sine_values,
            second_half * cosine_table - first_half * sine_values,
        ],
        -1,
    )


def positions(lengths, slot_table, first_row, count_of_rows):
    row_index = first_row + jnp.arange(count_of_rows, dtype=jnp.int32)
    block_index = row_index // BLK
    lookup = jnp.arange(slot_table.shape[0], dtype=jnp.int32)
    slot_of = jnp.sum(jnp.where(block_index[:, None] == lookup[None, :], slot_table[None, :], 0), 1)
    stream = slot_of * BLK + row_index % BLK
    seq_ends = jnp.cumsum(lengths)
    passed = stream[:, None] >= seq_ends[None, :]
    segment = jnp.sum(passed.astype(jnp.int32), 1)
    offset = jnp.sum(jnp.where(passed, seq_ends[None, :], 0), 1)
    return (stream, segment, stream - offset)


def norm_back(grad_normed, gain, source, scale):
    weighted = grad_normed * gain
    return scale * weighted - source * scale**3 * jnp.mean(weighted * source, -1, keepdims=True)


def full_product(left_side, whole_weight):
    return jnp.dot(left_side, whole_weight.T, preferred_element_type=jnp.float32)


def full_back(grad_side, whole_weight):
    return jnp.dot(grad_side, whole_weight, preferred_element_type=jnp.float32)


def owned_three(first_part, second_part, third_part):
    return (
        lax.psum_scatter(first_part, ("dp", "ctx"), scatter_dimension=0, tiled=True),
        lax.psum_scatter(second_part, ("dp", "ctx"), scatter_dimension=0, tiled=True),
        lax.psum_scatter(third_part, ("dp", "ctx"), scatter_dimension=0, tiled=True),
    )


def shards(
    tokens, norm_attn, w_qkv, w_out, norm_mlp, w_gate_up, w_down, cotangent, seq_lengths, block_slot
):
    count_of_rows = tokens.shape[0]
    ctx_place = lax.axis_index("ctx")
    lengths = seq_lengths[0]
    slot_table = block_slot[0]
    heads_ratio = QUERY_HEADS // KEY_VALUE_HEADS
    score_scale = 1.0 / math.sqrt(HEAD_SIZE)
    stream, segment, rope_pos = positions(
        lengths, slot_table, ctx_place * count_of_rows, count_of_rows
    )
    cosine_table, sine_values = rope_tables(rope_pos)
    gain_one, gain_two = (
        lax.all_gather(norm_attn, ("dp", "ctx"), axis=0, tiled=True),
        lax.all_gather(norm_mlp, ("dp", "ctx"), axis=0, tiled=True),
    )
    qkv_full, out_full = (
        lax.all_gather(w_qkv, ("dp", "ctx"), axis=0, tiled=True),
        lax.all_gather(w_out, ("dp", "ctx"), axis=0, tiled=True),
    )
    source = tokens.astype(jnp.float32)
    scale_one = lax.rsqrt(jnp.mean(source * source, -1, keepdims=True) + EPSILON)
    normed_one = (source * scale_one * gain_one).astype(jnp.bfloat16)
    projected_output = full_product(normed_one, qkv_full)
    query_rows = apply_rotation(
        projected_output[:, :QUERY_FEATURES].reshape(count_of_rows, QUERY_HEADS, HEAD_SIZE),
        cosine_table,
        sine_values,
    ).astype(jnp.bfloat16)
    keys_mine = apply_rotation(
        projected_output[:, QUERY_FEATURES : QUERY_FEATURES + KEY_FEATURES].reshape(
            count_of_rows, KEY_VALUE_HEADS, HEAD_SIZE
        ),
        cosine_table,
        sine_values,
    ).astype(jnp.bfloat16)
    values_mine = projected_output[:, QUERY_FEATURES + KEY_FEATURES :].astype(jnp.bfloat16)
    grouped_queries = query_rows.reshape(count_of_rows, KEY_VALUE_HEADS, heads_ratio, HEAD_SIZE)
    key_value = jnp.concatenate([keys_mine.reshape(count_of_rows, KEY_FEATURES), values_mine], 1)

    def masked(block_portion, start_row):
        portion_rows = block_portion.shape[0]
        key_stream, key_segment, unused = positions(lengths, slot_table, start_row, portion_rows)
        key_portion = block_portion[:, :KEY_FEATURES].reshape(
            portion_rows, KEY_VALUE_HEADS, HEAD_SIZE
        )
        value_portion = block_portion[:, KEY_FEATURES:].reshape(
            portion_rows, KEY_VALUE_HEADS, HEAD_SIZE
        )
        scores = (
            jnp.einsum(
                "rgjd,ngd->gjrn", grouped_queries, key_portion, preferred_element_type=jnp.float32
            )
            * score_scale
        )
        allowed = (
            (segment[:, None] == key_segment[None, :]) & (key_stream[None, :] <= stream[:, None])
        )[None, None]
        return (jnp.where(allowed, scores, MASK_FILL), allowed, key_portion, value_portion)

    highest_score = jnp.full((KEY_VALUE_HEADS, heads_ratio, count_of_rows), MASK_FILL, jnp.float32)
    scores, allowed, key_portion, value_portion = masked(
        lax.all_gather(key_value, "ctx", axis=0, tiled=True), jnp.int32(0)
    )
    new_high = jnp.maximum(highest_score, jnp.max(scores, -1))
    weights = jnp.where(allowed, jnp.exp(scores - new_high[..., None]), 0.0)
    weight_sum = jnp.sum(weights, -1)
    gained = jnp.einsum(
        "gjrn,ngd->rgjd",
        weights.astype(jnp.bfloat16),
        value_portion,
        preferred_element_type=jnp.float32,
    )
    accumulated = gained
    highest_score, weight_sum, accumulated = (new_high, weight_sum, accumulated)
    log_total = highest_score + jnp.log(weight_sum)
    attention_output = (
        (accumulated / jnp.transpose(weight_sum, (2, 0, 1))[..., None])
        .astype(jnp.bfloat16)
        .reshape(count_of_rows, QUERY_FEATURES)
    )
    residual = source + full_product(attention_output, out_full)
    scale_two = lax.rsqrt(jnp.mean(residual * residual, -1, keepdims=True) + EPSILON)
    normed_two = (residual * scale_two * gain_two).astype(jnp.bfloat16)
    gate_up_full, down_full = (
        lax.all_gather(w_gate_up, ("dp", "ctx"), axis=0, tiled=True),
        lax.all_gather(w_down, ("dp", "ctx"), axis=0, tiled=True),
    )
    gate_up = full_product(normed_two, gate_up_full)
    gate_part = gate_up[:, :FF]
    up_part = gate_up[:, FF:]
    sigmoid = jax.nn.sigmoid(gate_part)
    hidden = (gate_part * sigmoid * up_part).astype(jnp.bfloat16)
    mlp_term = full_product(hidden, down_full)
    result = (residual + mlp_term).astype(jnp.bfloat16)
    gate_up_full, down_full = (
        lax.all_gather(w_gate_up, ("dp", "ctx"), axis=0, tiled=True),
        lax.all_gather(w_down, ("dp", "ctx"), axis=0, tiled=True),
    )
    grad_hidden = full_back(cotangent, down_full)
    grad_down = jnp.dot(cotangent.T, hidden, preferred_element_type=jnp.float32)
    grad_gate = grad_hidden * up_part * sigmoid * (1.0 + gate_part * (1.0 - sigmoid))
    grad_upper = grad_hidden * gate_part * sigmoid
    grad_gu = jnp.concatenate([grad_gate, grad_upper], 1).astype(jnp.bfloat16)
    grad_normed_two = full_back(grad_gu, gate_up_full)
    grad_w_gate_up = jnp.dot(grad_gu.T, normed_two, preferred_element_type=jnp.float32)
    grad_gain_two = jnp.sum(grad_normed_two * residual * scale_two, 0)
    mlp_owned = owned_three(grad_gain_two, grad_w_gate_up, grad_down)
    grad_residual = cotangent.astype(jnp.float32) + norm_back(
        grad_normed_two, gain_two, residual, scale_two
    )
    grad_res_bf = grad_residual.astype(jnp.bfloat16)
    qkv_full, out_full = (
        lax.all_gather(w_qkv, ("dp", "ctx"), axis=0, tiled=True),
        lax.all_gather(w_out, ("dp", "ctx"), axis=0, tiled=True),
    )
    attention_gradient = full_back(grad_res_bf, out_full).astype(jnp.bfloat16)
    grad_w_out = jnp.dot(grad_res_bf.T, attention_output, preferred_element_type=jnp.float32)
    keys_values_all = lax.all_gather(key_value, "ctx", axis=0, tiled=True)
    grouped_gradient = attention_gradient.reshape(
        count_of_rows, KEY_VALUE_HEADS, heads_ratio, HEAD_SIZE
    )
    attention_grouped = attention_output.reshape(
        count_of_rows, KEY_VALUE_HEADS, heads_ratio, HEAD_SIZE
    )
    row_delta = jnp.transpose(
        jnp.sum(grouped_gradient.astype(jnp.float32) * attention_grouped.astype(jnp.float32), -1),
        (1, 2, 0),
    )
    grouped_rows = keys_values_all.shape[0]
    block_rows = min(512, grouped_rows)
    block_count = grouped_rows // block_rows

    def key_block(grad_queries, which_block):
        start_row = which_block * block_rows
        block_portion = lax.dynamic_slice_in_dim(keys_values_all, start_row, block_rows, 0)
        scores, allowed, key_portion, value_portion = masked(block_portion, start_row)
        weights = jnp.where(allowed, jnp.exp(scores - log_total[..., None]), 0.0)
        grad_values = jnp.einsum(
            "gjrn,rgjd->ngd",
            weights.astype(jnp.bfloat16),
            grouped_gradient,
            preferred_element_type=jnp.float32,
        )
        grad_weights = jnp.einsum(
            "rgjd,ngd->gjrn", grouped_gradient, value_portion, preferred_element_type=jnp.float32
        )
        grad_scores = (weights * (grad_weights - row_delta[..., None])).astype(jnp.bfloat16)
        grad_queries = (
            grad_queries
            + jnp.einsum(
                "gjrn,ngd->rgjd", grad_scores, key_portion, preferred_element_type=jnp.float32
            )
            * score_scale
        )
        grad_keys = (
            jnp.einsum(
                "gjrn,rgjd->ngd", grad_scores, grouped_queries, preferred_element_type=jnp.float32
            )
            * score_scale
        )
        return (
            grad_queries,
            jnp.concatenate(
                [
                    grad_keys.reshape(block_rows, KEY_FEATURES),
                    grad_values.reshape(block_rows, KEY_FEATURES),
                ],
                1,
            ),
        )

    grad_queries, key_terms = lax.scan(
        key_block,
        jnp.zeros((count_of_rows, KEY_VALUE_HEADS, heads_ratio, HEAD_SIZE), jnp.float32),
        jnp.arange(block_count, dtype=jnp.int32),
    )
    key_value_gradient = lax.psum_scatter(
        key_terms.reshape(grouped_rows, 2 * KEY_FEATURES).astype(jnp.bfloat16),
        "ctx",
        scatter_dimension=0,
        tiled=True,
    ).astype(jnp.float32)
    grad_queries = rotate_back(
        grad_queries.reshape(count_of_rows, QUERY_HEADS, HEAD_SIZE), cosine_table, sine_values
    ).reshape(count_of_rows, QUERY_FEATURES)
    grad_keys = rotate_back(
        key_value_gradient[:, :KEY_FEATURES].reshape(count_of_rows, KEY_VALUE_HEADS, HEAD_SIZE),
        cosine_table,
        sine_values,
    ).reshape(count_of_rows, KEY_FEATURES)
    grad_projected = jnp.concatenate(
        [grad_queries, grad_keys, key_value_gradient[:, KEY_FEATURES:]], 1
    ).astype(jnp.bfloat16)
    grad_normed_one = full_back(grad_projected, qkv_full)
    grad_w_qkv = jnp.dot(grad_projected.T, normed_one, preferred_element_type=jnp.float32)
    grad_gain_one = jnp.sum(grad_normed_one * source * scale_one, 0)
    grad_tokens = grad_residual + norm_back(grad_normed_one, gain_one, source, scale_one)
    attn_owned = owned_three(grad_gain_one, grad_w_qkv, grad_w_out)
    return (
        result,
        grad_tokens,
        attn_owned[0],
        attn_owned[1],
        attn_owned[2],
        mlp_owned[0],
        mlp_owned[1],
        mlp_owned[2],
    )


def solution(mesh):
    return jax.shard_map(
        shards,
        mesh=mesh,
        in_specs=(
            P(("dp", "ctx"), None),
            P(("dp", "ctx")),
            P(("dp", "ctx"), None),
            P(("dp", "ctx"), None),
            P(("dp", "ctx")),
            P(("dp", "ctx"), None),
            P(("dp", "ctx"), None),
            P(("dp", "ctx"), None),
            P("dp", None),
            P("dp", None),
        ),
        out_specs=(
            P(("dp", "ctx"), None),
            P(("dp", "ctx"), None),
            P(("dp", "ctx")),
            P(("dp", "ctx"), None),
            P(("dp", "ctx"), None),
            P(("dp", "ctx")),
            P(("dp", "ctx"), None),
            P(("dp", "ctx"), None),
        ),
        check_vma=False,
    )
```

profile of v0, /device:TPU:2, one launch (start us, length us, event | category | flops | bytes accessed | tf_op | source)
XLA Modules:
  0.0 1629.7 jit_solution(5330102366979640390)
XLA Ops:
  10.5 42.8 %all-reduce.5 = (f32[1536]{0:T(1024)S(1)}, f32[1536]{0:T(1024)S(1)}) all-reduce(f32[1536]{0:T(1024)S(1)} %dynamic-update-slice, f32[1536]{0:T(1024)S(1)} %dynamic-update-slice.1), channel_id=1, replica_groups=mesh['dp'=8,'ctx'=4] {'dp','ctx'}, use_global_device_ids=true, to_apply=%add | all-reduce | flops 3072 | bytes 24576
  56.4 37.9 %all-gather.6.cloned.1.call-done = bf16[3072,1536]{1,0:T(8,128)(2,1)} async-done(((bf16[96,1536]{1,0:T(8,128)(2,1)}), bf16[3072,1536]{1,0:T(8,128)(2,1)}) %all-gather.6.cloned.1.call-update) | async-done | bytes 9437200 | tf_op jit(solution)/shard_map/all_gather | solution.py:108
  109.4 21.0 %all-gather.8.cloned.1.call-done = bf16[1024,1536]{1,0:T(8,128)(2,1)} async-done(((bf16[256,1536]{1,0:T(8,128)(2,1)}), bf16[1024,1536]{1,0:T(8,128)(2,1)}) %all-gather.8.cloned.1.call-update) | async-done | bytes 3145744 | tf_op jit(solution)/shard_map/all_gather | solution.py:153
  147.4 49.4 %all-gather.10.cloned.1.call-done = bf16[1536,1536]{1,0:T(8,128)(2,1)} async-done(((bf16[48,1536]{1,0:T(8,128)(2,1)}), bf16[1536,1536]{1,0:T(8,128)(2,1)}) %all-gather.10.cloned.1.call-update) | async-done | bytes 4718608 | tf_op jit(solution)/shard_map/all_gather | solution.py:109
  200.8 151.2 %all-gather.12.cloned.1.call-done = bf16[8192,1536]{1,0:T(8,128)(2,1)} async-done(((bf16[256,1536]{1,0:T(8,128)(2,1)}), bf16[8192,1536]{1,0:T(8,128)(2,1)}) %all-gather.12.cloned.1.call-update) | async-done | bytes 25165840 | tf_op jit(solution)/shard_map/all_gather | solution.py:176
  352.0 13.7 fusion.66
  365.6 82.5 %all-gather.14.cloned.1.call-done = bf16[1536,4096]{1,0:T(8,128)(2,1)} async-done(((bf16[48,4096]{1,0:T(8,128)(2,1)}), bf16[1536,4096]{1,0:T(8,128)(2,1)}) %all-gather.14.cloned.1.call-update) | async-done | bytes 12582928 | tf_op jit(solution)/shard_map/all_gather | solution.py:177
  448.1 13.3 multiply_convert_fusion.1
  461.4 13.9 multiply_reduce_fusion
  480.9 60.0 %while.15 = (s32[]{:T(128)}, f32[256,8,2,96]{0,3,2,1:T(8,128)}, bf16[2,512,1536]{2,1,0:T(8,128)(2,1)}, s32[2]{0:T(128)S(1)}, bf16[1024,1536]{1,0:T(8,128)(2,1)},...) while((s32[]{:T(128)}, f32[256,8,2,96]{0,3,2,1:T(8,128)}, ...), condition=%wide.region_16.17_spmd.clone, body=%wide.region_13.16_spmd.clone.sunk | while | flops 2043966464 | bytes 114495864 | solution.py:263
  490.7 6.7 fusion.127
  520.2 6.7 fusion.127
  547.1 5.9 fusion.40
  555.6 26.4 %reduce-scatter.8.cloned.1.call-done = bf16[256,1536]{0,1:T(8,128)(2,1)} async-done(((bf16[1024,1536]{0,1:T(8,128)(2,1)}), bf16[256,1536]{0,1:T(8,128)(2,1)}) %reduce-scatter.8.cloned.1.call-update) | async-done | bytes 786448 | tf_op jit(solution)/shard_map/reduce_scatter | solution.py:268
  583.9 9.5 fusion.38
  593.5 15.0 convolution_bitcast_fusion
  608.5 25.3 %copy.83 = f32[1536,4096]{1,0:T(8,128)} copy(f32[1536,4096]{0,1:T(8,128)} %convolution_bitcast_fusion) | data formatting | bytes 50331648
  634.5 22.7 %fusion.23 = f32[8192,1536]{1,0:T(8,128)} fusion(bf16[256,4096]{1,0:T(8,128)(2,1)} %copy-done.14, bf16[256,4096]{1,0:T(8,128)(2,1)} %copy-done.13, f32[256,1536]{1,0:T(8,128)} %copy-done.6, f32[1536]{0:T(1024)S(1)} %copy-done.25, f32[256]{0:T(256)} %copy-done.30), kind=kOutput, calls=%fused_computation.54 | convolution fusion | flops 6452019200 | bytes 56105984 | tf_op jit(solution)/shard_map/dot_general | solution.py:196
  657.2 10.2 fusion.25
  667.4 8.5 fusion.34
  675.9 41.7 %all-reduce.4 = (f32[1536]{0:T(1024)S(1)}, f32[1536]{0:T(1024)S(1)}) all-reduce(f32[1536]{0:T(1024)} %get-tuple-element.305, f32[1536]{0:T(1024)} %get-tuple-element.303), channel_id=3, replica_groups=mesh['dp'=8,'ctx'=4] {'dp','ctx'}, use_global_device_ids=true, to_apply=%region_20.21.clone | all-reduce | flops 3072 | bytes 24576
  725.0 212.8 %reduce-scatter.10.cloned.1.call-done = f32[96,1536]{1,0:T(8,128)} async-done(((f32[3072,1536]{1,0:T(8,128)}), f32[96,1536]{1,0:T(8,128)}) %reduce-scatter.10.cloned.1.call-update) | async-done | bytes 589840 | tf_op jit(solution)/shard_map/reduce_scatter | solution.py:85
  937.9 249.2 %reduce-scatter.16.cloned.1.call-done = f32[48,4096]{1,0:T(8,128)} async-done(((f32[1536,4096]{1,0:T(8,128)}), f32[48,4096]{1,0:T(8,128)}) %reduce-scatter.16.cloned.1.call-update) | async-done | bytes 786448
  1187.1 435.5 %reduce-scatter.14.cloned.1.call-done = f32[256,1536]{1,0:T(8,128)} async-done(((f32[8192,1536]{1,0:T(8,128)}), f32[256,1536]{1,0:T(8,128)}) %reduce-scatter.14.cloned.1.call-update) | async-done | bytes 1572880 | tf_op jit(solution)/shard_map/reduce_scatter | solution.py:85
  (189 shorter events, 111.2 us)
Async XLA Ops:
  7.2 87.1 %all-gather.6.cloned.1.call-start = ((), (), s32[]{:S(2)}) async-start(), calls=%async_computation.5 | async-start | bytes 9732096 | tf_op jit(solution)/shard_map/all_gather | solution.py:108
  7.9 122.5 %all-gather.8.cloned.1.call-start = ((), (), s32[]{:S(2)}) async-start(), calls=%async_computation.6 | async-start | bytes 3932160 | tf_op jit(solution)/shard_map/all_gather | solution.py:153
  53.3 46.4 %copy-start.22 = (f32[1536]{0:T(1024)}, f32[1536]{0:T(1024)S(1)}, u32[]{:S(2)}) copy-start(f32[1536]{0:T(1024)S(1)} %get-tuple-element.337) | copy-start | bytes 18436
  53.3 421.9 %copy-start.24 = (f32[1536]{0:T(1024)}, f32[1536]{0:T(1024)S(1)}, u32[]{:S(2)}) copy-start(f32[1536]{0:T(1024)S(1)} %get-tuple-element.338) | copy-start | bytes 18436
  56.1 43.6 %copy-start.27 = (f32[256]{0:T(256)}, f32[256]{0:T(256)S(1)}, u32[]{:S(2)}) copy-start(f32[256]{0:T(256)S(1)} %get-tuple-element.359) | copy-start | bytes 3076
  56.4 51.6 %copy-start.18 = (f32[256,48]{0,1:T(8,128)}, f32[256,48]{0,1:T(8,128)S(1)}, u32[]{:S(2)}) copy-start(f32[256,48]{0,1:T(8,128)S(1)} %get-tuple-element.356) | copy-start | bytes 147460
  56.4 51.6 %copy-start.20 = (f32[256,48]{0,1:T(8,128)}, f32[256,48]{0,1:T(8,128)S(1)}, u32[]{:S(2)}) copy-start(f32[256,48]{0,1:T(8,128)S(1)} %get-tuple-element.357) | copy-start | bytes 147460
  103.2 93.7 %all-gather.10.cloned.1.call-start = ((), (), s32[]{:S(2)}) async-start(), calls=%async_computation.7 | async-start | bytes 4866048 | tf_op jit(solution)/shard_map/all_gather | solution.py:109
  103.9 248.1 %all-gather.12.cloned.1.call-start = ((), (), s32[]{:S(2)}) async-start(), calls=%async_computation.8 | async-start | bytes 25952256 | tf_op jit(solution)/shard_map/all_gather | solution.py:176
  104.5 343.6 %all-gather.14.cloned.1.call-start = ((), (), s32[]{:S(2)}) async-start(), calls=%async_computation.9 | async-start | bytes 12976128 | tf_op jit(solution)/shard_map/all_gather | solution.py:177
  105.1 477.0 %reduce-scatter.8.cloned.1.call-start = ((), (), s32[]{:S(2)}) async-start(), calls=%async_computation.10 | async-start | bytes 3932160 | tf_op jit(solution)/shard_map/reduce_scatter | solution.py:268
  143.3 53.6 %copy-start.4 = (bf16[256,1536]{1,0:T(8,128)(2,1)S(1)}, bf16[256,1536]{1,0:T(8,128)(2,1)}, u32[]{:S(2)}) copy-start(bf16[256,1536]{1,0:T(8,128)(2,1)} %param.12) | copy-start | bytes 2359300
  147.4 332.1 %copy-start.9 = (bf16[256,8,2,96]{0,3,2,1:T(8,128)(2,1)}, bf16[256,8,2,96]{0,3,2,1:T(8,128)(2,1)S(1)}, u32[]{:S(2)}) copy-start(bf16[256,8,2,96]{0,3,2,1:T(8,128)(2,1)S(1)} %fusion.35) | copy-start | bytes 2359300
  200.7 274.6 %copy-start.6 = (f32[256,1536]{1,0:T(8,128)}, f32[256,1536]{1,0:T(8,128)S(1)}, u32[]{:S(2)}) copy-start(f32[256,1536]{1,0:T(8,128)S(1)} %get-tuple-element.365) | copy-start | bytes 4718596
  200.7 274.6 %copy-start.30 = (f32[256]{0:T(256)}, f32[256]{0:T(256)S(1)}, u32[]{:S(2)}) copy-start(f32[256]{0:T(256)S(1)} %get-tuple-element.361) | copy-start | bytes 3076
  352.0 96.1 %copy-start.11 = (bf16[256,1536]{1,0:T(8,128)(2,1)S(1)}, bf16[256,1536]{1,0:T(8,128)(2,1)}, u32[]{:S(2)}) copy-start(bf16[256,1536]{1,0:T(8,128)(2,1)} %param.19) | copy-start | bytes 2359300
  448.1 28.8 %slice-start = ((s8[4718592]{0:T(1024)(128)(4,1)}), s8[4194304]{0:T(1024)(128)(4,1)S(1)}, s32[]{:S(2)}) async-start(s8[4718592]{0:T(1024)(128)(4,1)} %bitcast.195), calls=%async_computation.15 | async-start | bytes 8388608
  545.5 179.5 %reduce-scatter.12.cloned.1.call-start = ((), (), s32[]{:S(2)}) async-start(), calls=%async_computation.12 | async-start | bytes 9732096 | tf_op jit(solution)/shard_map/reduce_scatter | solution.py:86
  553.0 384.9 %reduce-scatter.10.cloned.1.call-start = ((), (), s32[]{:S(2)}) async-start(), calls=%async_computation.11 | async-start | bytes 19464192 | tf_op jit(solution)/shard_map/reduce_scatter | solution.py:85
  555.6 28.4 %copy-start.5 = (bf16[256,1536]{1,0:T(8,128)(2,1)S(1)}, bf16[256,1536]{1,0:T(8,128)(2,1)}, u32[]{:S(2)}) copy-start(bf16[256,1536]{1,0:T(8,128)(2,1)} %param.12) | copy-start | bytes 2359300
  555.6 28.4 %copy-start.23 = (f32[1536]{0:T(1024)S(1)}, f32[1536]{0:T(1024)}, u32[]{:S(2)}) copy-start(f32[1536]{0:T(1024)} %copy-done.22) | copy-start | bytes 18436
  593.5 593.6 %reduce-scatter.16.cloned.1.call-start = ((), (), s32[]{:S(2)}) async-start(), calls=%async_computation.14 | async-start | bytes 25952256
  633.8 988.8 %reduce-scatter.14.cloned.1.call-start = ((), (), s32[]{:S(2)}) async-start(), calls=%async_computation.13 | async-start | bytes 51904512 | tf_op jit(solution)/shard_map/reduce_scatter | solution.py:85
  667.4 52.0 %copy-start.31 = (f32[256]{0:T(256)S(1)}, f32[256]{0:T(256)}, u32[]{:S(2)}) copy-start(f32[256]{0:T(256)} %get-tuple-element.358) | copy-start | bytes 3076
  (23 other events, 132.2 us)
Sparse Core Ops, SparseCore 0:
  10.9 83.3 all-gather.5
  103.3 27.0 all-gather.7
  133.3 63.4 all-gather.9
  199.6 152.3 all-gather.11
  354.7 93.3 all-gather.13
  545.6 36.3 reduce-scatter.7
  588.5 136.5 reduce-scatter.11
  732.0 205.8 reduce-scatter.9
  944.9 242.1 reduce-scatter.15
  1193.9 428.6 reduce-scatter.13
where the time goes:
time: 1640 us; the launch traced here: 1630 us
  waiting for transfers between devices  1270 us (77%)
  matrix products  178 us (11%)
  blocking collectives  84.5 us (5%)
  local copies, waits for them, and re-layouts  59.5 us (4%)
  other arithmetic  19.4 us (1%)
    reduce_scatter x2, waiting for transfers between devices, owned_three(): lax.psum_scatter(second_part, ('dp', 'ctx'), scatter_dimension=0, tiled=T...  648 us
    unnamed x11, waiting for transfers between devices  252 us
    all_gather x1, waiting for transfers between devices, shards(): lax.all_gather(w_gate_up, ('dp', 'ctx'), axis=0, tiled=True)  151 us
    unnamed x2, blocking collectives  84.5 us
    all_gather x1, waiting for transfers between devices, shards(): lax.all_gather(w_down, ('dp', 'ctx'), axis=0, tiled=True)  82.5 us
    all_gather x1, waiting for transfers between devices, shards(): lax.all_gather(w_out, ('dp', 'ctx'), axis=0, tiled=True)  49.4 us
    all_gather x1, waiting for transfers between devices, shards(): lax.all_gather(w_qkv, ('dp', 'ctx'), axis=0, tiled=True)  37.9 us
    dot_general x4, matrix products, full_back(): return jnp.dot(grad_side, whole_weight, preferred_element_type=jnp.float32)  37.1 us
  transfers between devices with their start and end apart: 10, of which 10 were waited for; matrix products, arithmetic and copies ran while one was open for 9% of the time, Pallas kernels for 0%

commit v1 on v0

v1 whole, which is shorter than its diff:
```python
import functools
import math

import jax
import jax.numpy as jnp
from jax import lax
from jax.experimental import pallas as pl
from jax.experimental.pallas import tpu as pltpu
from jax.sharding import Mesh
from jax.sharding import PartitionSpec as P

QUERY_HEADS = 16
KEY_VALUE_HEADS = 8
HEAD_SIZE = 96
FF = 4096
BLK = 128
QUERY_FEATURES = 1536
KEY_FEATURES = 768

EPSILON = 1e-05
THETA = 100000.0
MASK_FILL = -1e30
BF = jnp.bfloat16
F32 = jnp.float32
PLANE = ("i", "ctx")
ALL = ("o", "i", "ctx")


def rope_tables(rope_pos):
    half_dim = HEAD_SIZE // 2
    exponent = jnp.arange(half_dim, dtype=F32) * (2.0 / HEAD_SIZE)
    frequency = jnp.power(F32(THETA), -exponent)
    angles = rope_pos.astype(F32)[..., None] * frequency
    return (jnp.cos(angles), jnp.sin(angles))


def rotate(values, cosine, sine):
    half_dim = HEAD_SIZE // 2
    first, second = values[..., :half_dim], values[..., half_dim:]
    return jnp.concatenate([first * cosine - second * sine, second * cosine + first * sine], -1)


def rotate_back(values, cosine, sine):
    return rotate(values, cosine, -sine)


def positions(lengths, slot_table, count_of_rows):
    row_index = jnp.arange(count_of_rows, dtype=jnp.int32)
    slot_of = jnp.repeat(slot_table, BLK)
    stream = slot_of * BLK + row_index % BLK
    seq_ends = jnp.cumsum(lengths)
    passed = stream[:, None] >= seq_ends[None, :]
    segment = jnp.sum(passed.astype(jnp.int32), 1)
    offset = jnp.max(jnp.where(passed, seq_ends[None, :], 0), 1)
    return (stream, segment, stream - offset)


def norm_back(grad_normed, gain, source, scale):
    weighted = grad_normed * gain
    return scale * weighted - source * scale**3 * jnp.mean(weighted * source, -1, keepdims=True)


def nt(a, b):
    return lax.dot_general(a, b, (((1,), (1,)), ((), ())), preferred_element_type=F32)


def nn(a, b):
    return lax.dot_general(a, b, (((1,), (0,)), ((), ())), preferred_element_type=F32)


def tn(a, b):
    return lax.dot_general(a, b, (((0,), (0,)), ((), ())), preferred_element_type=F32)


MESH = pl.DeviceIdType.MESH


def places(n_ctx):
    o, i, c = lax.axis_index("o"), lax.axis_index("i"), lax.axis_index("ctx")
    return o, i, c, c + 1 - 2 * (c % 2), (c + n_ctx // 2) % n_ctx


def greet(devices):
    barrier = pltpu.get_barrier_semaphore()
    for device in devices:
        pl.semaphore_signal(barrier, inc=1, device_id=device, device_id_type=MESH)
    pl.semaphore_wait(barrier, len(devices))


def send(src, dst, send_sem, recv_sem, device):
    copy = pltpu.make_async_remote_copy(
        src_ref=src, dst_ref=dst, send_sem=send_sem, recv_sem=recv_sem, device_id=device, device_id_type=MESH
    )
    copy.start()
    return copy


def gather_kernel(n_ctx, n_arrays, *refs):
    sources, outs = refs[:n_arrays], refs[n_arrays : 2 * n_arrays]
    send_sem, recv_sem, local_sem = refs[2 * n_arrays :]
    o, i, c, mate, far = places(n_ctx)
    j, core = 1 - i, c % 2
    d_mate, d_x, d_y = (o, i, mate), (o, j, c), (o, i, far)
    me, s_x, s_y, s_d = i * n_ctx + c, j * n_ctx + c, i * n_ctx + far, j * n_ctx + far
    greet([d_mate, d_x, d_y])
    relay = (o, j * core + i * (1 - core), c * core + far * (1 - core))
    relayed = s_y * core + s_x * (1 - core)
    copies = []

    def start(a, kind, src, slot, device):
        copy = send(src, outs[a].at[slot], send_sem.at[a, kind], recv_sem.at[a, kind], device)
        copies.append(copy)
        return copy

    first, later = [], []
    for a in range(n_arrays):
        own = pltpu.make_async_copy(sources[a], outs[a].at[me], local_sem.at[a])
        own.start()
        along_x = start(a, 1, sources[a], me, d_x)
        along_y = start(a, 2, sources[a], me, d_y)
        late = [start(a, 0, sources[a], me, d_mate)]
        along_x.wait_recv()
        late.append(start(a, 3, outs[a].at[s_x], s_x, d_mate))
        along_y.wait_recv()
        diagonal = start(a, 5, outs[a].at[relayed], relayed, relay)
        late.append(start(a, 4, outs[a].at[s_y], s_y, d_mate))
        first.append((own, diagonal))
        later += late
    for a, (own, diagonal) in enumerate(first):
        own.wait()
        diagonal.wait_recv()
        later.append(start(a, 6, outs[a].at[s_d], s_d, d_mate))
    for copy in later:
        copy.wait_recv()
    for copy in copies:
        copy.wait_send()


def plane_gather(arrays, n_ctx, number):
    n = len(arrays)
    outs = pl.pallas_call(
        functools.partial(gather_kernel, n_ctx, n),
        out_shape=[jax.ShapeDtypeStruct((2 * n_ctx,) + a.shape, a.dtype) for a in arrays],
        in_specs=[pl.BlockSpec(memory_space=pltpu.VMEM)] * n,
        out_specs=[pl.BlockSpec(memory_space=pl.ANY)] * n,
        scratch_shapes=[
            pltpu.SemaphoreType.DMA((n, 7)),
            pltpu.SemaphoreType.DMA((n, 7)),
            pltpu.SemaphoreType.DMA((n,)),
        ],
        compiler_params=pltpu.CompilerParams(collective_id=number, has_side_effects=True),
        name=f"plane_gather_{number}",
    )(*arrays)
    return [x.reshape(-1, x.shape[-1]) for x in outs]


def scatter_kernel(n_ctx, x_ref, out_ref, from_mate, got, going, send_sem, recv_sem):
    o, i, c, mate, far = places(n_ctx)
    j, core = 1 - i, c % 2
    rows = x_ref.shape[1]
    d_mate, d_x, d_y = (o, i, mate), (o, j, c), (o, i, far)
    greet([d_mate, d_x, d_y])
    far_mate = (mate + n_ctx // 2) % n_ctx
    mine = [j * n_ctx + far, j * n_ctx + c, i * n_ctx + far, i * n_ctx + c]
    theirs = [j * n_ctx + far_mate, j * n_ctx + mate, i * n_ctx + far_mate, i * n_ctx + mate]
    combined = (o, j * (1 - core) + i * core, c * (1 - core) + far * core)
    direct = (o, j * core + i * (1 - core), c * core + far * (1 - core))

    def start(kind, src, dst, device):
        return send(src, dst, send_sem.at[kind], recv_sem.at[kind], device)

    def each(body):
        @pl.loop(0, rows, step=32)
        def _(r):
            body(pl.ds(pl.multiple_of(r, 32), 32))

    mates = [start(n, x_ref.at[theirs[n]], from_mate.at[n], d_mate) for n in range(4)]
    mates[0].wait_recv()

    @each
    def _(r):
        going[0, r] = (x_ref[mine[0], r].astype(F32) + from_mate[0, r].astype(F32)).astype(BF)

    diagonal = start(4, going.at[0], got.at[0], direct)
    mates[1].wait_recv()
    mates[2].wait_recv()
    s_direct = mine[2] * (1 - core) + mine[1] * core
    s_combined = mine[1] * (1 - core) + mine[2] * core

    @each
    def _(r):
        going[1, r] = (x_ref[s_direct, r].astype(F32) + from_mate[2 - core, r].astype(F32)).astype(BF)

    straight = start(5, going.at[1], got.at[1], direct)
    diagonal.wait_recv()

    @each
    def _(r):
        pair = x_ref[s_combined, r].astype(F32) + from_mate[1 + core, r].astype(F32)
        going[2, r] = (pair + got[0, r].astype(F32)).astype(BF)

    joined = start(6, going.at[2], got.at[2], combined)
    mates[3].wait_recv()
    straight.wait_recv()
    joined.wait_recv()

    @each
    def _(r):
        pair = x_ref[mine[3], r].astype(F32) + from_mate[3, r].astype(F32)
        out_ref[r] = pair + got[1, r].astype(F32) + got[2, r].astype(F32)

    for copy in mates + [diagonal, straight, joined]:
        copy.wait_send()


def plane_scatter(x, n_ctx, number):
    n = 2 * n_ctx
    rows, width = x.shape[0] // n, x.shape[1]
    return pl.pallas_call(
        functools.partial(scatter_kernel, n_ctx),
        out_shape=jax.ShapeDtypeStruct((rows, width), F32),
        in_specs=[pl.BlockSpec(memory_space=pltpu.VMEM)],
        out_specs=pl.BlockSpec(memory_space=pltpu.VMEM),
        scratch_shapes=[
            pltpu.VMEM((4, rows, width), BF),
            pltpu.VMEM((3, rows, width), BF),
            pltpu.VMEM((3, rows, width), BF),
            pltpu.SemaphoreType.DMA((7,)),
            pltpu.SemaphoreType.DMA((7,)),
        ],
        compiler_params=pltpu.CompilerParams(collective_id=number, has_side_effects=True),
        name=f"plane_scatter_{number}",
    )(x.reshape(n, rows, width))


def swap_kernel(n_ctx, n_arrays, *refs):
    sources, outs = refs[:n_arrays], refs[n_arrays : 2 * n_arrays]
    send_sem, recv_sem, local_sem = refs[2 * n_arrays :]
    o, i, c, _, _ = places(n_ctx)
    n = 2 * n_ctx
    me = i * n_ctx + c
    others = [(me + k) % n for k in range(1, n)]
    greet([(o, d // n_ctx, d % n_ctx) for d in others])
    copies = []
    for a in range(n_arrays):
        for k, d in enumerate(others):
            copies.append(
                send(
                    sources[a].at[d],
                    outs[a].at[me],
                    send_sem.at[a, k],
                    recv_sem.at[a, k],
                    (o, d // n_ctx, d % n_ctx),
                )
            )
    own = [pltpu.make_async_copy(sources[a].at[me], outs[a].at[me], local_sem.at[a]) for a in range(n_arrays)]
    for copy in own:
        copy.start()
    for copy in copies:
        copy.wait_recv()
        copy.wait_send()
    for copy in own:
        copy.wait()


def plane_swap(arrays, n_ctx, number):
    n = len(arrays)
    return pl.pallas_call(
        functools.partial(swap_kernel, n_ctx, n),
        out_shape=[jax.ShapeDtypeStruct(a.shape, a.dtype) for a in arrays],
        in_specs=[pl.BlockSpec(memory_space=pltpu.VMEM)] * n,
        out_specs=[pl.BlockSpec(memory_space=pltpu.VMEM)] * n,
        scratch_shapes=[
            pltpu.SemaphoreType.DMA((n, 2 * n_ctx - 1)),
            pltpu.SemaphoreType.DMA((n, 2 * n_ctx - 1)),
            pltpu.SemaphoreType.DMA((n,)),
        ],
        compiler_params=pltpu.CompilerParams(collective_id=number, has_side_effects=True),
        name=f"plane_swap_{number}",
    )(*arrays)


def z_ag(x):
    return lax.all_gather(x, "o", axis=0, tiled=True)


def z_rs(x):
    return lax.psum_scatter(x, "o", scatter_dimension=0, tiled=True)


def inv_rms(x):
    return lax.rsqrt(jnp.mean(x * x, -1, keepdims=True) + EPSILON)


def feature_moves(n_outer, n_plane):
    moves = []
    half, quarter = n_outer // 2, n_outer // 4
    for block in range(n_outer * n_plane):
        if block < 4 * n_outer:
            place, step = block // half, block % half
        elif block < 6 * n_outer:
            place, step = divmod(block - 4 * n_outer, quarter)
            step += half
        else:
            place, step = divmod(block - 6 * n_outer, quarter)
            step += half + quarter
        moves.append((block, step * n_plane + place))
    return moves


def make_shards(n_outer, n_inner, n_ctx):
    n_plane = n_inner * n_ctx
    moves = feature_moves(n_outer, n_plane)
    back = [(b, a) for a, b in moves]
    heads = QUERY_HEADS // n_plane
    score_scale = 1.0 / math.sqrt(HEAD_SIZE)

    def shards(tokens, norm_attn, w_qkv, w_out, norm_mlp, w_gate_up, w_down, cotangent, seq_lengths, block_slot):
        rows, width = tokens.shape
        gain_rows = norm_attn.shape[0]
        feature_rows = w_qkv.shape[0]
        out_rows = w_out.shape[0]
        unit_rows = w_gate_up.shape[0]
        n_seqs = seq_lengths.shape[1]
        group_rows = n_ctx * rows
        out_parts = w_out.reshape(out_rows, n_plane, -1).transpose(1, 0, 2)
        down_parts = (
            w_down.reshape(out_rows, n_outer // 2, n_plane, unit_rows).transpose(2, 0, 1, 3).reshape(n_plane, out_rows, -1)
        )
        gain_part = jnp.pad(jnp.stack([norm_attn, norm_mlp]), ((0, 6), (0, 128 - gain_rows)))
        meta = jnp.concatenate([seq_lengths[0], block_slot[0]])
        meta = jnp.pad(meta[None], ((0, 7), (0, 128 - meta.shape[0])))
        out_parts, down_parts, gain_parts, metas = plane_swap(
            [out_parts, down_parts] + [jnp.broadcast_to(part, (n_plane, 8, 128)) for part in (gain_part, meta)], n_ctx, 0
        )
        stream, segment, rope_pos = jax.vmap(
            lambda m: positions(m[:n_seqs], m[n_seqs : n_seqs + block_slot.shape[1]], group_rows)
        )(metas[::n_ctx, 0])
        cosine, sine = rope_tables(rope_pos)
        gain_parts = gain_parts[:, :2, :gain_rows]
        gain_high = lax.reduce_precision(gain_parts, 8, 7)
        gain_row = jnp.stack([gain_high, gain_parts - gain_high]).astype(BF).reshape(1, -1)
        gain_row = jnp.pad(gain_row, ((0, 15), (0, width - gain_row.shape[1])))
        sent = jnp.concatenate(
            [lax.ppermute(w_qkv, ALL, moves), out_parts.reshape(out_rows, -1), gain_row], 0
        )
        got = z_ag(sent).reshape(n_outer, -1, width)
        qkv = got[:, :feature_rows].reshape(-1, width)
        out_w = got[:, feature_rows : feature_rows + out_rows].reshape(n_outer * n_plane * out_rows, -1)
        gains = got[:, feature_rows + out_rows, : 4 * n_plane * gain_rows].astype(F32)
        gains = gains.reshape(n_outer, 2, n_plane, 2, gain_rows).sum(1).transpose(2, 0, 1, 3).reshape(2, width)
        gain_one, gain_two = gains[0], gains[1]
        sent = jnp.concatenate([w_gate_up, down_parts.reshape(-1, width)], 0)
        got = z_ag(sent).reshape(n_outer, -1, width)
        gate_up = got[:, :unit_rows].reshape(-1, width)
        down_w = got[:, unit_rows:].reshape(width, -1)
        units = down_w.shape[1]
        source = tokens.astype(F32)
        scale_one = inv_rms(source)
        x_all, dy_all = plane_gather([tokens, cotangent], n_ctx, 1)
        x_all_f = x_all.astype(F32)
        xn1 = (x_all_f * inv_rms(x_all_f) * gain_one).astype(BF)
        proj = nt(xn1, qkv).reshape(n_inner, group_rows, -1)
        qf = heads * HEAD_SIZE
        c4, s4 = cosine[:, :, None], sine[:, :, None]
        q = rotate(proj[..., :qf].reshape(n_inner, group_rows, heads, HEAD_SIZE), c4, s4).astype(BF)
        k = rotate(proj[..., qf : qf + HEAD_SIZE], cosine, sine).astype(BF)
        v = proj[..., qf + HEAD_SIZE :].astype(BF)
        allowed = ((segment[:, :, None] == segment[:, None, :]) & (stream[:, None, :] <= stream[:, :, None]))[:, None]

        def score_of():
            s = jnp.einsum("gqhd,gkd->ghqk", q, k, preferred_element_type=F32) * score_scale
            return jnp.where(allowed, s, MASK_FILL)

        s = score_of()
        high = jnp.max(s, -1, keepdims=True)
        e = jnp.where(allowed, jnp.exp(s - high), 0.0)
        total = jnp.sum(e, -1, keepdims=True)
        lse = high + jnp.log(total)
        p = (e / total).astype(BF)
        attn = jnp.einsum("ghqk,gkd->gqhd", p, v, preferred_element_type=F32).astype(BF)
        attn_flat = attn.reshape(n_inner * group_rows, qf)
        out_term = plane_scatter(nt(attn_flat, out_w).astype(BF), n_ctx, 2)
        residual = source + out_term
        scale_two = inv_rms(residual)
        xn2 = plane_gather([(residual * scale_two * gain_two).astype(BF)], n_ctx, 3)[0]
        gu = nt(xn2, gate_up)
        gate, up = gu[:, :units], gu[:, units:]
        sg = jax.nn.sigmoid(gate)
        hidden = (gate * sg * up).astype(BF)
        result = (residual + plane_scatter(nt(hidden, down_w).astype(BF), n_ctx, 6)).astype(BF)
        dhid = nn(dy_all, down_w)
        dgu = jnp.concatenate([dhid * up * sg * (1.0 + gate * (1.0 - sg)), dhid * gate * sg], 1).astype(BF)
        g_down = z_rs(tn(dy_all, hidden).astype(BF))
        grad_gate_up = z_rs(tn(dgu, xn2).astype(BF)).astype(F32)
        dxn2 = plane_scatter(nn(dgu, gate_up).astype(BF), n_ctx, 4)
        grad_gain_two = jnp.sum(dxn2 * residual * scale_two, 0)
        dh1 = cotangent.astype(F32) + norm_back(dxn2, gain_two, residual, scale_two)
        dh1_all = plane_gather([dh1.astype(BF)], n_ctx, 5)[0]
        dattn = nn(dh1_all, out_w).astype(BF)
        g_out = z_rs(tn(dh1_all, attn_flat).astype(BF))
        da = dattn.reshape(n_inner, group_rows, heads, HEAD_SIZE)
        delta = jnp.sum(da.astype(F32) * attn.astype(F32), -1).transpose(0, 2, 1)[..., None]
        pf = jnp.where(allowed, jnp.exp(score_of() - lse), 0.0)
        dv = jnp.einsum("ghqk,gqhd->gkd", pf.astype(BF), da, preferred_element_type=F32)
        dpf = jnp.einsum("gqhd,gkd->ghqk", da, v, preferred_element_type=F32)
        ds = (pf * (dpf - delta)).astype(BF)
        dq = jnp.einsum("ghqk,gkd->gqhd", ds, k, preferred_element_type=F32) * score_scale
        dk = jnp.einsum("ghqk,gqhd->gkd", ds, q, preferred_element_type=F32) * score_scale
        dq = rotate_back(dq, c4, s4).reshape(n_inner, group_rows, qf)
        dk = rotate_back(dk, cosine, sine)
        dproj = jnp.concatenate([dq, dk, dv], -1).astype(BF).reshape(n_inner * group_rows, -1)
        g_qkv = z_rs(tn(dproj, xn1).astype(BF))
        grad_qkv = lax.ppermute(g_qkv, ALL, back).astype(F32)
        dxn1 = plane_scatter(nn(dproj, qkv).astype(BF), n_ctx, 7)
        grad_gain_one = jnp.sum(dxn1 * source * scale_one, 0)
        grad_input = dh1 + norm_back(dxn1, gain_one, source, scale_one)
        g_gain = jnp.stack([grad_gain_one, grad_gain_two]).reshape(2, n_outer, n_plane, gain_rows)
        g_gain = g_gain.transpose(2, 1, 0, 3).reshape(n_plane, 2 * n_outer, gain_rows)
        g_gain = jnp.pad(g_gain, ((0, 0), (0, 0), (0, 128 - gain_rows)))
        g_out, g_down, g_gain = plane_swap(
            [g_out.reshape(n_plane, out_rows, -1), g_down.reshape(n_plane, out_rows, -1), g_gain], n_ctx, 8
        )
        grad_out = g_out.transpose(1, 0, 2).reshape(out_rows, -1).astype(F32)
        grad_down = g_down.reshape(n_plane, out_rows, n_outer // 2, unit_rows).transpose(1, 2, 0, 3)
        grad_down = grad_down.reshape(out_rows, -1).astype(F32)
        g = lax.psum_scatter(jnp.sum(g_gain, 0).reshape(n_outer, 2, 128), "o", scatter_dimension=0, tiled=True)
        g = g[0, :, :gain_rows]
        return (result, grad_input, g[0], grad_qkv, grad_out, g[1], grad_gate_up, grad_down)

    return shards


def solution(mesh):
    n_inner = 2
    n_ctx = mesh.shape["ctx"]
    n_outer = mesh.shape["dp"] // n_inner
    split = Mesh(mesh.devices.reshape(n_outer, n_inner, n_ctx), ALL)
    rows, vec, grp = P(ALL, None), P(ALL), P(("o", "i"), None)
    return jax.shard_map(
        make_shards(n_outer, n_inner, n_ctx),
        mesh=split,
        in_specs=(rows, vec, rows, rows, vec, rows, rows, rows, grp, grp),
        out_specs=(rows, rows, vec, rows, rows, vec, rows, rows),
        check_vma=False,
    )
```

time: 1640 us -> 597 us (0.36)
  waiting for transfers between devices: 1270 us -> 47.9 us
  Pallas kernels: 0 us -> 301 us
  blocking collectives: 84.5 us -> 11.2 us
  matrix products: 178 us -> 116 us
  other arithmetic: 19.4 us -> 55.4 us
  local copies, waits for them, and re-layouts: 59.5 us -> 37.8 us
    reduce_scatter x4, waiting for transfers between devices: 677 us -> 37.5 us  [z_rs(): return lax.psum_scatter(x, 'o', scatter_dimension=0, tiled=True)]
    all_gather x5 -> x2, waiting for transfers between devices: 342 us -> 0.01 us  [z_ag(): return lax.all_gather(x, 'o', axis=0, tiled=True)]
    pallas_call x0 -> x9, Pallas kernels: none -> 301 us  [the longest x4 141 us: plane_scatter(): pl.pallas_call(functools.partial(scatter_kernel, n_ctx), out_shape=jax.Sh...]
    unnamed x11 -> x6, waiting for transfers between devices: 252 us -> 0.1 us
    unnamed x2 -> x1, blocking collectives: 84.5 us -> 11.2 us
    dot_general x24 -> x18, matrix products: 178 us -> 116 us  [the longest x4 30 us: nn(): lax.dot_general(a, b, (((1,), (0,)), ((), ())), preferred_element_type=F32)]
    unnamed x73 -> x98, local copies, waits for them, and re-layouts: 34.6 us -> 9.25 us
    convert_element_type x1 -> x9, other arithmetic: 0.01 us -> 22.3 us  [the longest x2 11.5 us: shards(): xn1 = (x_all_f * inv_rms(x_all_f) * gain_one).astype(BF)]
  transfers between devices with their start and end apart: 10 -> 8, of which waited for: 10 -> 3; matrix products, arithmetic and copies ran while one was open for 9% -> 19% of each run, Pallas kernels for 0% -> 33%
where the time goes in v1:
time: 597 us; the launch traced here: 591 us
  Pallas kernels  301 us (50%)
  matrix products  116 us (19%)
  other arithmetic  55.4 us (9%)
  waiting for transfers between devices  47.9 us (8%)
  local copies, waits for them, and re-layouts  37.8 us (6%)
  between operations  15.3 us (3%)
  blocking collectives  11.2 us (2%)
  starting transfers between devices  6.95 us (1%)
    pallas_call x4, Pallas kernels, plane_scatter(): pl.pallas_call(functools.partial(scatter_kernel, n_ctx), out_shape=jax.Sh...  141 us
    pallas_call x3, Pallas kernels, plane_gather(): pl.pallas_call(functools.partial(gather_kernel, n_ctx, n), out_shape=[jax...  131 us
    reduce_scatter x4, waiting for transfers between devices, z_rs(): return lax.psum_scatter(x, 'o', scatter_dimension=0, tiled=True)  37.5 us
    dot_general x4, matrix products, nn(): lax.dot_general(a, b, (((1,), (0,)), ((), ())), preferred_element_type=F32)  30 us
    pallas_call x2, Pallas kernels, plane_swap(): pl.pallas_call(functools.partial(swap_kernel, n_ctx, n), out_shape=[jax.S...  28.8 us
    dot_general x4, matrix products, tn(): lax.dot_general(a, b, (((0,), (0,)), ((), ())), preferred_element_type=F32)  27.5 us
    dot_general x4, matrix products, nt(): lax.dot_general(a, b, (((1,), (1,)), ((), ())), preferred_element_type=F32)  22.5 us
  transfers between devices with their start and end apart: 8, of which 3 were waited for; matrix products, arithmetic and copies ran while one was open for 19% of the time, Pallas kernels for 33%

profile of v1, /device:TPU:2, one launch (start us, length us, event | category | flops | bytes accessed | tf_op | source)
XLA Modules:
  0.0 591.5 jit_solution(2951523633567237727)
XLA Ops:
  17.5 14.0 %plane_swap_0.1 = (bf16[8,48,192]{2,1,0:T(8,128)(2,1)}, bf16[8,48,512]{2,1,0:T(8,128)(2,1)}, f32[8,8,128]{2,1,0:T(8,128)}, s32[8,8,128]{2,1,0:T(8,128)}) custom-call(bf16[8,48,192]{2,1,0:T(8,128)(2,1)} %bitcast.210, bf16[8,48,512]{2,1,0:T(8,128)(2,1)} %reshape.321.refs_1_, f32[8,8,128]{2,1,0:T(8,128)} %broadcast_in_dim.69.refs_2_, ...), custom_call_target="tpu_custom_call" | custom-call | tf_op jit(solution)/shard_map/plane_swap_0/pallas_call | solution.py:268
  41.2 62.1 %plane_gather_1.1 = (bf16[8,256,1536]{2,1,0:T(8,128)(2,1)}, bf16[8,256,1536]{2,1,0:T(8,128)(2,1)}) custom-call(bf16[256,1536]{1,0:T(8,128)(2,1)} %refs_0_.1, bf16[256,1536]{1,0:T(8,128)(2,1)} %refs_1_.1), custom_call_target="tpu_custom_call" | custom-call | tf_op jit(solution)/shard_map/plane_gather_1/pallas_call | solution.py:141
  133.3 6.6 %fusion.23 = bf16[2,1024,2,96]{1,3,2,0:T(8,128)(2,1)S(1)} fusion(f32[2,1024,1024,2]{2,1,3,0:T(8,128)S(1)} %get-tuple-element.65, f32[2,2,1024]{2,1,0:T(2,128)S(1)} %fusion.2, f32[2,2,1024]{2,1,0:T(2,128)S(1)} %get-tuple-element.64, pred[2,1024,1024]{1,2,0:T(8,128)(4,1)S(1)} %compare_and_fusion, f32[2,1024,384]{1,2,0:T(8,128)S(1)} %fusion.77), kind=kOutput, calls=%fused_computation.57 | convolution fusion | flops 830865408 | bytes 20086784 | tf_op jit(solution)/shard_map/ghqk,gkd->gqhd/dot_general | solution.py:381
  145.5 35.2 %plane_scatter_2.1 = f32[256,1536]{1,0:T(8,128)} custom-call(bf16[8,256,1536]{2,1,0:T(8,128)(2,1)} %bitcast.176), custom_call_target="tpu_custom_call" | custom-call | tf_op jit(solution)/shard_map/plane_scatter_2/pallas_call | solution.py:219
  184.8 34.2 %plane_gather_3.1 = bf16[8,256,1536]{2,1,0:T(8,128)(2,1)} custom-call(bf16[256,1536]{1,0:T(8,128)(2,1)} %multiply_convert_fusion.4.refs_0_), custom_call_target="tpu_custom_call" | custom-call | tf_op jit(solution)/shard_map/plane_gather_3/pallas_call | solution.py:141
  219.6 6.9 %fusion.5 = bf16[2048,1536]{1,0:T(8,128)(2,1)} fusion(f32[1536]{0:T(1024)S(1)} %mul.337, f32[2048]{0:T(1024)S(1)} %bitcast.216, bf16[8,256,1536]{2,1,0:T(8,128)(2,1)} %get-tuple-element.17), kind=kLoop, calls=%fused_computation.11 | loop fusion | flops 12582912 | bytes 12597248 | tf_op jit(solution)/shard_map/convert_element_type | solution.py:362
  233.4 9.9 %fusion.78 = f32[2048,1024]{0,1:T(8,128)S(1)} fusion(bf16[2048,1536]{1,0:T(8,128)(2,1)} %bitcast.177, bf16[1024,1536]{1,0:T(8,128)(2,1)} %bitcast.192), kind=kOutput, calls=%fused_computation.156 | convolution fusion | flops 6442450944 | bytes 17825792 | tf_op jit(solution)/shard_map/dot_general | solution.py:64
  243.3 9.9 %multiply_convert_fusion.2 = (bf16[2048,512]{0,1:T(8,128)(2,1)S(1)}, bf16[2048,512]{0,1:T(8,128)(2,1)S(1)}, bf16[2048,512]{0,1:T(8,128)(2,1)}) fusion(f32[2048,1024]{0,1:T(8,128)S(1)} %fusion.78, bf16[2048,1536]{1,0:T(8,128)(2,1)} %bitcast.223, bf16[1536,512]{1,0:T(8,128)(2,1)S(1)} %copy-done.18), kind=kOutput, calls=%fused_computation.25 | convolution fusion | flops 3238002688 | bytes 22544384 | tf_op jit(solution)/shard_map/dot_general | solution.py:68
  253.2 8.8 %convolution_convert_fusion.2 = bf16[2048,1536]{1,0:T(8,128)(2,1)} fusion(bf16[1024,1536]{1,0:T(8,128)(2,1)S(1)} %bitcast.193, bf16[2048,512]{0,1:T(8,128)(2,1)S(1)} %get-tuple-element.39, bf16[2048,512]{0,1:T(8,128)(2,1)S(1)} %get-tuple-element.38), kind=kOutput, calls=%fused_computation.21 | convolution fusion | flops 6453985280 | bytes 13631488 | tf_op jit(solution)/shard_map/dot_general | solution.py:68
  262.0 35.1 %plane_scatter_4.1 = f32[256,1536]{1,0:T(8,128)} custom-call(bf16[8,256,1536]{2,1,0:T(8,128)(2,1)} %bitcast.186), custom_call_target="tpu_custom_call" | custom-call | tf_op jit(solution)/shard_map/plane_scatter_4/pallas_call | solution.py:219
  300.3 5.4 convolution_convert_fusion.3
  305.7 35.3 %plane_scatter_6.1 = f32[256,1536]{1,0:T(8,128)} custom-call(bf16[8,256,1536]{2,1,0:T(8,128)(2,1)} %bitcast.187), custom_call_target="tpu_custom_call" | custom-call | tf_op jit(solution)/shard_map/plane_scatter_6/pallas_call | solution.py:219
  344.9 34.9 %plane_gather_5.1 = bf16[8,256,1536]{2,1,0:T(8,128)(2,1)} custom-call(bf16[256,1536]{1,0:T(8,128)(2,1)} %get-tuple-element.34.refs_0_), custom_call_target="tpu_custom_call" | custom-call | tf_op jit(solution)/shard_map/plane_gather_5/pallas_call | solution.py:141
  379.8 5.9 %convolution_convert_fusion.8 = bf16[2048,192]{0,1:T(8,128)(2,1)} fusion(bf16[2048,1536]{1,0:T(8,128)(2,1)} %bitcast.181, bf16[1536,192]{1,0:T(8,128)(2,1)S(1)} %copy-done.11), kind=kOutput, calls=%fused_computation.37 | convolution fusion | flops 1208352768 | bytes 7667712 | tf_op jit(solution)/shard_map/dot_general | solution.py:68
  390.8 10.1 %fusion.27 = bf16[2,12,8,1024]{3,2,1,0:T(8,128)(2,1)} fusion(f32[2,1024,1024,2]{2,1,3,0:T(8,128)} %copy-done, f32[2,2,1024]{2,1,0:T(2,128)S(1)} %copy-done.32, pred[2,1024,1024]{1,2,0:T(8,128)(4,1)S(1)} %copy-done.6, bf16[2,1024,2,96]{1,0,3,2:T(2,128)(2,1)} %reshape.338), kind=kOutput, calls=%fused_computation.59 | convolution fusion | flops 826474496 | bytes 20070400 | tf_op jit(solution)/shard_map/ghqk,gqhd->gkd/dot_general | solution.py:405
  400.9 10.3 %fusion.1 = bf16[2,2,1024,1024]{2,3,1,0:T(8,128)(2,1)S(1)} fusion(f32[2,1024,1024,2]{2,1,3,0:T(8,128)} %copy-done, f32[2,2,1024]{2,1,0:T(2,128)S(1)} %bitcast.217, f32[2,2,1024]{2,1,0:T(2,128)S(1)} %copy-done.32, pred[2,1024,1024]{1,2,0:T(8,128)(4,1)S(1)} %copy-done.6, bf16[2,1024,2,96]{1,0,3,2:T(2,128)(2,1)S(1)} %copy-done.14, f32[2,1024,384]{1,2,0:T(8,128)} %copy-done.15), kind=kOutput, calls=%fused_computation.2 | convolution fusion | flops 834666496 | bytes 28475392 | tf_op jit(solution)/shard_map/gqhd,gkd->ghqk/dot_general | solution.py:406
  429.4 8.1 %convolution_convert_fusion.5 = bf16[1536,512]{1,0:T(8,128)(2,1)} fusion(bf16[2048,1536]{1,0:T(8,128)(2,1)} %bitcast.224, bf16[2048,512]{0,1:T(8,128)(2,1)} %get-tuple-element.40), kind=kOutput, calls=%fused_computation.34 | convolution fusion | flops 3222011904 | bytes 9961472 | tf_op jit(solution)/shard_map/dot_general | solution.py:72
  437.6 11.6 %convolution_convert_fusion.4 = bf16[1024,1536]{1,0:T(8,128)(2,1)} fusion(bf16[2048,1536]{1,0:T(8,128)(2,1)} %bitcast.178, bf16[2048,512]{0,1:T(8,128)(2,1)} %copy-done.40, bf16[2048,512]{0,1:T(8,128)(2,1)} %copy-done.39), kind=kOutput, calls=%fused_computation.28 | convolution fusion | flops 6452412416 | bytes 13631488 | tf_op jit(solution)/shard_map/dot_general | solution.py:72
  455.8 35.2 %plane_scatter_7.1 = f32[256,1536]{1,0:T(8,128)} custom-call(bf16[8,256,1536]{2,1,0:T(8,128)(2,1)} %bitcast.185), custom_call_target="tpu_custom_call" | custom-call | tf_op jit(solution)/shard_map/plane_scatter_7/pallas_call | solution.py:219
  500.0 10.3 %collective-permute-done.1 = bf16[96,1536]{1,0:T(8,128)(2,1)S(1)} collective-permute-done((bf16[96,1536]{1,0:T(8,128)(2,1)}, bf16[96,1536]{1,0:T(8,128)(2,1)S(1)}, u32[]{:S(2)}, u32[]{:S(2)}) %collective-permute-start.1) | collective-permute-done | bytes 294944 | tf_op jit(solution)/shard_map/ppermute | solution.py:414
  511.2 6.1 %reduce-scatter.7.cloned.1.call-done = bf16[384,512]{1,0:T(8,128)(2,1)} async-done(((bf16[1536,512]{1,0:T(8,128)(2,1)}), bf16[384,512]{1,0:T(8,128)(2,1)}) %reduce-scatter.7.cloned.1.call-update) | async-done | bytes 393232 | tf_op jit(solution)/shard_map/reduce_scatter | solution.py:288
  517.3 14.8 %plane_swap_8.1 = (bf16[8,48,192]{2,1,0:T(8,128)(2,1)}, bf16[8,48,512]{2,1,0:T(8,128)(2,1)}, f32[8,8,128]{2,1,0:T(8,128)}) custom-call(bf16[8,48,192]{2,1,0:T(8,128)(2,1)} %bitcast.213, bf16[8,48,512]{2,1,0:T(8,128)(2,1)} %bitcast.212, f32[8,8,128]{2,1,0:T(8,128)} %pad.19.refs_2_), custom_call_target="tpu_custom_call" | custom-call | tf_op jit(solution)/shard_map/plane_swap_8/pallas_call | solution.py:268
  538.2 11.2 %all-reduce.4 = f32[4,2,128]{2,1,0:T(2,128)S(1)} all-reduce(f32[4,2,128]{2,1,0:T(2,128)S(1)} %bitcast.218), channel_id=4, replica_groups=mesh['o'=4,'i'=2,'ctx'=4] {'o'}, use_global_device_ids=true, to_apply=%region_17.18.clone | all-reduce | flops 1024 | bytes 8192
  550.5 31.4 %reduce-scatter.11.cloned.1.call-done = bf16[256,1536]{1,0:T(8,128)(2,1)} async-done(((bf16[1024,1536]{1,0:T(8,128)(2,1)}), bf16[256,1536]{1,0:T(8,128)(2,1)}) %reduce-scatter.11.cloned.1.call-update) | async-done | bytes 786448 | tf_op jit(solution)/shard_map/reduce_scatter | solution.py:288
  (205 shorter events, 123.0 us)
Async XLA Ops:
  7.2 100.9 %all-gather.3.cloned.1.call-start = ((), (), s32[]{:S(2)}) async-start(), calls=%async_computation.4 | async-start | bytes 2457600 | tf_op jit(solution)/shard_map/all_gather | solution.py:284
  7.2 26.3 %collective-permute-start = (bf16[96,1536]{1,0:T(8,128)(2,1)}, bf16[96,1536]{1,0:T(8,128)(2,1)S(1)}, u32[]{:S(2)}, u32[]{:S(2)}) collective-permute-start(bf16[96,1536]{1,0:T(8,128)(2,1)} %param.12), channel_id=1, source_target_pairs={{0,0},{1,8},{2,1},{3,9},{4,2},{5,10},{6,3},{7,11},{8,4},{9,12},{10... | collective-permute-start | bytes 884744 | tf_op jit(solution)/shard_map/ppermute | solution.py:345
  11.7 23.8 %copy-start.21 = (bf16[256,1536]{1,0:T(8,128)(2,1)S(1)}, bf16[256,1536]{1,0:T(8,128)(2,1)}, u32[]{:S(2)}) copy-start(bf16[256,1536]{1,0:T(8,128)(2,1)} %param.15) | copy-start | bytes 2359300
  34.3 192.2 %all-gather.5.cloned.1.call-start = ((), (), s32[]{:S(2)}) async-start(), calls=%async_computation.5 | async-start | bytes 5898240 | tf_op jit(solution)/shard_map/all_gather | solution.py:284
  36.7 456.4 %reduce-scatter.9.cloned.1.call-start = ((), (), s32[]{:S(2)}) async-start(), calls=%async_computation.7 | async-start | bytes 1474560 | tf_op jit(solution)/shard_map/reduce_scatter | solution.py:288
  41.2 90.9 %copy-start.5 = (pred[2,1024,1024]{1,2,0:T(8,128)(4,1)}, pred[2,1024,1024]{1,2,0:T(8,128)(4,1)S(1)}, u32[]{:S(2)}) copy-start(pred[2,1024,1024]{1,2,0:T(8,128)(4,1)S(1)} %compare_and_fusion) | copy-start | bytes 6291460
  113.6 27.3 %copy-start.10 = (bf16[1536,192]{1,0:T(8,128)(2,1)}, bf16[1536,192]{1,0:T(8,128)(2,1)S(1)}, u32[]{:S(2)}) copy-start(bf16[1536,192]{1,0:T(8,128)(2,1)S(1)} %reshape.327) | copy-start | bytes 1769476
  120.8 11.2 %copy-start.15 = (f32[2,1024,384]{1,2,0:T(8,128)}, f32[2,1024,384]{1,2,0:T(8,128)S(1)}, u32[]{:S(2)}) copy-start(f32[2,1024,384]{1,2,0:T(8,128)S(1)} %fusion.77) | copy-start | bytes 9437188
  145.5 35.3 %copy-start.3 = (bf16[256,1536]{1,0:T(8,128)(2,1)S(1)}, bf16[256,1536]{1,0:T(8,128)(2,1)}, u32[]{:S(2)}) copy-start(bf16[256,1536]{1,0:T(8,128)(2,1)} %refs_0_.1) | copy-start | bytes 2359300
  184.8 34.8 %copy-start.30 = (f32[1,2,8,128]{3,1,2,0:T(2,128)S(1)}, f32[1,2,8,128]{3,1,2,0:T(2,128)}, u32[]{:S(2)}) copy-start(f32[1,2,8,128]{3,1,2,0:T(2,128)} %copy.96) | copy-start | bytes 24580
  233.4 9.9 %copy-start.18 = (bf16[1536,512]{1,0:T(8,128)(2,1)S(1)}, bf16[1536,512]{1,0:T(8,128)(2,1)}, u32[]{:S(2)}) copy-start(bf16[1536,512]{1,0:T(8,128)(2,1)} %reshape.333) | copy-start | bytes 4718596
  243.3 9.9 %copy-start.9 = (bf16[4,256,1536]{2,1,0:T(8,128)(2,1)S(1)}, bf16[4,256,1536]{2,1,0:T(8,128)(2,1)}, u32[]{:S(2)}) copy-start(bf16[4,256,1536]{2,1,0:T(8,128)(2,1)} %slice.122) | copy-start | bytes 9437188
  253.2 8.8 %copy-start.40 = (bf16[2048,512]{0,1:T(8,128)(2,1)}, bf16[2048,512]{0,1:T(8,128)(2,1)S(1)}, u32[]{:S(2)}) copy-start(bf16[2048,512]{0,1:T(8,128)(2,1)S(1)} %get-tuple-element.39) | copy-start | bytes 6291460
  305.7 35.3 %copy-start.2 = (f32[256,1536]{1,0:T(8,128)S(1)}, f32[256,1536]{1,0:T(8,128)}, u32[]{:S(2)}) copy-start(f32[256,1536]{1,0:T(8,128)} %plane_scatter_4.1) | copy-start | bytes 4718596
  344.9 34.9 %copy-start.11 = (bf16[1536,192]{1,0:T(8,128)(2,1)S(1)}, bf16[1536,192]{1,0:T(8,128)(2,1)}, u32[]{:S(2)}) copy-start(bf16[1536,192]{1,0:T(8,128)(2,1)} %copy-done.10) | copy-start | bytes 1769476
  379.8 9.5 %copy-start.13 = (bf16[2,1024,2,96]{1,3,2,0:T(8,128)(2,1)S(1)}, bf16[2,1024,2,96]{1,3,2,0:T(8,128)(2,1)}, u32[]{:S(2)}) copy-start(bf16[2,1024,2,96]{1,3,2,0:T(8,128)(2,1)} %copy-done.12) | copy-start | bytes 2359300
  390.8 10.1 %copy-start.14 = (bf16[2,1024,2,96]{1,0,3,2:T(2,128)(2,1)S(1)}, bf16[2,1024,2,96]{1,0,3,2:T(2,128)(2,1)}, u32[]{:S(2)}) copy-start(bf16[2,1024,2,96]{1,0,3,2:T(2,128)(2,1)} %reshape.338) | copy-start | bytes 2359300
  424.0 87.2 %reduce-scatter.13.cloned.1.call-start = ((), (), s32[]{:S(2)}) async-start(), calls=%async_computation.9 | async-start | bytes 983040 | tf_op jit(solution)/shard_map/reduce_scatter | solution.py:288
  429.4 87.9 %reduce-scatter.7.cloned.1.call-start = ((), (), s32[]{:S(2)}) async-start(), calls=%async_computation.6 | async-start | bytes 1966080 | tf_op jit(solution)/shard_map/reduce_scatter | solution.py:288
  437.6 144.4 %reduce-scatter.11.cloned.1.call-start = ((), (), s32[]{:S(2)}) async-start(), calls=%async_computation.8 | async-start | bytes 3932160 | tf_op jit(solution)/shard_map/reduce_scatter | solution.py:288
  455.8 35.2 %copy-start.4 = (bf16[256,1536]{1,0:T(8,128)(2,1)S(1)}, bf16[256,1536]{1,0:T(8,128)(2,1)}, u32[]{:S(2)}) copy-start(bf16[256,1536]{1,0:T(8,128)(2,1)} %refs_0_.1) | copy-start | bytes 2359300
  455.8 35.2 %copy-start.33 = (f32[256]{0:T(256)S(1)}, f32[256]{0:T(256)}, u32[]{:S(2)}) copy-start(f32[256]{0:T(256)} %get-tuple-element.61) | copy-start | bytes 3076
  455.8 40.4 %copy-start.34 = (f32[256]{0:T(256)S(1)}, f32[256]{0:T(256)}, u32[]{:S(2)}) copy-start(f32[256]{0:T(256)} %get-tuple-element.60) | copy-start | bytes 3076
  493.1 17.3 %collective-permute-start.1 = (bf16[96,1536]{1,0:T(8,128)(2,1)}, bf16[96,1536]{1,0:T(8,128)(2,1)S(1)}, u32[]{:S(2)}, u32[]{:S(2)}) collective-permute-start(bf16[96,1536]{1,0:T(8,128)(2,1)} %reduce-scatter.9.cloned.1.call-done), channel_id=1, source_target_pairs={{0,0},{8,1},{1,2},{9,3},{2,4},{10,5},{3,6},{11,7},{4,8},{12,9},{5,... | collective-permute-start | bytes 884744 | tf_op jit(solution)/shard_map/ppermute | solution.py:414
  (27 other events, 96.8 us)
Sparse Core Ops, SparseCore 0:
  34.4 42.2 all-gather.2
  78.9 88.2 all-gather.4
  424.1 28.2 reduce-scatter.8
  455.1 21.7 reduce-scatter.12
  479.0 38.1 reduce-scatter.6
  519.4 62.4 reduce-scatter.10

commit v2 on v1

v2 whole, which is shorter than its diff:
```python
import functools
import math

import jax
import jax.numpy as jnp
import numpy as np
from jax import lax
from jax.experimental import pallas as pl
from jax.experimental.pallas import tpu as pltpu
from jax.sharding import Mesh
from jax.sharding import PartitionSpec as P

QUERY_HEADS = 16
KEY_VALUE_HEADS = 8
HEAD_SIZE = 96
FF = 4096
BLK = 128
LANES = 128
QUERY_BLOCK = 512
CHUNKS = 4

EPSILON = 1e-05
THETA = 100000.0
MASK_FILL = -1e30
BF = jnp.bfloat16
F32 = jnp.float32
ALL = ("o", "i", "ctx")
MESH = pl.DeviceIdType.MESH
SCALE = 1.0 / math.sqrt(HEAD_SIZE)


def nt(a, b):
    return lax.dot_general(a, b, (((1,), (1,)), ((), ())), preferred_element_type=F32)


def nn(a, b):
    return lax.dot_general(a, b, (((1,), (0,)), ((), ())), preferred_element_type=F32)


def tn(a, b):
    return lax.dot_general(a, b, (((0,), (0,)), ((), ())), preferred_element_type=F32)


def z_ag(x):
    return lax.all_gather(x, "o", axis=0, tiled=True)


def z_rs(x):
    return lax.psum_scatter(x, "o", scatter_dimension=0, tiled=True)


def inv_rms(x):
    return lax.rsqrt(jnp.mean(x * x, -1, keepdims=True) + EPSILON)


def norm_back(grad_normed, gain, source, scale):
    weighted = grad_normed * gain
    return scale * weighted - source * scale**3 * jnp.mean(weighted * source, -1, keepdims=True)


def feature_moves(n_outer, n_plane):
    moves = []
    half, quarter = n_outer // 2, n_outer // 4
    for block in range(n_outer * n_plane):
        if block < 4 * n_outer:
            place, step = block // half, block % half
        elif block < 6 * n_outer:
            place, step = divmod(block - 4 * n_outer, quarter)
            step += half
        else:
            place, step = divmod(block - 6 * n_outer, quarter)
            step += half + quarter
        moves.append((block, step * n_plane + place))
    return moves


def pad_heads(x, axis):
    half = HEAD_SIZE // 2
    shape = x.shape
    x = x.reshape(shape[:axis] + (-1, half) + shape[axis + 1 :])
    pads = [(0, 0)] * x.ndim
    pads[axis + 1] = (0, LANES // 2 - half)
    return jnp.pad(x, pads).reshape(shape[:axis] + (-1,) + shape[axis + 1 :])


def cut_heads(x, axis):
    half = HEAD_SIZE // 2
    shape = x.shape
    x = x.reshape(shape[:axis] + (-1, LANES // 2) + shape[axis + 1 :])
    x = lax.slice_in_dim(x, 0, half, axis=axis + 1)
    return x.reshape(shape[:axis] + (-1,) + shape[axis + 1 :])


def pack_down(w, chunks):
    width, units = w.shape
    span = width // units
    w = w.reshape(chunks, span, width // (chunks * span), units)
    return w.transpose(0, 2, 1, 3).reshape(chunks, -1, width)


def in_chunks(weights, unit_rows, units):
    n_outer, _, width = weights.shape
    if n_outer == CHUNKS:
        return weights
    gate_up = weights[:, :unit_rows].reshape(CHUNKS, -1, width)
    down = weights[:, unit_rows:].reshape(n_outer, -1, width // units, units).transpose(0, 2, 1, 3)
    return jnp.concatenate([gate_up, pack_down(down.reshape(width, units), CHUNKS)], 1)


def places(n_ctx):
    o, i, c = lax.axis_index("o"), lax.axis_index("i"), lax.axis_index("ctx")
    return o, i, c, c + 1 - 2 * (c % 2), (c + n_ctx // 2) % n_ctx


def greet(devices):
    barrier = pltpu.get_barrier_semaphore()
    for device in devices:
        pl.semaphore_signal(barrier, inc=1, device_id=device, device_id_type=MESH)
    pl.semaphore_wait(barrier, len(devices))


def greet_neighbours(n_ctx):
    o, i, c, mate, far = places(n_ctx)
    greet([(o, i, mate), (o, 1 - i, c), (o, i, far)])


def send(src, dst, send_sem, recv_sem, device):
    copy = pltpu.make_async_remote_copy(
        src_ref=src, dst_ref=dst, send_sem=send_sem, recv_sem=recv_sem, device_id=device, device_id_type=MESH
    )
    copy.start()
    return copy


class Gather:
    def __init__(self, n_ctx, src, out, send_sem, recv_sem, local_sem):
        self.src, self.out, self.sems = src, out, (send_sem, recv_sem, local_sem)
        o, i, c, mate, far = places(n_ctx)
        j, core = 1 - i, c % 2
        self.mate, self.x, self.y = (o, i, mate), (o, j, c), (o, i, far)
        self.me, self.s_x = i * n_ctx + c, j * n_ctx + c
        self.s_y, self.s_d = i * n_ctx + far, j * n_ctx + far
        self.relay = (o, j * core + i * (1 - core), c * core + far * (1 - core))
        self.relayed = self.s_y * core + self.s_x * (1 - core)
        mate_far = (mate + n_ctx // 2) % n_ctx
        self.mates_slots = [i * n_ctx + mate, j * n_ctx + mate, i * n_ctx + mate_far, j * n_ctx + mate_far]
        self.copies = {}

    def go(self, kind, src, slot, device):
        copy = send(src, self.out.at[slot], self.sems[0].at[kind], self.sems[1].at[kind], device)
        self.copies[kind] = copy

    def begin(self):
        self.go(1, self.src, self.me, self.x)
        self.go(2, self.src, self.me, self.y)
        self.go(0, self.src, self.me, self.mate)
        self.own = pltpu.make_async_copy(self.src, self.out.at[self.me], self.sems[2])
        self.own.start()

    def middle(self):
        self.copies[1].wait_recv()
        self.copies[2].wait_recv()
        self.go(5, self.out.at[self.relayed], self.relayed, self.relay)
        self.go(3, self.out.at[self.s_x], self.s_x, self.mate)
        self.go(4, self.out.at[self.s_y], self.s_y, self.mate)

    def corner(self):
        self.copies[5].wait_recv()
        self.go(6, self.out.at[self.s_d], self.s_d, self.mate)

    def arrived(self, kind):
        self.copies[kind].wait_recv()

    def sent(self):
        self.own.wait()
        for copy in self.copies.values():
            copy.wait_send()

    def end(self):
        self.corner()
        for kind in (0, 3, 4, 6):
            self.arrived(kind)
        self.sent()


GATHER_SEMS = [pltpu.SemaphoreType.DMA((7,)), pltpu.SemaphoreType.DMA((7,)), pltpu.SemaphoreType.DMA]


class Scatter:
    def __init__(self, n_ctx, partial, tile, ready, from_mate, going, got, send_sem, recv_sem, total):
        self.partial, self.tile = partial, tile
        self.ready, self.from_mate, self.going, self.got = ready, from_mate, going, got
        self.sems, self.total = (send_sem, recv_sem), total
        o, i, c, mate, far = places(n_ctx)
        j, core = 1 - i, c % 2
        self.core = core
        far_mate = (mate + n_ctx // 2) % n_ctx
        self.mine = [j * n_ctx + far, j * n_ctx + c, i * n_ctx + far, i * n_ctx + c]
        self.theirs = [j * n_ctx + far_mate, j * n_ctx + mate, i * n_ctx + far_mate, i * n_ctx + mate]
        self.mate = (o, i, mate)
        self.combined = (o, j * (1 - core) + i * core, c * (1 - core) + far * core)
        self.direct = (o, j * core + i * (1 - core), c * core + far * (1 - core))
        self.s_direct = self.mine[2] * (1 - core) + self.mine[1] * core
        self.s_combined = self.mine[1] * (1 - core) + self.mine[2] * core
        self.copies = []

    def go(self, kind, part, src, dst, device):
        copy = send(src.at[part], dst.at[part], self.sems[0].at[kind, part], self.sems[1].at[kind, part], device)
        self.copies.append(copy)
        return copy

    def each(self, part, body):
        tiles = self.ready.shape[-1] // self.tile

        @pl.loop(0, tiles)
        def _(t):
            at = pl.multiple_of(t * self.tile, self.tile)
            body(part * tiles + t, pl.ds(at, self.tile), pl.ds(part * tiles * self.tile + at, self.tile))

    def fill(self, n, part):
        def body(t, lanes, _):
            self.ready[n, part, :, lanes] = self.partial(self.theirs[n], t).astype(BF)

        self.each(part, body)

    def give(self, n, part):
        self.mates[n, part] = self.go(n, part, self.ready.at[n], self.from_mate.at[n], self.mate)

    def pair(self, slot, n, part, place):
        def body(t, lanes, _):
            pair = self.partial(slot, t) + self.from_mate[n, part, :, lanes].astype(F32)
            self.going[place, part, :, lanes] = pair.astype(BF)

        self.each(part, body)

    def to_mate(self):
        self.mates, self.straights, self.diagonals, self.joins = {}, [], [], []
        order = [(0, 0), (0, 1), (1, 0), (2, 0), (1, 1), (2, 1), (3, 0), (3, 1)]
        self.fill(*order[0])
        for k, at in enumerate(order[1:]):
            self.fill(*at)
            self.give(*order[k])
            if k == 2:
                self.mates[0, 0].wait_recv()
                self.pair(self.mine[0], 0, 0, 0)
            if k == 3:
                self.diagonals.append(self.go(4, 0, self.going.at[0], self.got.at[0], self.direct))
                self.mates[0, 1].wait_recv()
                self.pair(self.mine[0], 0, 1, 0)
            if k == 4:
                self.diagonals.append(self.go(4, 1, self.going.at[0], self.got.at[0], self.direct))
        self.last = order[-1]

    def pairs(self):
        for part in range(PARTS):
            self.mates[1, part].wait_recv()
            self.mates[2, part].wait_recv()
            self.pair(self.s_direct, 2 - self.core, part, 1)
            if part == 0:
                self.give(*self.last)
            else:
                self.straights.append(self.go(5, part - 1, self.going.at[1], self.got.at[1], self.direct))

    def join(self):
        for part in range(PARTS):
            self.diagonals[part].wait_recv()

            def combined(t, lanes, _):
                pair = self.partial(self.s_combined, t) + self.from_mate[1 + self.core, part, :, lanes].astype(F32)
                self.going[2, part, :, lanes] = (pair + self.got[0, part, :, lanes].astype(F32)).astype(BF)

            self.each(part, combined)
            if part == 0:
                self.straights.append(self.go(5, PARTS - 1, self.going.at[1], self.got.at[1], self.direct))
            else:
                self.joins.append(self.go(6, part - 1, self.going.at[2], self.got.at[2], self.combined))
        self.own(0)
        self.joins.append(self.go(6, PARTS - 1, self.going.at[2], self.got.at[2], self.combined))

    def own(self, part):
        self.mates[3, part].wait_recv()

        def body(t, lanes, out):
            self.total[:, out] = self.partial(self.mine[3], t) + self.from_mate[3, part, :, lanes].astype(F32)

        self.each(part, body)

    def end(self):
        total = self.total
        for part in range(1, PARTS):
            self.own(part)
        for part in range(PARTS):
            self.straights[part].wait_recv()
            self.joins[part].wait_recv()

            def rest(t, lanes, out):
                other = self.got[1, part, :, lanes].astype(F32) + self.got[2, part, :, lanes].astype(F32)
                total[:, out] = total[:, out] + other

            self.each(part, rest)
        for copy in self.copies:
            copy.wait_send()


PARTS = 2


def scatter_scratch(rows, width):
    return [
        pltpu.VMEM((4, PARTS, rows, width // PARTS), BF),
        pltpu.VMEM((4, PARTS, rows, width // PARTS), BF),
        pltpu.VMEM((3, PARTS, rows, width // PARTS), BF),
        pltpu.VMEM((3, PARTS, rows, width // PARTS), BF),
        pltpu.SemaphoreType.DMA((7, PARTS)),
        pltpu.SemaphoreType.DMA((7, PARTS)),
        pltpu.VMEM((rows, width), F32),
    ]


def row_chunks(rows, step, body):
    @pl.loop(0, rows // step)
    def _(r):
        body(pl.ds(pl.multiple_of(r * step, step), step))


class Load:
    def __init__(self, parts, sem):
        self.copies = [pltpu.make_async_copy(src, dst, sem.at[n]) for n, (src, dst) in enumerate(parts)]

    def begin(self):
        for copy in self.copies:
            copy.start()
        return self

    def wait(self):
        for copy in self.copies:
            copy.wait()


IN_VMEM = pl.BlockSpec(memory_space=pltpu.VMEM)
ANYWHERE = pl.BlockSpec(memory_space=pl.ANY)


def remote_call(kernel, name, number, ins, outs, scratch, any_outs=(), any_ins=()):
    return pl.pallas_call(
        kernel,
        out_shape=outs,
        in_specs=[ANYWHERE if n in any_ins else IN_VMEM for n in range(len(ins))],
        out_specs=[ANYWHERE if n in any_outs else IN_VMEM for n in range(len(outs))],
        scratch_shapes=scratch,
        compiler_params=pltpu.CompilerParams(collective_id=number, has_side_effects=True, vmem_limit_bytes=60 << 20),
        name=name,
    )(*ins)


def shape(dims, dtype):
    return jax.ShapeDtypeStruct(tuple(dims), dtype)


class Swap:
    def __init__(self, n_ctx, pairs, send_sem, recv_sem, local_sem):
        self.pairs, self.sems = pairs, (send_sem, recv_sem, local_sem)
        self.o, i, c, _, _ = places(n_ctx)
        self.n, self.n_ctx = 2 * n_ctx, n_ctx
        self.me = i * n_ctx + c
        self.others = [(self.me + k) % self.n for k in range(1, self.n)]
        self.devices = [(self.o, d // n_ctx, d % n_ctx) for d in self.others]

    def begin(self):
        self.copies, self.own = [], []
        for a, (src, dst) in enumerate(self.pairs):
            for k, (d, device) in enumerate(zip(self.others, self.devices)):
                self.copies.append(
                    send(src.at[d], dst.at[self.me], self.sems[0].at[a, k], self.sems[1].at[a, k], device)
                )
            own = pltpu.make_async_copy(src.at[self.me], dst.at[self.me], self.sems[2].at[a])
            own.start()
            self.own.append(own)

    def end(self):
        for copy in self.copies:
            copy.wait_recv()
            copy.wait_send()
        for copy in self.own:
            copy.wait()


def swap_sems(n_arrays, n_ctx):
    return [
        pltpu.SemaphoreType.DMA((n_arrays, 2 * n_ctx - 1)),
        pltpu.SemaphoreType.DMA((n_arrays, 2 * n_ctx - 1)),
        pltpu.SemaphoreType.DMA((n_arrays,)),
    ]


def outer_peers(n_outer):
    o, i, c = lax.axis_index("o"), lax.axis_index("i"), lax.axis_index("ctx")
    return [(lax.rem(o + k, n_outer), i, c) for k in range(1, n_outer)]


def rotary_constants():
    frequency = THETA ** -(np.arange(HEAD_SIZE // 2) * (2.0 / HEAD_SIZE))
    rates = np.zeros((8, LANES), np.float32)
    for half, sign in ((0, -1.0), (LANES // 2, 1.0)):
        rates[0, half : half + HEAD_SIZE // 2] = frequency
        rates[1, half : half + HEAD_SIZE // 2] = sign
    angles = np.arange(BLK)[:, None] * rates[0].astype(np.float64)
    return rates, np.stack([np.cos(angles), np.sin(angles)]).astype(np.float32)


def exchange(meta, gains, n_outer, n_ctx, number):
    n = 2 * n_ctx

    def kernel(meta_ref, gains_ref, metas_out, gains_out, send_sem, recv_sem, local_sem):
        o, i, c, _, _ = places(n_ctx)
        me = i * n_ctx + c
        plane = [lax.rem(me + k, n) for k in range(1, n)]
        plane = [(o, d // n_ctx, d % n_ctx) for d in plane]
        peers = outer_peers(n_outer)
        greet(plane + peers)
        first, second, later = [], [], []
        for k, device in enumerate(plane):
            first.append(send(gains_ref, gains_out.at[o, me], send_sem.at[0, k], recv_sem.at[0, k], device))
        own = [
            pltpu.make_async_copy(gains_ref, gains_out.at[o, me], local_sem.at[0]),
            pltpu.make_async_copy(meta_ref, metas_out.at[me], local_sem.at[1]),
        ]
        for copy in own:
            copy.start()
        for k, device in enumerate(plane):
            later.append(send(meta_ref, metas_out.at[me], send_sem.at[1, k], recv_sem.at[1, k], device))
        for copy in own:
            copy.wait()
        for copy in first:
            copy.wait_recv()
        for k, device in enumerate(peers):
            second.append(send(gains_out.at[o], gains_out.at[o], send_sem.at[2, k], recv_sem.at[2, k], device))
        for copy in second + later:
            copy.wait_recv()
        for copy in first + second + later:
            copy.wait_send()

    outs = [shape((n,) + meta.shape, meta.dtype), shape((n_outer, n) + gains.shape, F32)]
    most = max(n, n_outer) - 1
    sems = [pltpu.SemaphoreType.DMA((3, most)), pltpu.SemaphoreType.DMA((3, most)), pltpu.SemaphoreType.DMA((2,))]
    return remote_call(kernel, "exchange", number, [meta, gains], outs, sems)


def prologue(xn, outs_parts, down_parts, metas, n_seqs, n_ctx, number):
    rows, width = xn.shape
    n = 2 * n_ctx
    blocks = n_ctx * rows // BLK

    def kernel(
        x_ref,
        out_src,
        down_src,
        metas_ref,
        rates_ref,
        angles_ref,
        xn_all,
        out_dst,
        down_dst,
        cos_ref,
        sin_ref,
        rows_ref,
        columns_ref,
        *sems,
    ):
        out_swap = Swap(n_ctx, [(out_src, out_dst), (down_src, down_dst)], *sems[:3])
        gather = Gather(n_ctx, x_ref, xn_all, *sems[3:6])
        greet(out_swap.devices)
        gather.begin()
        lane = lax.broadcasted_iota(jnp.int32, (BLK, LANES), 1)
        row = lax.broadcasted_iota(jnp.int32, (BLK, LANES), 0)
        rows_ref[...] = jnp.zeros_like(rows_ref)
        pieces = 2 * blocks * n_seqs
        piece = lax.broadcasted_iota(jnp.int32, (pieces, LANES), 0)
        bases = jnp.zeros((pieces, LANES), jnp.int32)
        places_of = []
        for g in range(2):
            starts, end = [], jnp.zeros((1, 1), jnp.int32)
            for q in range(n_seqs):
                starts.append(end)
                end = end + metas_ref[g * n_ctx, 0:1, q : q + 1]
            for b in range(blocks):
                first = metas_ref[g * n_ctx, 0:1, n_seqs + b : n_seqs + b + 1] * BLK
                for q in range(n_seqs):
                    index = (g * blocks + b) * n_seqs + q
                    bases = jnp.where(piece == index, first - starts[q], bases)
                places_of.append((first, starts))
        angle = bases.astype(F32) * rates_ref[0:1]
        base_cos, base_sin = jnp.cos(angle), jnp.sin(angle)
        for n_block, (first, starts) in enumerate(places_of):
            at = slice(n_block * BLK, (n_block + 1) * BLK)
            stream, lanes_stream = first + row, first + lane[0:1]
            start, lanes_start = jnp.zeros_like(stream), jnp.zeros_like(lanes_stream)
            cos, sin = angles_ref[0], angles_ref[1]
            for q in range(n_seqs):
                index = n_block * n_seqs + q
                cos_0, sin_0 = base_cos[index : index + 1], base_sin[index : index + 1]
                cos_q = cos_0 * angles_ref[0] - sin_0 * angles_ref[1]
                sin_q = sin_0 * angles_ref[0] + cos_0 * angles_ref[1]
                inside = stream >= starts[q]
                start = jnp.where(inside, starts[q], start)
                lanes_start = jnp.where(lanes_stream >= starts[q], starts[q], lanes_start)
                cos, sin = jnp.where(inside, cos_q, cos), jnp.where(inside, sin_q, sin)
            cos_ref[at] = cos
            sin_ref[at] = sin * rates_ref[1:2]
            columns_ref[at] = jnp.where(lane == 0, stream, start)
            rows_ref[0:1, at] = lanes_stream
            rows_ref[1:2, at] = lanes_start
        gather.middle()
        out_swap.begin()
        gather.end()
        out_swap.end()

    outs = [
        shape((n, rows, width), BF),
        shape(outs_parts.shape, BF),
        shape(down_parts.shape, BF),
        shape((n * rows, LANES), F32),
        shape((n * rows, LANES), F32),
        shape((8, n * rows), jnp.int32),
        shape((n * rows, LANES), jnp.int32),
    ]
    rates, angles = rotary_constants()
    ins = [xn, outs_parts, down_parts, metas, jnp.asarray(rates), jnp.asarray(angles)]
    return remote_call(kernel, "prologue", number, ins, outs, swap_sems(2, n_ctx) + GATHER_SEMS, any_outs=(0,))


def plane_gather(x, n_ctx, number):
    def kernel(src, out, *sems):
        gather = Gather(n_ctx, src, out, *sems)
        greet_neighbours(n_ctx)
        gather.begin()
        gather.middle()
        gather.end()

    outs = [shape((2 * n_ctx,) + x.shape, x.dtype)]
    got = remote_call(kernel, f"gather_{number}", number, [x], outs, GATHER_SEMS, any_outs=(0,))
    return got[0].reshape(-1, x.shape[-1])


def rotate(x, cosine, sine):
    return x * cosine + pltpu.roll(x, LANES // 2, 1) * sine


def padded_loads(w_ref, w_pad):
    half = HEAD_SIZE // 2
    rows = w_ref.shape[1]
    pairs, at = [], 0
    for row in range(half, w_pad.shape[0], LANES // 2):
        w_pad[row : row + LANES // 2 - half] = jnp.zeros((LANES // 2 - half, w_pad.shape[1]), BF)
    for n in range(w_ref.shape[0]):
        for b in range(rows // half):
            src = w_ref.at[n, pl.ds(b * half, half)]
            pairs.append((src, w_pad.at[pl.ds(at * LANES // 2, half)]))
            at += 1
    return pairs


def attention_forward(xn, w, cosine, sine, pos_rows, pos_columns, dy, n_ctx, number):
    rows, width = xn.shape
    group = rows // 2
    heads = QUERY_HEADS // (2 * n_ctx)
    features = (heads + 2) * LANES
    k_at, v_at = heads * LANES, (heads + 1) * LANES
    block = min(QUERY_BLOCK, group)
    n_loads = w.shape[0] * w.shape[1] // (HEAD_SIZE // 2)

    def kernel(
        xn_ref, w_hbm, cos_ref, sin_ref, rows_ref, columns_ref, dy_ref, qkv_ref, attn_ref, lse_ref, dy_all, w_ref, load_sem, *sems
    ):
        gather = Gather(n_ctx, dy_ref, dy_all, *sems)
        load = Load(padded_loads(w_hbm, w_ref), load_sem).begin()
        greet_neighbours(n_ctx)
        gather.begin()
        load.wait()

        def project(r):
            cos, sin = cos_ref[r], sin_ref[r]
            for h in range(heads + 2):
                lanes = slice(h * LANES, (h + 1) * LANES)
                part = nt(xn_ref[r], w_ref[lanes])
                qkv_ref[r, lanes] = (rotate(part, cos, sin) if h <= heads else part).astype(BF)

        def attend(g):
            keys_at = pl.ds(g * group, group)

            @pl.loop(0, group // block)
            def _(b):
                r = pl.ds(pl.multiple_of(g * group + b * block, block), block)
                key_pos = rows_ref[0:1, keys_at]
                ok = (key_pos >= columns_ref[r, 1:2]) & (key_pos <= columns_ref[r, 0:1])
                for h in range(heads):
                    lanes = slice(h * LANES, (h + 1) * LANES)
                    s = nt(qkv_ref[r, lanes], qkv_ref[keys_at, k_at : k_at + LANES])
                    s = jnp.where(ok, s, MASK_FILL)
                    high = jnp.max(s, -1, keepdims=True)
                    e = jnp.exp((s - high) * SCALE)
                    total = jnp.sum(e, -1, keepdims=True)
                    mixed = nn(e.astype(BF), qkv_ref[keys_at, v_at : v_at + LANES])
                    attn_ref[r, lanes] = (mixed / total).astype(BF)
                    lse = jnp.broadcast_to(high * SCALE + jnp.log(total), (block, LANES))
                    lse_ref[h : h + 1, r] = jnp.transpose(lse)[0:1]

        row_chunks(rows, block, project)
        attend(0)
        gather.middle()
        attend(1)
        gather.end()

    outs = [
        shape((rows, features), BF),
        shape((rows, heads * LANES), BF),
        shape((8, rows), F32),
        shape((2 * n_ctx,) + dy.shape, BF),
    ]
    ins = [xn, w, cosine, sine, pos_rows, pos_columns, dy]
    scratch = [pltpu.VMEM((features, width), BF), pltpu.SemaphoreType.DMA((n_loads,))] + GATHER_SEMS
    got = remote_call(kernel, "attention_forward", number, ins, outs, scratch, any_outs=(3,), any_ins=(1,))
    return got[0], got[1], got[2], got[3].reshape(rows, width)


def out_loads(w_ref, w_pad):
    features = w_pad.shape[1]
    chunks, _, width = w_ref.shape
    rows = features // chunks
    span = width // features
    pairs = []
    for n in range(chunks):
        for b in range(span):
            dst = w_pad.at[pl.ds((n * span + b) * rows, rows)]
            pairs.append((w_ref.at[n, pl.ds(0, rows), pl.ds(b * features, features)], dst))
    return pairs


def output_projection(attn, out_w, tokens, gain, n_ctx, number):
    rows, width = tokens.shape
    tile = 256

    features = attn.shape[1]

    def kernel(attn_ref, w_hbm, x_ref, gain_ref, h_ref, xn_ref, w_ref, load_sem, *scratch):
        total = scratch[-1]
        load = Load(out_loads(w_hbm, w_ref), load_sem).begin()

        def partial(slot, t):
            a = attn_ref[pl.ds(pl.multiple_of(slot * rows, rows), rows)]
            return nt(a, w_ref[pl.ds(pl.multiple_of(t * tile, tile), tile)])

        scatter = Scatter(n_ctx, partial, tile, *scratch)
        greet_neighbours(n_ctx)
        load.wait()
        scatter.to_mate()
        scatter.pairs()
        scatter.join()
        scatter.end()

        def finish(r):
            h = x_ref[r].astype(F32) + total[r]
            h_ref[r] = h
            xn_ref[r] = (h * inv_rms(h) * gain_ref[1:2]).astype(BF)

        row_chunks(rows, 32, finish)

    outs = [shape((rows, width), F32), shape((rows, width), BF)]
    n_loads = out_w.shape[0] * width // features
    scratch = [pltpu.VMEM((width, features), BF), pltpu.SemaphoreType.DMA((n_loads,))] + scatter_scratch(rows, width)
    return remote_call(kernel, "output_projection", number, [attn, out_w, tokens, gain], outs, scratch, any_ins=(1,))


def feed_forward(xn, dy, weights, unit_rows, number_of_units):
    rows, width = xn.shape
    n_outer = weights.shape[0]
    block = 256
    pack = weights.shape[1] - unit_rows
    span = width // number_of_units

    def kernel(x_ref, dy_ref, w_ref, hidden_ref, dgu_ref):
        x, dy = x_ref[...], dy_ref[...]
        half = n_outer // 2
        for n in range(half):
            lanes = slice(n * unit_rows, (n + 1) * unit_rows)
            gate = nt(x, w_ref[n, :unit_rows])
            up = nt(x, w_ref[half + n, :unit_rows])
            dhid = jnp.zeros_like(gate)
            for m in range(n_outer):
                for b in range(span):
                    at = (m * span + b) * pack
                    u = b * number_of_units + n * unit_rows
                    dhid = dhid + nn(dy[:, at : at + pack], w_ref[m, unit_rows:, u : u + unit_rows])
            sg = 1.0 / (1.0 + jnp.exp(-gate))
            act = gate * sg
            hidden_ref[:, lanes] = (act * up).astype(BF)
            dgu_ref[:, lanes] = (dhid * up * sg * (1.0 + gate * (1.0 - sg))).astype(BF)
            second = slice(number_of_units + n * unit_rows, number_of_units + (n + 1) * unit_rows)
            dgu_ref[:, second] = (dhid * act).astype(BF)

    return pl.pallas_call(
        kernel,
        grid=(rows // block,),
        out_shape=[shape((rows, number_of_units), BF), shape((rows, 2 * number_of_units), BF)],
        in_specs=[
            pl.BlockSpec((block, width), lambda b: (b, 0)),
            pl.BlockSpec((block, width), lambda b: (b, 0)),
            IN_VMEM,
        ],
        out_specs=[
            pl.BlockSpec((block, number_of_units), lambda b: (b, 0)),
            pl.BlockSpec((block, 2 * number_of_units), lambda b: (b, 0)),
        ],
        compiler_params=pltpu.CompilerParams(vmem_limit_bytes=60 << 20),
        cost_estimate=pl.CostEstimate(
            flops=6 * rows * width * number_of_units, bytes_accessed=4 * rows * width, transcendentals=rows * number_of_units
        ),
        name="feed_forward",
    )(xn, dy, weights)


def feed_forward_input(dgu, weights, unit_rows, h1, cotangent, gain, n_ctx, number):
    rows, width = h1.shape
    n_outer = weights.shape[0]
    tile = 256

    def kernel(dgu_ref, w_ref, h_ref, dy_ref, gain_ref, dh_ref, dhb_ref, dgain_ref, *scratch):
        total = scratch[-1]

        def partial(slot, t):
            r = pl.ds(pl.multiple_of(slot * rows, rows), rows)
            lanes = pl.ds(pl.multiple_of(t * tile, tile), tile)
            acc = nn(dgu_ref[r, :unit_rows], w_ref[0, :unit_rows, lanes])
            for n in range(1, n_outer):
                acc = acc + nn(dgu_ref[r, n * unit_rows : (n + 1) * unit_rows], w_ref[n, :unit_rows, lanes])
            return acc

        scatter = Scatter(n_ctx, partial, tile, *scratch)
        greet_neighbours(n_ctx)
        scatter.to_mate()
        scatter.pairs()
        scatter.join()
        scatter.end()
        dgain_ref[...] = jnp.zeros_like(dgain_ref)

        def finish(r):
            h, d = h_ref[r], total[r]
            scale = inv_rms(h)
            dgain_ref[0:1] += jnp.sum(d * h * scale, 0, keepdims=True)
            dh = dy_ref[r].astype(F32) + norm_back(d, gain_ref[1:2], h, scale)
            dh_ref[r] = dh
            dhb_ref[r] = dh.astype(BF)

        row_chunks(rows, 32, finish)

    outs = [shape((rows, width), F32), shape((rows, width), BF), shape((8, width), F32)]
    return remote_call(
        kernel,
        "feed_forward_input",
        number,
        [dgu, weights, h1, cotangent, gain],
        outs,
        scatter_scratch(rows, width),
    )


def attention_backward(
    dh_all, out_w, qkv, attn, lse, cosine, sine, pos_rows, pos_columns, hidden, weights, unit_rows, h1, swapped, g_out, n_outer, n_ctx, number
):
    rows = dh_all.shape[0]
    own_rows, width = h1.shape
    group = rows // 2
    heads = attn.shape[1] // LANES
    k_at, v_at = heads * LANES, (heads + 1) * LANES
    block = min(QUERY_BLOCK, group)
    pack = weights.shape[1] - unit_rows
    units = hidden.shape[1]
    span = width // units

    def kernel(
        dh_hbm,
        ow_hbm,
        qkv_ref,
        attn_ref,
        lse_ref,
        cos_ref,
        sin_ref,
        rows_ref,
        columns_ref,
        hidden_ref,
        w_hbm,
        h_ref,
        swap_src,
        g_ref,
        dproj_ref,
        result_ref,
        swap_dst,
        g_dst,
        g_arrived,
        g_sum,
        g_send,
        g_recv,
        dk_ref,
        dv_ref,
        w_ref,
        out_w_ref,
        dh_ref,
        load_sem,
        out_load_sem,
        dh_sem,
        *scratch,
    ):
        swap_sem, g_swap_sem, scratch = scratch[:3], scratch[3:6], scratch[6:]
        total = scratch[-1]
        o = lax.axis_index("o")
        peers = outer_peers(n_outer)
        load = Load([(w_hbm.at[:, pl.ds(unit_rows, pack)], w_ref)], load_sem).begin()
        out_load = Load(out_loads(ow_hbm, out_w_ref), out_load_sem).begin()
        dh_load = Load([(dh_hbm, dh_ref)], dh_sem).begin()
        swap = Swap(n_ctx, [(swap_src, swap_dst)], *swap_sem)
        g_swap = Swap(n_ctx, [(g_sum, g_dst)], *g_swap_sem)

        def partial(slot, t):
            a = hidden_ref[pl.ds(pl.multiple_of(slot * own_rows, own_rows), own_rows)]
            lanes = pl.ds(pl.multiple_of((t % span) * units, units), units)
            return nt(a, w_ref[t // span, :, lanes])

        scatter = Scatter(n_ctx, partial, pack, *scratch)
        greet(swap.devices + peers)
        g_copies = [
            send(g_ref.at[device[0]], g_arrived.at[k], g_send.at[k], g_recv.at[k], device) for k, device in enumerate(peers)
        ]

        def back(g):
            keys_at = pl.ds(g * group, group)
            dk_ref[...] = jnp.zeros_like(dk_ref)
            dv_ref[...] = jnp.zeros_like(dv_ref)

            @pl.loop(0, group // block)
            def _(b):
                r = pl.ds(pl.multiple_of(g * group + b * block, block), block)
                key_pos = columns_ref[keys_at, 0:1]
                ok = (key_pos >= rows_ref[1:2, r]) & (key_pos <= rows_ref[0:1, r])
                da_all = nn(dh_ref[r], out_w_ref[...]).astype(BF)
                for h in range(heads):
                    lanes = slice(h * LANES, (h + 1) * LANES)
                    da, q = da_all[:, lanes], qkv_ref[r, lanes]
                    keys = qkv_ref[keys_at, k_at : k_at + LANES]
                    s = nt(keys, q) * SCALE - lse_ref[h : h + 1, r]
                    p = jnp.exp(jnp.where(ok, s, MASK_FILL))
                    dv_ref[...] += nn(p.astype(BF), da)
                    delta = jnp.transpose(da.astype(F32) * attn_ref[r, lanes].astype(F32))
                    delta = jnp.sum(delta, 0, keepdims=True)
                    dp = nt(qkv_ref[keys_at, v_at : v_at + LANES], da)
                    ds = (p * (dp - delta)).astype(BF)
                    dk_ref[...] += nn(ds, q)
                    dq = tn(ds, keys) * SCALE
                    dproj_ref[r, lanes] = rotate(dq, cos_ref[r], -sin_ref[r]).astype(BF)

            dk = rotate(dk_ref[...] * SCALE, cos_ref[keys_at], -sin_ref[keys_at])
            dproj_ref[keys_at, k_at : k_at + LANES] = dk.astype(BF)
            dproj_ref[keys_at, v_at : v_at + LANES] = dv_ref[...].astype(BF)

        load.wait()
        scatter.to_mate()
        scatter.pairs()
        swap.begin()
        out_load.wait()
        dh_load.wait()
        back(0)
        scatter.join()
        for copy in g_copies:
            copy.wait_recv()
        for d in range(2 * n_ctx):
            g_part = g_ref[o, d].astype(F32)
            for k in range(n_outer - 1):
                g_part = g_part + g_arrived[k, d].astype(F32)
            g_sum[d] = g_part.astype(BF)
        back(1)
        g_swap.begin()
        scatter.end()
        swap.end()

        def finish(r):
            result_ref[r] = (h_ref[r] + total[r]).astype(BF)

        row_chunks(own_rows, 32, finish)
        g_swap.end()
        for copy in g_copies:
            copy.wait_send()

    outs = [shape(qkv.shape, BF), shape((own_rows, width), BF), shape(swapped.shape, BF), shape(g_out.shape[1:], BF)]
    ins = [dh_all, out_w, qkv, attn, lse, cosine, sine, pos_rows, pos_columns, hidden, weights, h1, swapped, g_out]
    features = attn.shape[1]
    n_loads = out_w.shape[0] * width // features
    scratch = [
        pltpu.VMEM((n_outer - 1,) + g_out.shape[1:], BF),
        pltpu.VMEM(g_out.shape[1:], BF),
        pltpu.SemaphoreType.DMA((n_outer - 1,)),
        pltpu.SemaphoreType.DMA((n_outer - 1,)),
        pltpu.VMEM((group, LANES), F32),
        pltpu.VMEM((group, LANES), F32),
        pltpu.VMEM((weights.shape[0], pack, width), BF),
        pltpu.VMEM((width, features), BF),
        pltpu.VMEM(dh_all.shape, BF),
        pltpu.SemaphoreType.DMA((1,)),
        pltpu.SemaphoreType.DMA((n_loads,)),
        pltpu.SemaphoreType.DMA((1,)),
    ]
    scratch += swap_sems(1, n_ctx) + swap_sems(1, n_ctx) + scatter_scratch(own_rows, width)
    return remote_call(kernel, "attention_backward", number, ins, outs, scratch, any_ins=(0, 1, 10))


def attention_input(dproj, w, tokens, dh1, gain, gain_terms, n_outer, n_ctx, number):
    rows, width = tokens.shape
    tile = 256
    features = dproj.shape[1]
    n = 2 * n_ctx

    def kernel(
        d_ref, w_hbm, x_ref, dh_ref, gain_ref, terms_ref, out_ref, sum_ref, w_ref, load_sem, *scratch
    ):
        swap_sem, scratch = scratch[:3], scratch[3:]
        terms, summed, arrived, send_sem, recv_sem, local_sem = scratch[:6]
        scratch = scratch[6:]
        total = scratch[-1]
        load = Load(padded_loads(w_hbm, w_ref), load_sem).begin()
        o = lax.axis_index("o")

        def partial(slot, t):
            a = d_ref[pl.ds(pl.multiple_of(slot * rows, rows), rows)]
            return nn(a, w_ref[:, pl.ds(pl.multiple_of(t * tile, tile), tile)])

        scatter = Scatter(n_ctx, partial, tile, *scratch)
        swap = Swap(n_ctx, [(terms_ref, terms)], *swap_sem)
        peers = outer_peers(n_outer)
        greet(swap.devices + peers)
        swap.begin()
        load.wait()
        scatter.to_mate()
        scatter.pairs()
        swap.end()
        summed[...] = jnp.sum(terms[...], 0)
        scatter.join()
        copies = []
        for k, device in enumerate(peers):
            copies.append(send(summed.at[device[0]], arrived.at[o], send_sem.at[k], recv_sem.at[k], device))
        own = pltpu.make_async_copy(summed.at[o], arrived.at[o], local_sem)
        own.start()
        scatter.end()

        def finish(r):
            x, d = x_ref[r].astype(F32), total[r]
            out_ref[r] = dh_ref[r] + norm_back(d, gain_ref[0:1], x, inv_rms(x))

        row_chunks(rows, 32, finish)
        for copy in copies:
            copy.wait_recv()
        own.wait()
        sum_ref[...] = jnp.sum(arrived[...], 0)
        for copy in copies:
            copy.wait_send()

    outs = [shape((rows, width), F32), shape((8, LANES), F32)]
    ins = [dproj, w, tokens, dh1, gain, gain_terms]
    n_loads = w.shape[0] * w.shape[1] // (HEAD_SIZE // 2)
    scratch = [pltpu.VMEM((features, width), BF), pltpu.SemaphoreType.DMA((n_loads,))]
    scratch += swap_sems(1, n_ctx)
    scratch += [
        pltpu.VMEM((n, n_outer, 8, LANES), F32),
        pltpu.VMEM((n_outer, 8, LANES), F32),
        pltpu.VMEM((n_outer, 8, LANES), F32),
        pltpu.SemaphoreType.DMA((n_outer - 1,)),
        pltpu.SemaphoreType.DMA((n_outer - 1,)),
        pltpu.SemaphoreType.DMA,
    ]
    scratch += scatter_scratch(rows, width)
    return remote_call(kernel, "attention_input", number, ins, outs, scratch, any_ins=(1,))


def make_shards(n_outer, n_inner, n_ctx):
    n_plane = n_inner * n_ctx
    moves = feature_moves(n_outer, n_plane)
    back = [(b, a) for a, b in moves]

    def shards(tokens, norm_attn, w_qkv, w_out, norm_mlp, w_gate_up, w_down, cotangent, seq_lengths, block_slot):
        rows, width = tokens.shape
        gain_rows = norm_attn.shape[0]
        feature_rows = w_qkv.shape[0]
        out_rows = w_out.shape[0]
        unit_rows = w_gate_up.shape[0]
        n_seqs, n_slots = seq_lengths.shape[1], block_slot.shape[1]
        units = FF // n_plane
        gain_part = jnp.pad(jnp.stack([norm_attn, norm_mlp]), ((0, 6), (0, LANES - gain_rows)))
        meta = jnp.concatenate([seq_lengths[0], block_slot[0]])
        meta = jnp.pad(meta[None], ((0, 7), (0, LANES - n_seqs - n_slots)))
        moved_qkv = lax.ppermute(w_qkv, ALL, moves)
        metas, gains = exchange(meta, gain_part, n_outer, n_ctx, 0)
        gains = gains[:, :, :2, :gain_rows].transpose(2, 0, 1, 3).reshape(2, width)
        moved_qkv, metas = lax.optimization_barrier((moved_qkv, metas))
        qkv_w = z_ag(moved_qkv).reshape(CHUNKS, -1, width)
        source = tokens.astype(F32)
        xn1 = (source * inv_rms(source) * gains[0:1]).astype(BF)
        out_parts = pad_heads(w_out, 1).reshape(out_rows, n_plane, -1).transpose(1, 0, 2)
        down_parts = w_down.reshape(out_rows, n_outer // 2, n_plane, unit_rows).transpose(2, 0, 1, 3)
        down_parts = down_parts.reshape(n_plane, out_rows, units)
        xn1, out_parts, down_parts, cosine, sine, pos_rows, pos_columns = prologue(
            xn1, out_parts, down_parts, metas, n_seqs, n_ctx, 1
        )
        xn1 = xn1.reshape(-1, width)
        features = out_parts.shape[-1]
        out_pack = out_parts.reshape(width // features, -1, features).transpose(1, 0, 2).reshape(-1, width)
        short = -(-(1 << 20) // (2 * width * n_outer * 16)) * 16 - out_pack.shape[0]
        out_w = z_ag(jnp.pad(out_pack, ((0, max(short, 0)), (0, 0)))).reshape(n_outer, -1, width)
        if n_outer != CHUNKS:
            out_w = out_w[:, : out_pack.shape[0]].reshape(n_outer, -1, width // features, features).transpose(0, 2, 1, 3)
            out_w = pack_down(out_w.reshape(width, features), CHUNKS)
        down_pack = down_parts.reshape(width // units, -1, units).transpose(1, 0, 2).reshape(-1, width)
        mlp_w = z_ag(jnp.concatenate([w_gate_up, down_pack], 0)).reshape(n_outer, -1, width)
        mlp_w = in_chunks(mlp_w, unit_rows, units)
        qkv, attn, lse, dy_all = attention_forward(xn1, qkv_w, cosine, sine, pos_rows, pos_columns, cotangent, n_ctx, 2)
        h1, xn2 = output_projection(attn, out_w, tokens, gains, n_ctx, 3)
        xn2_all = plane_gather(xn2, n_ctx, 4)
        chunk_rows = 2 * units // CHUNKS
        hidden, dgu = feed_forward(xn2_all, dy_all, mlp_w, chunk_rows, units)
        g_down = tn(dy_all, hidden).astype(BF)
        dgu, g_down = lax.optimization_barrier((dgu, g_down))
        g_gate_up = tn(dgu, xn2_all).astype(BF)
        dgu, g_gate_up = lax.optimization_barrier((dgu, g_gate_up))
        g_down, g_gate_up = z_rs(g_down), z_rs(g_gate_up)
        dh1, dh1_bf, dgain_two = feed_forward_input(dgu, mlp_w, chunk_rows, h1, cotangent, gains, n_ctx, 5)
        dh1_all = plane_gather(dh1_bf, n_ctx, 6)
        dh1_all, g_gate_up, g_down = lax.optimization_barrier((dh1_all, g_gate_up, g_down))
        g_down = g_down.reshape(n_plane, out_rows, units)
        g_out = tn(dh1_all, attn).astype(BF).reshape(n_outer, n_plane, out_rows, -1)
        dproj, result, g_down, g_out = attention_backward(
            dh1_all, out_w, qkv, attn, lse, cosine, sine, pos_rows, pos_columns, hidden, mlp_w, chunk_rows, h1, g_down, g_out, n_outer, n_ctx, 7
        )
        g_qkv = cut_heads(tn(dproj, xn1).astype(BF), 0)
        terms = jnp.sum(qkv_w.reshape(-1, width).astype(F32) * g_qkv.astype(F32), 0) / gains[0]
        terms = jnp.stack([terms, dgain_two[0]]).reshape(2, n_outer, n_plane, gain_rows).transpose(2, 1, 0, 3)
        terms = jnp.pad(terms, ((0, 0), (0, 0), (0, 6), (0, LANES - gain_rows)))
        dproj, g_qkv = lax.optimization_barrier((dproj, g_qkv))
        g_qkv = z_rs(g_qkv)
        grad_input, g = attention_input(dproj, qkv_w, tokens, dh1, gains, terms, n_outer, n_ctx, 8)
        grad_input, g_qkv = lax.optimization_barrier((grad_input, g_qkv))
        grad_qkv = lax.ppermute(g_qkv, ALL, back).astype(F32)
        grad_out = cut_heads(g_out.transpose(1, 0, 2).reshape(out_rows, -1), 1).astype(F32)
        grad_down = g_down.reshape(n_plane, out_rows, n_outer // 2, unit_rows).transpose(1, 2, 0, 3)
        grad_down = grad_down.reshape(out_rows, -1).astype(F32)
        g = g[:, :gain_rows]
        return (result, grad_input, g[0], grad_qkv, grad_out, g[1], g_gate_up.astype(F32), grad_down)

    return shards


def solution(mesh):
    n_inner = 2
    n_ctx = mesh.shape["ctx"]
    n_outer = mesh.shape["dp"] // n_inner
    split = Mesh(mesh.devices.reshape(n_outer, n_inner, n_ctx), ALL)
    rows, vec, grp = P(ALL, None), P(ALL), P(("o", "i"), None)
    return jax.shard_map(
        make_shards(n_outer, n_inner, n_ctx),
        mesh=split,
        in_specs=(rows, vec, rows, rows, vec, rows, rows, rows, grp, grp),
        out_specs=(rows, rows, vec, rows, rows, vec, rows, rows),
        check_vma=False,
    )
```

time: 597 us -> 458 us (0.77)
  matrix products: 116 us -> 31.9 us
  Pallas kernels: 301 us -> 351 us
  other arithmetic: 55.4 us -> 7.24 us
  waiting for transfers between devices: 47.9 us -> 21.3 us
  local copies, waits for them, and re-layouts: 37.8 us -> 20 us
  blocking collectives: 11.2 us -> 0 us
    dot_general x14 -> x0, matrix products: 88.7 us -> none  [the longest x4 30 us: nn(): lax.dot_general(a, b, (((1,), (0,)), ((), ())), preferred_element_type=F32)]
    pallas_call x9 -> x10, Pallas kernels: 301 us -> 351 us  [the longest x9 332 us: remote_call(): pl.pallas_call(kernel, out_shape=outs, in_specs=[ANYWHERE if n in any_ins...]
    reduce_scatter x4 -> x3, waiting for transfers between devices: 37.5 us -> 6.37 us  [z_rs(): return lax.psum_scatter(x, 'o', scatter_dimension=0, tiled=True)]
    convert_element_type x8 -> x3, other arithmetic: 21.4 us -> 2.55 us  [the longest x1 1.33 us: shards(): g_gate_up.astype(F32)]
    unnamed x1 -> x0, blocking collectives: 11.2 us -> none
    reduce_sum x7 -> x1, other arithmetic: 11.4 us -> 0.41 us  [shards(): jnp.sum(qkv_w.reshape(-1, width).astype(F32) * g_qkv.astype(F32), 0)]
    slice x7 -> x4, local copies, waits for them, and re-layouts: 9.68 us -> 2.02 us  [the longest x1 1.1 us: cut_heads(): x = lax.slice_in_dim(x, 0, half, axis=axis + 1)]
  transfers between devices with their start and end apart: 8 -> 8, of which waited for: 3 -> 3; matrix products, arithmetic and copies ran while one was open for 19% -> 7% of each run, Pallas kernels for 33% -> 62%
where the time goes in v2:
time: 458 us; the launch traced here: 454 us
  Pallas kernels  351 us (77%)
  matrix products  31.9 us (7%)
  waiting for transfers between devices  21.3 us (5%)
  local copies, waits for them, and re-layouts  20 us (4%)
  between operations  14.7 us (3%)
  starting transfers between devices  7.52 us (2%)
  other arithmetic  7.24 us (2%)
    pallas_call x9, Pallas kernels, remote_call(): pl.pallas_call(kernel, out_shape=outs, in_specs=[ANYWHERE if n in any_ins...  332 us
    dot_general x4, matrix products, tn(): lax.dot_general(a, b, (((0,), (0,)), ((), ())), preferred_element_type=F32)  31.9 us
    pallas_call x1, Pallas kernels, feed_forward(): pl.pallas_call(kernel, grid=(rows // block,), out_shape=[shape((rows, num...  18.5 us
  transfers between devices with their start and end apart: 8, of which 3 were waited for; matrix products, arithmetic and copies ran while one was open for 7% of the time, Pallas kernels for 62%

profile of v2, /device:TPU:2, one launch (start us, length us, event | category | flops | bytes accessed | tf_op | source)
XLA Modules:
  0.0 453.6 jit_solution(5457160722751372731)
XLA Ops:
  7.2 3.5 collective-permute-start
  12.1 1.3 select_maximum_fusion.gains_ref
  13.4 10.5 %exchange.1 = (s32[8,8,128]{2,1,0:T(8,128)}, f32[4,8,8,128]{3,2,1,0:T(8,128)}) custom-call(s32[8,128]{1,0:T(8,128)} %pad.20.meta_ref, f32[8,128]{1,0:T(8,128)} %select_maximum_fusion.gains_ref), custom_call_target="tpu_custom_call" | custom-call | tf_op jit(solution)/shard_map/exchange/pallas_call | solution.py:345
  25.7 1.3 reshape.99
  30.9 40.7 %prologue.1 = (bf16[8,256,1536]{2,1,0:T(8,128)(2,1)}, bf16[8,48,256]{2,1,0:T(8,128)(2,1)}, bf16[8,48,512]{2,1,0:T(8,128)(2,1)}, f32[2048,128]{1,0:T(8,128)}, f32...) custom-call(bf16[256,1536]{1,0:T(8,128)(2,1)} %fusion.2.x_ref, bf16[8,48,256]{2,1,0:T(8,128)(2,1)} %bitcast.83, ...), custom_call_target="tpu_custom_call" | custom-call | tf_op jit(solution)/shard_map/prologue/pallas_call | solution.py:345
  76.8 39.9 %attention_forward.1 = (bf16[2048,512]{1,0:T(8,128)(2,1)}, bf16[2048,256]{1,0:T(8,128)(2,1)}, f32[8,2048]{1,0:T(8,128)}, bf16[8,256,1536]{2,1,0:T(8,128)(2,1)}) custom-call(bf16[2048,1536]{1,0:T(8,128)(2,1)} %bitcast.72, bf16[4,96,1536]{2,1,0:T(8,128)(2,1)} %bitcast.67, f32[2048,128]{1,0:T(8,128)} %get-tuple-element.52.cos_ref, ...), custom_call_target="tpu_custom_call" | custom-call | tf_op jit(solution)/shard_map/attention_forward/pallas_call | solution.py:345
  116.8 37.1 %output_projection.1 = (f32[256,1536]{1,0:T(8,128)}, bf16[256,1536]{1,0:T(8,128)(2,1)}) custom-call(bf16[2048,256]{1,0:T(8,128)(2,1)} %get-tuple-element.56.attn_ref, bf16[4,96,1536]{2,1,0:T(8,128)(2,1)} %bitcast.74, bf16[256,1536]{1,0:T(8,128)(2,1)} %x_ref.3, f32[2,1536]{1,0:T(2,128)} %reshape.107.gain_ref), custom_call_target="tpu_custom_call" | custom-call | tf_op jit(solution)/shard_map/output_projection/pallas_call | solution.py:345
  153.9 35.2 %gather_4.1 = bf16[8,256,1536]{2,1,0:T(8,128)(2,1)} custom-call(bf16[256,1536]{1,0:T(8,128)(2,1)} %get-tuple-element.58.src), custom_call_target="tpu_custom_call" | custom-call | tf_op jit(solution)/shard_map/gather_4/pallas_call | solution.py:345
  189.1 5.8 %all-gather.8.cloned.1.call-done = bf16[1536,1536]{1,0:T(8,128)(2,1)} async-done(((bf16[384,1536]{1,0:T(8,128)(2,1)}), bf16[1536,1536]{1,0:T(8,128)(2,1)}) %all-gather.8.cloned.1.call-update) | async-done | bytes 4718608 | tf_op jit(solution)/shard_map/all_gather | solution.py:45
  194.9 18.5 %feed_forward.1 = (bf16[2048,512]{1,0:T(8,128)(2,1)}, bf16[2048,1024]{1,0:T(8,128)(2,1)}) custom-call(bf16[2048,1536]{1,0:T(8,128)(2,1)} %bitcast.70, bf16[2048,1536]{1,0:T(8,128)(2,1)} %bitcast.93, bf16[4,384,1536]{2,1,0:T(8,128)(2,1)} %bitcast.64), custom_call_target="tpu_custom_call" | custom-call | flops 9663676416 | bytes 12582912 | tf_op jit(solution)/shard_map/feed_forward/pallas_call | solution.py:701
  213.4 8.0 %convolution_convert_fusion.2 = bf16[1536,512]{1,0:T(8,128)(2,1)} fusion(bf16[2048,1536]{1,0:T(8,128)(2,1)} %bitcast.94, bf16[2048,512]{1,0:T(8,128)(2,1)} %get-tuple-element.62.hidden_ref), kind=kOutput, calls=%fused_computation.2 | convolution fusion | flops 3222011904 | bytes 9961472 | tf_op jit(solution)/shard_map/dot_general | solution.py:41
  221.5 11.5 %convolution_convert_fusion = bf16[1024,1536]{1,0:T(8,128)(2,1)} fusion(bf16[2048,1024]{1,0:T(8,128)(2,1)} %get-tuple-element.64.dgu_ref, bf16[2048,1536]{1,0:T(8,128)(2,1)} %bitcast.71), kind=kOutput, calls=%fused_computation | convolution fusion | flops 6444023808 | bytes 13631488 | tf_op jit(solution)/shard_map/dot_general | solution.py:41
  233.1 41.6 %feed_forward_input.1 = (f32[256,1536]{1,0:T(8,128)}, bf16[256,1536]{1,0:T(8,128)(2,1)}, f32[8,1536]{1,0:T(8,128)}) custom-call(bf16[2048,1024]{1,0:T(8,128)(2,1)} %get-tuple-element.64.dgu_ref, bf16[4,384,1536]{2,1,0:T(8,128)(2,1)} %bitcast.65, f32[256,1536]{1,0:T(8,128)} %get-tuple-element.65.h_ref, bf16[256,1536]{1,0:T(8,128)(2,1)} %dy_ref.3, ...), custom_call_target="tpu_custom_call" | custom-call | tf_op jit(solution)/shard_map/feed_forward_input/pallas_call | solution.py:345
  274.7 35.8 %gather_6.1 = bf16[8,256,1536]{2,1,0:T(8,128)(2,1)} custom-call(bf16[256,1536]{1,0:T(8,128)(2,1)} %get-tuple-element.66.src), custom_call_target="tpu_custom_call" | custom-call | tf_op jit(solution)/shard_map/gather_6/pallas_call | solution.py:345
  310.6 6.3 %reduce-scatter.4.cloned.1.call-done = bf16[256,1536]{1,0:T(8,128)(2,1)} async-done(((bf16[1024,1536]{1,0:T(8,128)(2,1)}), bf16[256,1536]{1,0:T(8,128)(2,1)}) %reduce-scatter.4.cloned.1.call-update) | async-done | bytes 786448 | tf_op jit(solution)/shard_map/reduce_scatter | solution.py:49
  316.9 5.5 %convolution_convert_fusion.3 = bf16[1536,256]{1,0:T(8,128)(2,1)} fusion(bf16[2048,1536]{1,0:T(8,128)(2,1)} %bitcast.62, bf16[2048,256]{1,0:T(8,128)(2,1)S(1)} %copy-done.3), kind=kOutput, calls=%fused_computation.3 | convolution fusion | flops 1611005952 | bytes 8126464 | tf_op jit(solution)/shard_map/dot_general | solution.py:41
  322.4 53.3 %attention_backward.1 = (bf16[2048,512]{1,0:T(8,128)(2,1)}, bf16[256,1536]{1,0:T(8,128)(2,1)}, bf16[8,48,512]{2,1,0:T(8,128)(2,1)}, bf16[8,48,256]{2,1,0:T(8,128)(2,1)}) custom-call(bf16[2048,1536]{1,0:T(8,128)(2,1)} %bitcast.63, bf16[4,96,1536]{2,1,0:T(8,128)(2,1)} %bitcast.75, bf16[2048,512]{1,0:T(8,128)(2,1)} %get-tuple-element.70.qkv_ref, ...), custom_call_target="tpu_custom_call" | custom-call | tf_op jit(solution)/shard_map/attention_backward/pallas_call | solution.py:345
  375.8 6.9 %convolution_convert_fusion.1 = bf16[512,1536]{1,0:T(8,128)(2,1)S(1)} fusion(bf16[2048,512]{1,0:T(8,128)(2,1)} %get-tuple-element.75.d_ref, bf16[2048,1536]{1,0:T(8,128)(2,1)} %bitcast.73), kind=kOutput, calls=%fused_computation.1 | convolution fusion | flops 3222011904 | bytes 9961472 | tf_op jit(solution)/shard_map/dot_general | solution.py:41
  386.6 38.3 %attention_input.1 = (f32[256,1536]{1,0:T(8,128)}, f32[8,128]{1,0:T(8,128)}) custom-call(bf16[2048,512]{1,0:T(8,128)(2,1)} %get-tuple-element.75.d_ref, bf16[4,96,1536]{2,1,0:T(8,128)(2,1)} %bitcast.68, bf16[256,1536]{1,0:T(8,128)(2,1)} %x_ref.3, f32[256,1536]{1,0:T(8,128)} %get-tuple-element.76.dh_ref, f32[2,1536]{1,0:T(2,128)} %reshape.107.gain_ref, ...), custom_call_target="tpu_custom_call" | custom-call | tf_op jit(solution)/shard_map/attention_input/pallas_call | solution.py:345
  425.0 3.6 collective-permute-start.1
  430.8 1.3 copy.39
  432.1 1.3 convert_element_type.67
  433.4 1.3 slice_bitcast_fusion.1
  434.7 8.9 %collective-permute-done.1 = bf16[96,1536]{1,0:T(8,128)(2,1)S(1)} collective-permute-done((bf16[96,1536]{1,0:T(8,128)(2,1)}, bf16[96,1536]{1,0:T(8,128)(2,1)S(1)}, u32[]{:S(2)}, u32[]{:S(2)}) %collective-permute-start.1) | collective-permute-done | bytes 294944 | tf_op jit(solution)/shard_map/ppermute | solution.py:1047
  (81 shorter events, 21.3 us)
Async XLA Ops:
  7.2 21.0 %copy-start.8 = (bf16[48,4096]{1,0:T(8,128)(2,1)S(1)}, bf16[48,4096]{1,0:T(8,128)(2,1)}, u32[]{:S(2)}) copy-start(bf16[48,4096]{1,0:T(8,128)(2,1)} %param.18) | copy-start | bytes 1179652
  7.2 69.6 %all-gather.4.cloned.1.call-start = ((), (), s32[]{:S(2)}) async-start(), calls=%async_computation.3 | async-start | bytes 1474560 | tf_op jit(solution)/shard_map/all_gather | solution.py:45
  7.2 16.7 %collective-permute-start = (bf16[96,1536]{1,0:T(8,128)(2,1)}, bf16[96,1536]{1,0:T(8,128)(2,1)S(1)}, u32[]{:S(2)}, u32[]{:S(2)}) collective-permute-start(bf16[96,1536]{1,0:T(8,128)(2,1)} %param.14), channel_id=1, source_target_pairs={{0,0},{1,8},{2,1},{3,9},{4,2},{5,10},{6,3},{7,11},{8,4},{9,12},{10... | collective-permute-start | bytes 884744 | tf_op jit(solution)/shard_map/ppermute | solution.py:997
  23.9 0.7 copy-start.10
  24.7 92.1 %all-gather.6.cloned.1.call-start = ((), (), s32[]{:S(2)}) async-start(), calls=%async_computation.4 | async-start | bytes 1474560 | tf_op jit(solution)/shard_map/all_gather | solution.py:45
  27.0 2.5 copy-start
  30.9 43.8 %copy-start.6 = (bf16[256,1536]{1,0:T(8,128)(2,1)S(1)}, bf16[256,1536]{1,0:T(8,128)(2,1)}, u32[]{:S(2)}) copy-start(bf16[256,1536]{1,0:T(8,128)(2,1)} %param.17) | copy-start | bytes 2359300
  73.3 121.6 %all-gather.8.cloned.1.call-start = ((), (), s32[]{:S(2)}) async-start(), calls=%async_computation.5 | async-start | bytes 5898240 | tf_op jit(solution)/shard_map/all_gather | solution.py:45
  75.9 234.7 %reduce-scatter.6.cloned.1.call-start = ((), (), s32[]{:S(2)}) async-start(), calls=%async_computation.7 | async-start | bytes 1966080 | tf_op jit(solution)/shard_map/reduce_scatter | solution.py:49
  221.5 95.5 %reduce-scatter.4.cloned.1.call-start = ((), (), s32[]{:S(2)}) async-start(), calls=%async_computation.6 | async-start | bytes 3932160 | tf_op jit(solution)/shard_map/reduce_scatter | solution.py:49
  233.1 191.9 %reduce-scatter.8.cloned.1.call-start = ((), (), s32[]{:S(2)}) async-start(), calls=%async_computation.8 | async-start | bytes 1474560 | tf_op jit(solution)/shard_map/reduce_scatter | solution.py:49
  274.7 42.2 %copy-start.3 = (bf16[2048,256]{1,0:T(8,128)(2,1)S(1)}, bf16[2048,256]{1,0:T(8,128)(2,1)}, u32[]{:S(2)}) copy-start(bf16[2048,256]{1,0:T(8,128)(2,1)} %get-tuple-element.56.attn_ref) | copy-start | bytes 3145732
  382.7 2.2 copy-start.11
  382.7 2.2 copy-start.1
  383.8 1.4 copy-start.2
  424.9 4.9 %copy-start.9 = (bf16[8,48,512]{2,1,0:T(8,128)(2,1)S(1)}, bf16[8,48,512]{2,1,0:T(8,128)(2,1)}, u32[]{:S(2)}) copy-start(bf16[8,48,512]{2,1,0:T(8,128)(2,1)} %get-tuple-element.85) | copy-start | bytes 1179652
  425.0 18.7 %collective-permute-start.1 = (bf16[96,1536]{1,0:T(8,128)(2,1)}, bf16[96,1536]{1,0:T(8,128)(2,1)S(1)}, u32[]{:S(2)}, u32[]{:S(2)}) collective-permute-start(bf16[96,1536]{1,0:T(8,128)(2,1)} %reduce-scatter.8.cloned.1.call-done), channel_id=1, source_target_pairs={{0,0},{8,1},{1,2},{9,3},{2,4},{10,5},{3,6},{11,7},{4,8},{12,9},{5,... | collective-permute-start | bytes 884744 | tf_op jit(solution)/shard_map/ppermute | solution.py:1047
  429.8 2.3 copy-start.7
  430.8 13.8 %copy-start.5 = (bf16[256,1536]{1,0:T(8,128)(2,1)S(1)}, bf16[256,1536]{1,0:T(8,128)(2,1)}, u32[]{:S(2)}) copy-start(bf16[256,1536]{1,0:T(8,128)(2,1)} %get-tuple-element.96) | copy-start | bytes 2359300
  432.1 13.3 %copy-start.4 = (f32[256,1536]{1,0:T(8,128)S(1)}, f32[256,1536]{1,0:T(8,128)}, u32[]{:S(2)}) copy-start(f32[256,1536]{1,0:T(8,128)} %get-tuple-element.97) | copy-start | bytes 4718596
Sparse Core Ops, SparseCore 0:
  24.8 30.4 all-gather.3
  73.4 30.6 all-gather.5
  106.2 88.6 all-gather.7
  221.6 33.8 reduce-scatter.5
  257.7 59.2 reduce-scatter.3
  383.9 27.8 reduce-scatter.7

commit v3 on v2

--- a/solution.py
+++ b/solution.py
@@ -1,4 +1,3 @@
-import functools
 import math
 
 import jax
@@ -10,8 +9,8 @@
 from jax.sharding import Mesh
 from jax.sharding import PartitionSpec as P
 
+
 QUERY_HEADS = 16
-KEY_VALUE_HEADS = 8
 HEAD_SIZE = 96
 FF = 4096
 BLK = 128
@@ -63,13 +62,14 @@
     half, quarter = n_outer // 2, n_outer // 4
     for block in range(n_outer * n_plane):
         if block < 4 * n_outer:
-            place, step = block // half, block % half
+            head, step = block // half, block % half
         elif block < 6 * n_outer:
-            place, step = divmod(block - 4 * n_outer, quarter)
+            head, step = divmod(block - 4 * n_outer, quarter)
             step += half
         else:
-            place, step = divmod(block - 6 * n_outer, quarter)
+            head, step = divmod(block - 6 * n_outer, quarter)
             step += half + quarter
+        place = 2 * (head % (n_plane // 2)) + head // (n_plane // 2)
         moves.append((block, step * n_plane + place))
     return moves
 
@@ -89,22 +89,6 @@
     x = x.reshape(shape[:axis] + (-1, LANES // 2) + shape[axis + 1 :])
     x = lax.slice_in_dim(x, 0, half, axis=axis + 1)
     return x.reshape(shape[:axis] + (-1,) + shape[axis + 1 :])
-
-
-def pack_down(w, chunks):
-    width, units = w.shape
-    span = width // units
-    w = w.reshape(chunks, span, width // (chunks * span), units)
-    return w.transpose(0, 2, 1, 3).reshape(chunks, -1, width)
-
-
-def in_chunks(weights, unit_rows, units):
-    n_outer, _, width = weights.shape
-    if n_outer == CHUNKS:
-        return weights
-    gate_up = weights[:, :unit_rows].reshape(CHUNKS, -1, width)
-    down = weights[:, unit_rows:].reshape(n_outer, -1, width // units, units).transpose(0, 2, 1, 3)
-    return jnp.concatenate([gate_up, pack_down(down.reshape(width, units), CHUNKS)], 1)
 
 
 def places(n_ctx):
@@ -264,15 +248,15 @@
     def join(self):
         for part in range(PARTS):
             self.diagonals[part].wait_recv()
+            if part == 0:
+                self.straights.append(self.go(5, PARTS - 1, self.going.at[1], self.got.at[1], self.direct))
 
             def combined(t, lanes, _):
                 pair = self.partial(self.s_combined, t) + self.from_mate[1 + self.core, part, :, lanes].astype(F32)
                 self.going[2, part, :, lanes] = (pair + self.got[0, part, :, lanes].astype(F32)).astype(BF)
 
             self.each(part, combined)
-            if part == 0:
-                self.straights.append(self.go(5, PARTS - 1, self.going.at[1], self.got.at[1], self.direct))
-            else:
+            if part:
                 self.joins.append(self.go(6, part - 1, self.going.at[2], self.got.at[2], self.combined))
         self.own(0)
         self.joins.append(self.go(6, PARTS - 1, self.going.at[2], self.got.at[2], self.combined))
@@ -341,7 +325,7 @@
 ANYWHERE = pl.BlockSpec(memory_space=pl.ANY)
 
 
-def remote_call(kernel, name, number, ins, outs, scratch, any_outs=(), any_ins=()):
+def remote_call(kernel, number, ins, outs, scratch, any_outs=(), any_ins=()):
     return pl.pallas_call(
         kernel,
         out_shape=outs,
@@ -349,7 +333,6 @@
         out_specs=[ANYWHERE if n in any_outs else IN_VMEM for n in range(len(outs))],
         scratch_shapes=scratch,
         compiler_params=pltpu.CompilerParams(collective_id=number, has_side_effects=True, vmem_limit_bytes=60 << 20),
-        name=name,
     )(*ins)
 
 
@@ -408,46 +391,8 @@
     return rates, np.stack([np.cos(angles), np.sin(angles)]).astype(np.float32)
 
 
-def exchange(meta, gains, n_outer, n_ctx, number):
-    n = 2 * n_ctx
-
-    def kernel(meta_ref, gains_ref, metas_out, gains_out, send_sem, recv_sem, local_sem):
-        o, i, c, _, _ = places(n_ctx)
-        me = i * n_ctx + c
-        plane = [lax.rem(me + k, n) for k in range(1, n)]
-        plane = [(o, d // n_ctx, d % n_ctx) for d in plane]
-        peers = outer_peers(n_outer)
-        greet(plane + peers)
-        first, second, later = [], [], []
-        for k, device in enumerate(plane):
-            first.append(send(gains_ref, gains_out.at[o, me], send_sem.at[0, k], recv_sem.at[0, k], device))
-        own = [
-            pltpu.make_async_copy(gains_ref, gains_out.at[o, me], local_sem.at[0]),
-            pltpu.make_async_copy(meta_ref, metas_out.at[me], local_sem.at[1]),
-        ]
-        for copy in own:
-            copy.start()
-        for k, device in enumerate(plane):
-            later.append(send(meta_ref, metas_out.at[me], send_sem.at[1, k], recv_sem.at[1, k], device))
-        for copy in own:
-            copy.wait()
-        for copy in first:
-            copy.wait_recv()
-        for k, device in enumerate(peers):
-            second.append(send(gains_out.at[o], gains_out.at[o], send_sem.at[2, k], recv_sem.at[2, k], device))
-        for copy in second + later:
-            copy.wait_recv()
-        for copy in first + second + later:
-            copy.wait_send()
-
-    outs = [shape((n,) + meta.shape, meta.dtype), shape((n_outer, n) + gains.shape, F32)]
-    most = max(n, n_outer) - 1
-    sems = [pltpu.SemaphoreType.DMA((3, most)), pltpu.SemaphoreType.DMA((3, most)), pltpu.SemaphoreType.DMA((2,))]
-    return remote_call(kernel, "exchange", number, [meta, gains], outs, sems)
-
-
-def prologue(xn, outs_parts, down_parts, metas, n_seqs, n_ctx, number):
-    rows, width = xn.shape
+def prologue(tokens, out_parts, down_parts, gains, meta, n_seqs, n_outer, n_ctx, number):
+    rows, width = tokens.shape
     n = 2 * n_ctx
     blocks = n_ctx * rows // BLK
 
@@ -455,22 +400,44 @@
         x_ref,
         out_src,
         down_src,
-        metas_ref,
+        gains_ref,
+        meta_ref,
         rates_ref,
         angles_ref,
-        xn_all,
+        x_all,
         out_dst,
         down_dst,
+        gains_out,
         cos_ref,
         sin_ref,
         rows_ref,
         columns_ref,
         *sems,
     ):
-        out_swap = Swap(n_ctx, [(out_src, out_dst), (down_src, down_dst)], *sems[:3])
-        gather = Gather(n_ctx, x_ref, xn_all, *sems[3:6])
-        greet(out_swap.devices)
+        o = lax.axis_index("o")
+        metas_ref, send_sem, recv_sem, local_sem = sems[:4]
+        out_swap = Swap(n_ctx, [(out_src, out_dst)], *sems[4:7])
+        down_swap = Swap(n_ctx, [(down_src, down_dst)], *sems[7:10])
+        gather = Gather(n_ctx, x_ref, x_all, *sems[10:])
+        peers = outer_peers(n_outer)
+        me = out_swap.me
+        greet(out_swap.devices + peers)
         gather.begin()
+        own = [
+            pltpu.make_async_copy(meta_ref, metas_ref.at[me], local_sem.at[0]),
+            pltpu.make_async_copy(gains_ref, gains_out.at[o, me], local_sem.at[1]),
+        ]
+        meta_copies, gain_copies, z_copies = [], [], []
+        for copy in own:
+            copy.start()
+        for k, device in enumerate(out_swap.devices):
+            meta_copies.append(send(meta_ref, metas_ref.at[me], send_sem.at[0, k], recv_sem.at[0, k], device))
+            gain_copies.append(send(gains_ref, gains_out.at[o, me], send_sem.at[1, k], recv_sem.at[1, k], device))
+        out_swap.begin()
+        for copy in own:
+            copy.wait()
+        for copy in meta_copies:
+            copy.wait_recv()
         lane = lax.broadcasted_iota(jnp.int32, (BLK, LANES), 1)
         row = lax.broadcasted_iota(jnp.int32, (BLK, LANES), 0)
         rows_ref[...] = jnp.zeros_like(rows_ref)
@@ -510,23 +477,41 @@
             columns_ref[at] = jnp.where(lane == 0, stream, start)
             rows_ref[0:1, at] = lanes_stream
             rows_ref[1:2, at] = lanes_start
+        for copy in gain_copies:
+            copy.wait_recv()
+        for k, device in enumerate(peers):
+            z_copies.append(send(gains_out.at[o], gains_out.at[o], send_sem.at[2, k], recv_sem.at[2, k], device))
         gather.middle()
-        out_swap.begin()
+        down_swap.begin()
         gather.end()
         out_swap.end()
+        down_swap.end()
+        for copy in z_copies:
+            copy.wait_recv()
+        for copy in meta_copies + gain_copies + z_copies:
+            copy.wait_send()
 
     outs = [
         shape((n, rows, width), BF),
-        shape(outs_parts.shape, BF),
+        shape(out_parts.shape, BF),
         shape(down_parts.shape, BF),
+        shape((n_outer, n) + gains.shape, F32),
         shape((n * rows, LANES), F32),
         shape((n * rows, LANES), F32),
         shape((8, n * rows), jnp.int32),
         shape((n * rows, LANES), jnp.int32),
     ]
     rates, angles = rotary_constants()
-    ins = [xn, outs_parts, down_parts, metas, jnp.asarray(rates), jnp.asarray(angles)]
-    return remote_call(kernel, "prologue", number, ins, outs, swap_sems(2, n_ctx) + GATHER_SEMS, any_outs=(0,))
+    ins = [tokens, out_parts, down_parts, gains, meta, jnp.asarray(rates), jnp.asarray(angles)]
+    most = max(n, n_outer) - 1
+    scratch = [
+        pltpu.VMEM((n,) + meta.shape, jnp.int32),
+        pltpu.SemaphoreType.DMA((3, most)),
+        pltpu.SemaphoreType.DMA((3, most)),
+        pltpu.SemaphoreType.DMA((2,)),
+    ]
+    scratch += swap_sems(1, n_ctx) + swap_sems(1, n_ctx) + GATHER_SEMS
+    return remote_call(kernel, number, ins, outs, scratch, any_outs=(0,))
 
 
 def plane_gather(x, n_ctx, number):
@@ -538,7 +523,7 @@
         gather.end()
 
     outs = [shape((2 * n_ctx,) + x.shape, x.dtype)]
-    got = remote_call(kernel, f"gather_{number}", number, [x], outs, GATHER_SEMS, any_outs=(0,))
+    got = remote_call(kernel, number, [x], outs, GATHER_SEMS, any_outs=(0,))
     return got[0].reshape(-1, x.shape[-1])
 
 
@@ -546,9 +531,13 @@
     return x * cosine + pltpu.roll(x, LANES // 2, 1) * sine
 
 
+def qkv_rows(features):
+    return features // LANES * HEAD_SIZE // CHUNKS
+
+
 def padded_loads(w_ref, w_pad):
     half = HEAD_SIZE // 2
-    rows = w_ref.shape[1]
+    rows = qkv_rows(w_pad.shape[0])
     pairs, at = [], 0
     for row in range(half, w_pad.shape[0], LANES // 2):
         w_pad[row : row + LANES // 2 - half] = jnp.zeros((LANES // 2 - half, w_pad.shape[1]), BF)
@@ -560,23 +549,57 @@
     return pairs
 
 
-def attention_forward(xn, w, cosine, sine, pos_rows, pos_columns, dy, n_ctx, number):
-    rows, width = xn.shape
+def attention_forward(x_all, gains, w, cosine, sine, pos_rows, pos_columns, dy, out_part, n_outer, n_ctx, number):
+    rows, width = x_all.shape
     group = rows // 2
     heads = QUERY_HEADS // (2 * n_ctx)
     features = (heads + 2) * LANES
     k_at, v_at = heads * LANES, (heads + 1) * LANES
     block = min(QUERY_BLOCK, group)
-    n_loads = w.shape[0] * w.shape[1] // (HEAD_SIZE // 2)
+    n_loads = features // (LANES // 2)
 
     def kernel(
-        xn_ref, w_hbm, cos_ref, sin_ref, rows_ref, columns_ref, dy_ref, qkv_ref, attn_ref, lse_ref, dy_all, w_ref, load_sem, *sems
+        x_hbm,
+        gain_ref,
+        w_hbm,
+        cos_ref,
+        sin_ref,
+        rows_ref,
+        columns_ref,
+        dy_ref,
+        part_ref,
+        qkv_ref,
+        attn_ref,
+        lse_ref,
+        dy_all,
+        xn_out,
+        out_w,
+        w_ref,
+        xn_ref,
+        load_sem,
+        xn_sem,
+        store_sem,
+        z_send,
+        z_recv,
+        z_local,
+        *sems,
     ):
         gather = Gather(n_ctx, dy_ref, dy_all, *sems)
         load = Load(padded_loads(w_hbm, w_ref), load_sem).begin()
-        greet_neighbours(n_ctx)
+        xn_load = Load([(x_hbm, xn_ref)], xn_sem).begin()
+        o = lax.axis_index("o")
+        peers = outer_peers(n_outer)
+        greet([gather.mate, gather.x, gather.y] + peers)
         gather.begin()
+        z_copies = [send(part_ref, out_w.at[o], z_send.at[k], z_recv.at[k], device) for k, device in enumerate(peers)]
+        own_part = pltpu.make_async_copy(part_ref, out_w.at[o], z_local)
+        own_part.start()
         load.wait()
+        xn_load.wait()
+
+        def normalise(r):
+            x = xn_ref[r].astype(F32)
+            xn_ref[r] = (x * inv_rms(x) * gain_ref[0:1]).astype(BF)
 
         def project(r):
             cos, sin = cos_ref[r], sin_ref[r]
@@ -605,141 +628,250 @@
                     lse = jnp.broadcast_to(high * SCALE + jnp.log(total), (block, LANES))
                     lse_ref[h : h + 1, r] = jnp.transpose(lse)[0:1]
 
+        row_chunks(rows, 64, normalise)
         row_chunks(rows, block, project)
+        gather.middle()
+        store = Load([(xn_ref, xn_out)], store_sem).begin()
         attend(0)
-        gather.middle()
         attend(1)
         gather.end()
+        store.wait()
+        own_part.wait()
+        for copy in z_copies:
+            copy.wait_recv()
+            copy.wait_send()
 
     outs = [
         shape((rows, features), BF),
         shape((rows, heads * LANES), BF),
         shape((8, rows), F32),
         shape((2 * n_ctx,) + dy.shape, BF),
+        shape(x_all.shape, BF),
+        shape((n_outer,) + out_part.shape, BF),
     ]
-    ins = [xn, w, cosine, sine, pos_rows, pos_columns, dy]
-    scratch = [pltpu.VMEM((features, width), BF), pltpu.SemaphoreType.DMA((n_loads,))] + GATHER_SEMS
-    got = remote_call(kernel, "attention_forward", number, ins, outs, scratch, any_outs=(3,), any_ins=(1,))
-    return got[0], got[1], got[2], got[3].reshape(rows, width)
-
-
-def out_loads(w_ref, w_pad):
-    features = w_pad.shape[1]
-    chunks, _, width = w_ref.shape
-    rows = features // chunks
-    span = width // features
-    pairs = []
-    for n in range(chunks):
-        for b in range(span):
-            dst = w_pad.at[pl.ds((n * span + b) * rows, rows)]
-            pairs.append((w_ref.at[n, pl.ds(0, rows), pl.ds(b * features, features)], dst))
-    return pairs
+    ins = [x_all, gains, w, cosine, sine, pos_rows, pos_columns, dy, out_part]
+    scratch = [
+        pltpu.VMEM((features, width), BF),
+        pltpu.VMEM(x_all.shape, BF),
+        pltpu.SemaphoreType.DMA((n_loads,)),
+        pltpu.SemaphoreType.DMA((1,)),
+        pltpu.SemaphoreType.DMA((1,)),
+        pltpu.SemaphoreType.DMA((n_outer - 1,)),
+        pltpu.SemaphoreType.DMA((n_outer - 1,)),
+        pltpu.SemaphoreType.DMA,
+    ]
+    scratch += GATHER_SEMS
+    got = remote_call(kernel, number, ins, outs, scratch, any_outs=(3, 4), any_ins=(0, 2))
+    return got[0], got[1], got[2], got[3].reshape(rows, width), got[4], got[5]
 
 
 def output_projection(attn, out_w, tokens, gain, n_ctx, number):
     rows, width = tokens.shape
     tile = 256
 
-    features = attn.shape[1]
-
-    def kernel(attn_ref, w_hbm, x_ref, gain_ref, h_ref, xn_ref, w_ref, load_sem, *scratch):
+
+    def kernel(attn_ref, w_ref, x_ref, gain_ref, h_ref, xn_ref, *scratch):
         total = scratch[-1]
-        load = Load(out_loads(w_hbm, w_ref), load_sem).begin()
 
         def partial(slot, t):
             a = attn_ref[pl.ds(pl.multiple_of(slot * rows, rows), rows)]
             return nt(a, w_ref[pl.ds(pl.multiple_of(t * tile, tile), tile)])
-
-        scatter = Scatter(n_ctx, partial, tile, *scratch)
-        greet_neighbours(n_ctx)
-        load.wait()
-        scatter.to_mate()
-        scatter.pairs()
-        scatter.join()
-        scatter.end()
-
-        def finish(r):
-            h = x_ref[r].astype(F32) + total[r]
-            h_ref[r] = h
-            xn_ref[r] = (h * inv_rms(h) * gain_ref[1:2]).astype(BF)
-
-        row_chunks(rows, 32, finish)
-
-    outs = [shape((rows, width), F32), shape((rows, width), BF)]
-    n_loads = out_w.shape[0] * width // features
-    scratch = [pltpu.VMEM((width, features), BF), pltpu.SemaphoreType.DMA((n_loads,))] + scatter_scratch(rows, width)
-    return remote_call(kernel, "output_projection", number, [attn, out_w, tokens, gain], outs, scratch, any_ins=(1,))
-
-
-def feed_forward(xn, dy, weights, unit_rows, number_of_units):
-    rows, width = xn.shape
-    n_outer = weights.shape[0]
-    block = 256
-    pack = weights.shape[1] - unit_rows
-    span = width // number_of_units
-
-    def kernel(x_ref, dy_ref, w_ref, hidden_ref, dgu_ref):
-        x, dy = x_ref[...], dy_ref[...]
-        half = n_outer // 2
-        for n in range(half):
-            lanes = slice(n * unit_rows, (n + 1) * unit_rows)
-            gate = nt(x, w_ref[n, :unit_rows])
-            up = nt(x, w_ref[half + n, :unit_rows])
-            dhid = jnp.zeros_like(gate)
-            for m in range(n_outer):
-                for b in range(span):
-                    at = (m * span + b) * pack
-                    u = b * number_of_units + n * unit_rows
-                    dhid = dhid + nn(dy[:, at : at + pack], w_ref[m, unit_rows:, u : u + unit_rows])
-            sg = 1.0 / (1.0 + jnp.exp(-gate))
-            act = gate * sg
-            hidden_ref[:, lanes] = (act * up).astype(BF)
-            dgu_ref[:, lanes] = (dhid * up * sg * (1.0 + gate * (1.0 - sg))).astype(BF)
-            second = slice(number_of_units + n * unit_rows, number_of_units + (n + 1) * unit_rows)
-            dgu_ref[:, second] = (dhid * act).astype(BF)
-
-    return pl.pallas_call(
-        kernel,
-        grid=(rows // block,),
-        out_shape=[shape((rows, number_of_units), BF), shape((rows, 2 * number_of_units), BF)],
-        in_specs=[
-            pl.BlockSpec((block, width), lambda b: (b, 0)),
-            pl.BlockSpec((block, width), lambda b: (b, 0)),
-            IN_VMEM,
-        ],
-        out_specs=[
-            pl.BlockSpec((block, number_of_units), lambda b: (b, 0)),
-            pl.BlockSpec((block, 2 * number_of_units), lambda b: (b, 0)),
-        ],
-        compiler_params=pltpu.CompilerParams(vmem_limit_bytes=60 << 20),
-        cost_estimate=pl.CostEstimate(
-            flops=6 * rows * width * number_of_units, bytes_accessed=4 * rows * width, transcendentals=rows * number_of_units
-        ),
-        name="feed_forward",
-    )(xn, dy, weights)
-
-
-def feed_forward_input(dgu, weights, unit_rows, h1, cotangent, gain, n_ctx, number):
-    rows, width = h1.shape
-    n_outer = weights.shape[0]
-    tile = 256
-
-    def kernel(dgu_ref, w_ref, h_ref, dy_ref, gain_ref, dh_ref, dhb_ref, dgain_ref, *scratch):
-        total = scratch[-1]
-
-        def partial(slot, t):
-            r = pl.ds(pl.multiple_of(slot * rows, rows), rows)
-            lanes = pl.ds(pl.multiple_of(t * tile, tile), tile)
-            acc = nn(dgu_ref[r, :unit_rows], w_ref[0, :unit_rows, lanes])
-            for n in range(1, n_outer):
-                acc = acc + nn(dgu_ref[r, n * unit_rows : (n + 1) * unit_rows], w_ref[n, :unit_rows, lanes])
-            return acc
 
         scatter = Scatter(n_ctx, partial, tile, *scratch)
         greet_neighbours(n_ctx)
         scatter.to_mate()
         scatter.pairs()
         scatter.join()
+        scatter.end()
+
+        def finish(r):
+            h = x_ref[r].astype(F32) + total[r]
+            h_ref[r] = h
+            xn_ref[r] = (h * inv_rms(h) * gain_ref[1:2]).astype(BF)
+
+        row_chunks(rows, 32, finish)
+
+    outs = [shape((rows, width), F32), shape((rows, width), BF)]
+    return remote_call(kernel, number, [attn, out_w, tokens, gain], outs, scatter_scratch(rows, width))
+
+
+def feed_forward(xn, dy, gate_up, down, n_ctx, number):
+    rows, width = xn.shape
+    n = 2 * n_ctx
+    chunks, unit_rows, _ = gate_up.shape
+    units = down.shape[1]
+    tile = 256
+
+    def kernel(
+        x_ref,
+        dy_hbm,
+        up_hbm,
+        down_hbm,
+        xn_all,
+        hidden_ref,
+        dgu_ref,
+        dgu_t,
+        g_down_ref,
+        raw,
+        dy_ref,
+        up_ref,
+        down_ref,
+        hidden_t,
+        g_acc,
+        load_sem,
+        store_sem,
+        *sems,
+    ):
+        gather = Gather(n_ctx, x_ref, raw, *sems)
+        pairs = [(up_hbm, up_ref), (down_hbm, down_ref), (dy_hbm, dy_ref)]
+        load = Load(pairs, load_sem).begin()
+        greet_neighbours(n_ctx)
+        gather.begin()
+        half = chunks // 2
+        core = gather.me % 2
+
+        def chip(slot):
+            both = pl.ds(pl.multiple_of((slot - core) * rows, 2 * rows), 2 * rows)
+            x = raw[pl.ds(slot - core, 2)].reshape(2 * rows, width)
+            for m in range(half):
+                lanes = slice(m * unit_rows, (m + 1) * unit_rows)
+                second = slice(units + m * unit_rows, units + (m + 1) * unit_rows)
+                gate = nt(x, up_ref[m])
+                up = nt(x, up_ref[half + m])
+                dhid = nn(dy_ref[both], down_ref[:, lanes])
+                sg = 1.0 / (1.0 + jnp.exp(-gate))
+                act = gate * sg
+                hidden = act * up
+                dgate = dhid * up * sg * (1.0 + gate * (1.0 - sg))
+                dup = dhid * act
+                hidden_ref[both, lanes] = hidden.astype(BF)
+                dgu_ref[both, lanes] = dgate.astype(BF)
+                dgu_ref[both, second] = dup.astype(BF)
+                hidden_t[lanes] = jnp.transpose(hidden).astype(BF)
+                dgu_t[lanes, both] = jnp.transpose(dgate).astype(BF)
+                dgu_t[second, both] = jnp.transpose(dup).astype(BF)
+
+            @pl.loop(0, width // tile)
+            def _(t):
+                lanes = pl.ds(pl.multiple_of(t * tile, tile), tile)
+                g = nn(hidden_t[...], dy_ref[both, lanes])
+                g_acc[:, lanes] = g if slot is gather.me else g_acc[:, lanes] + g
+
+        stores = []
+
+        def store(slot):
+            copy = pltpu.make_async_copy(raw.at[slot], xn_all.at[slot], store_sem.at[len(stores)])
+            copy.start()
+            stores.append(copy)
+
+        load.wait()
+        gather.arrived(0)
+        gather.own.wait()
+        store(gather.me)
+        store(gather.mates_slots[0])
+        chip(gather.me)
+        gather.middle()
+        gather.arrived(3)
+        store(gather.s_x)
+        store(gather.mates_slots[1])
+        chip(gather.s_x)
+        gather.arrived(4)
+        store(gather.s_y)
+        store(gather.mates_slots[2])
+        chip(gather.s_y)
+        gather.corner()
+        gather.arrived(6)
+        store(gather.s_d)
+        store(gather.mates_slots[3])
+        chip(gather.s_d)
+
+        @pl.loop(0, width // tile)
+        def _(t):
+            lanes = pl.ds(pl.multiple_of(t * tile, tile), tile)
+            g_down_ref[lanes] = jnp.transpose(g_acc[:, lanes]).astype(BF)
+
+        for copy in gather.copies.values():
+            copy.wait_send()
+        for copy in stores:
+            copy.wait()
+
+    outs = [
+        shape((n, rows, width), BF),
+        shape((n * rows, units), BF),
+        shape((n * rows, 2 * units), BF),
+        shape((2 * units, n * rows), BF),
+        shape((width, units), BF),
+    ]
+    scratch = [
+        pltpu.VMEM((n, rows, width), BF),
+        pltpu.VMEM(dy.shape, BF),
+        pltpu.VMEM(gate_up.shape, BF),
+        pltpu.VMEM(down.shape, BF),
+        pltpu.VMEM((units, 2 * rows), BF),
+        pltpu.VMEM((units, width), F32),
+        pltpu.SemaphoreType.DMA((3,)),
+        pltpu.SemaphoreType.DMA((n,)),
+    ]
+    ins = [xn, dy, gate_up, down]
+    return remote_call(kernel, number, ins, outs, scratch + GATHER_SEMS, any_outs=(0,), any_ins=(1, 2, 3))
+
+
+def feed_forward_input(dgu, gate_up, h1, cotangent, gain, xn_all, dgu_t, n_ctx, number):
+    rows, width = h1.shape
+    chunks, unit_rows, _ = gate_up.shape
+    units = chunks * unit_rows // 2
+    tile, part = 256, 256
+
+    def kernel(
+        dgu_ref,
+        w_hbm,
+        h_ref,
+        dy_ref,
+        gain_ref,
+        xn_hbm,
+        dgu_t_hbm,
+        dh_ref,
+        dhb_ref,
+        dgain_ref,
+        g_up_ref,
+        w_ref,
+        xn_ref,
+        dgu_t_ref,
+        w_sem,
+        load_sem,
+        *scratch,
+    ):
+        total = scratch[-1]
+        w_load = Load([(w_hbm, w_ref)], w_sem).begin()
+        load = Load([(dgu_t_hbm, dgu_t_ref), (xn_hbm, xn_ref)], load_sem).begin()
+
+        def partial(slot, t):
+            r = pl.ds(pl.multiple_of(slot * rows, rows), rows)
+            lanes = pl.ds(pl.multiple_of(t * tile, tile), tile)
+            acc = nn(dgu_ref[r, :unit_rows], w_ref[0, :, lanes])
+            for n in range(1, chunks):
+                acc = acc + nn(dgu_ref[r, n * unit_rows : (n + 1) * unit_rows], w_ref[n, :, lanes])
+            return acc
+
+        def up_gradient(first, last):
+            @pl.loop(first, last)
+            def _(k):
+                r = pl.ds(pl.multiple_of(k * part, part), part)
+
+                @pl.loop(0, width // tile)
+                def _(t):
+                    lanes = pl.ds(pl.multiple_of(t * tile, tile), tile)
+                    g_up_ref[r, lanes] = nn(dgu_t_ref[r], xn_ref[:, lanes]).astype(BF)
+
+        scatter = Scatter(n_ctx, partial, tile, *scratch)
+        greet_neighbours(n_ctx)
+        w_load.wait()
+        scatter.to_mate()
+        scatter.pairs()
+        load.wait()
+        up_gradient(0, units // part)
+        scatter.join()
+        up_gradient(units // part, 2 * units // part)
         scatter.end()
         dgain_ref[...] = jnp.zeros_like(dgain_ref)
 
@@ -753,19 +885,31 @@
 
         row_chunks(rows, 32, finish)
 
-    outs = [shape((rows, width), F32), shape((rows, width), BF), shape((8, width), F32)]
+    outs = [
+        shape((rows, width), F32),
+        shape((rows, width), BF),
+        shape((8, width), F32),
+        shape((2 * units, width), BF),
+    ]
+    scratch = [
+        pltpu.VMEM((chunks, unit_rows, width), BF),
+        pltpu.VMEM(xn_all.shape, BF),
+        pltpu.VMEM(dgu_t.shape, BF),
+        pltpu.SemaphoreType.DMA((1,)),
+        pltpu.SemaphoreType.DMA((2,)),
+    ]
     return remote_call(
         kernel,
-        "feed_forward_input",
         number,
-        [dgu, weights, h1, cotangent, gain],
+        [dgu, gate_up, h1, cotangent, gain, xn_all, dgu_t],
         outs,
-        scatter_scratch(rows, width),
+        scratch + scatter_scratch(rows, width),
+        any_ins=(1, 5, 6),
     )
 
 
 def attention_backward(
-    dh_all, out_w, qkv, attn, lse, cosine, sine, pos_rows, pos_columns, hidden, weights, unit_rows, h1, swapped, g_out, n_outer, n_ctx, number
+    dh_all, xn, qkv, attn, lse, cosine, sine, pos_rows, pos_columns, hidden, out_w, down_w, h1, swapped, n_outer, n_ctx, number
 ):
     rows = dh_all.shape[0]
     own_rows, width = h1.shape
@@ -773,29 +917,37 @@
     heads = attn.shape[1] // LANES
     k_at, v_at = heads * LANES, (heads + 1) * LANES
     block = min(QUERY_BLOCK, group)
-    pack = weights.shape[1] - unit_rows
-    units = hidden.shape[1]
-    span = width // units
+    features = attn.shape[1]
+    tile = 256
+    place_rows = width // n_outer // (2 * n_ctx)
 
     def kernel(
         dh_hbm,
-        ow_hbm,
-        qkv_ref,
-        attn_ref,
+        xn_hbm,
+        qkv_hbm,
+        attn_hbm,
         lse_ref,
-        cos_ref,
-        sin_ref,
+        cos_hbm,
+        sin_hbm,
         rows_ref,
-        columns_ref,
+        columns_hbm,
         hidden_ref,
+        out_w_hbm,
         w_hbm,
         h_ref,
         swap_src,
-        g_ref,
         dproj_ref,
         result_ref,
         swap_dst,
         g_dst,
+        g_qkv_ref,
+        xn_ref,
+        qkv_ref,
+        attn_ref,
+        cos_ref,
+        sin_ref,
+        columns_ref,
+        g_ref,
         g_arrived,
         g_sum,
         g_send,
@@ -806,7 +958,6 @@
         out_w_ref,
         dh_ref,
         load_sem,
-        out_load_sem,
         dh_sem,
         *scratch,
     ):
@@ -814,69 +965,94 @@
         total = scratch[-1]
         o = lax.axis_index("o")
         peers = outer_peers(n_outer)
-        load = Load([(w_hbm.at[:, pl.ds(unit_rows, pack)], w_ref)], load_sem).begin()
-        out_load = Load(out_loads(ow_hbm, out_w_ref), out_load_sem).begin()
-        dh_load = Load([(dh_hbm, dh_ref)], dh_sem).begin()
+        load = Load([(w_hbm, w_ref)], load_sem).begin()
+        pairs = [(out_w_hbm, out_w_ref), (dh_hbm, dh_ref), (attn_hbm, attn_ref), (qkv_hbm, qkv_ref), (cos_hbm, cos_ref), (sin_hbm, sin_ref)]
+        dh_load = Load(pairs + [(columns_hbm, columns_ref), (xn_hbm, xn_ref)], dh_sem).begin()
         swap = Swap(n_ctx, [(swap_src, swap_dst)], *swap_sem)
         g_swap = Swap(n_ctx, [(g_sum, g_dst)], *g_swap_sem)
 
         def partial(slot, t):
             a = hidden_ref[pl.ds(pl.multiple_of(slot * own_rows, own_rows), own_rows)]
-            lanes = pl.ds(pl.multiple_of((t % span) * units, units), units)
-            return nt(a, w_ref[t // span, :, lanes])
-
-        scatter = Scatter(n_ctx, partial, pack, *scratch)
+            return nt(a, w_ref[pl.ds(pl.multiple_of(t * tile, tile), tile)])
+
+        scatter = Scatter(n_ctx, partial, tile, *scratch)
         greet(swap.devices + peers)
-        g_copies = [
-            send(g_ref.at[device[0]], g_arrived.at[k], g_send.at[k], g_recv.at[k], device) for k, device in enumerate(peers)
-        ]
-
-        def back(g):
+
+        def back(g, b):
             keys_at = pl.ds(g * group, group)
-            dk_ref[...] = jnp.zeros_like(dk_ref)
-            dv_ref[...] = jnp.zeros_like(dv_ref)
-
-            @pl.loop(0, group // block)
-            def _(b):
-                r = pl.ds(pl.multiple_of(g * group + b * block, block), block)
-                key_pos = columns_ref[keys_at, 0:1]
-                ok = (key_pos >= rows_ref[1:2, r]) & (key_pos <= rows_ref[0:1, r])
-                da_all = nn(dh_ref[r], out_w_ref[...]).astype(BF)
-                for h in range(heads):
-                    lanes = slice(h * LANES, (h + 1) * LANES)
-                    da, q = da_all[:, lanes], qkv_ref[r, lanes]
-                    keys = qkv_ref[keys_at, k_at : k_at + LANES]
-                    s = nt(keys, q) * SCALE - lse_ref[h : h + 1, r]
-                    p = jnp.exp(jnp.where(ok, s, MASK_FILL))
-                    dv_ref[...] += nn(p.astype(BF), da)
-                    delta = jnp.transpose(da.astype(F32) * attn_ref[r, lanes].astype(F32))
-                    delta = jnp.sum(delta, 0, keepdims=True)
-                    dp = nt(qkv_ref[keys_at, v_at : v_at + LANES], da)
-                    ds = (p * (dp - delta)).astype(BF)
-                    dk_ref[...] += nn(ds, q)
-                    dq = tn(ds, keys) * SCALE
-                    dproj_ref[r, lanes] = rotate(dq, cos_ref[r], -sin_ref[r]).astype(BF)
-
-            dk = rotate(dk_ref[...] * SCALE, cos_ref[keys_at], -sin_ref[keys_at])
-            dproj_ref[keys_at, k_at : k_at + LANES] = dk.astype(BF)
-            dproj_ref[keys_at, v_at : v_at + LANES] = dv_ref[...].astype(BF)
+            r = pl.ds(g * group + b * block, block)
+            if b == 0:
+                dk_ref[...] = jnp.zeros_like(dk_ref)
+                dv_ref[...] = jnp.zeros_like(dv_ref)
+            key_pos = columns_ref[keys_at, 0:1]
+            ok = (key_pos >= rows_ref[1:2, r]) & (key_pos <= rows_ref[0:1, r])
+            da_all = nn(dh_ref[r], out_w_ref[...]).astype(BF)
+
+            for h in range(heads):
+                lanes = slice(h * LANES, (h + 1) * LANES)
+                da, q = da_all[:, lanes], qkv_ref[r, lanes]
+                keys = qkv_ref[keys_at, k_at : k_at + LANES]
+                s = nt(keys, q) * SCALE - lse_ref[h : h + 1, r]
+                p = jnp.exp(jnp.where(ok, s, MASK_FILL))
+                dv_ref[...] += nn(p.astype(BF), da)
+                delta = jnp.transpose(da.astype(F32) * attn_ref[r, lanes].astype(F32))
+                delta = jnp.sum(delta, 0, keepdims=True)
+                dp = nt(qkv_ref[keys_at, v_at : v_at + LANES], da)
+                ds = (p * (dp - delta)).astype(BF)
+                dk_ref[...] += nn(ds, q)
+                dq = tn(ds, keys) * SCALE
+                dproj_ref[r, lanes] = rotate(dq, cos_ref[r], -sin_ref[r]).astype(BF)
+
+            if b == group // block - 1:
+                dk = rotate(dk_ref[...] * SCALE, cos_ref[keys_at], -sin_ref[keys_at])
+                dproj_ref[keys_at, k_at : k_at + LANES] = dk.astype(BF)
+                dproj_ref[keys_at, v_at : v_at + LANES] = dv_ref[...].astype(BF)
+
+        def out_gradient():
+            @pl.loop(0, width // 384)
+            def _(k):
+                d = pl.ds(pl.multiple_of(k * 384, 384), 384)
+                g_ref[d] = jnp.transpose(tn(attn_ref[...], dh_ref[:, d])).astype(BF)
+
+        def own_place(outer):
+            return pl.ds(pl.multiple_of(outer * (width // n_outer), 16), width // n_outer)
+
+        def qkv_gradient():
+            half = HEAD_SIZE // 2
+
+            @pl.loop(0, width // 256)
+            def _(t):
+                lanes = pl.ds(pl.multiple_of(t * 256, 256), 256)
+                for h in range(heads + 2):
+                    g = tn(dproj_ref[:, h * LANES : (h + 1) * LANES], xn_ref[:, lanes]).astype(BF)
+                    for k in range(2):
+                        at = h * HEAD_SIZE + k * half
+                        g_qkv_ref[at : at + half, lanes] = g[k * LANES // 2 : k * LANES // 2 + half]
 
         load.wait()
+        units = [(g, b) for g in range(2) for b in range(group // block)]
         scatter.to_mate()
+        dh_load.wait()
+        back(*units[0])
         scatter.pairs()
         swap.begin()
-        out_load.wait()
-        dh_load.wait()
-        back(0)
+        out_gradient()
+        back(*units[1])
         scatter.join()
+        g_copies = [
+            send(g_ref.at[own_place(device[0])], g_arrived.at[k], g_send.at[k], g_recv.at[k], device)
+            for k, device in enumerate(peers)
+        ]
+        for unit in units[2:]:
+            back(*unit)
         for copy in g_copies:
             copy.wait_recv()
+        g_total = g_ref[own_place(o)].astype(F32)
+        for k in range(n_outer - 1):
+            g_total = g_total + g_arrived[k].astype(F32)
         for d in range(2 * n_ctx):
-            g_part = g_ref[o, d].astype(F32)
-            for k in range(n_outer - 1):
-                g_part = g_part + g_arrived[k, d].astype(F32)
-            g_sum[d] = g_part.astype(BF)
-        back(1)
+            g_sum[d] = g_total[d * place_rows : (d + 1) * place_rows].astype(BF)
+        qkv_gradient()
         g_swap.begin()
         scatter.end()
         swap.end()
@@ -889,26 +1065,36 @@
         for copy in g_copies:
             copy.wait_send()
 
-    outs = [shape(qkv.shape, BF), shape((own_rows, width), BF), shape(swapped.shape, BF), shape(g_out.shape[1:], BF)]
-    ins = [dh_all, out_w, qkv, attn, lse, cosine, sine, pos_rows, pos_columns, hidden, weights, h1, swapped, g_out]
-    features = attn.shape[1]
-    n_loads = out_w.shape[0] * width // features
+    outs = [
+        shape(qkv.shape, BF),
+        shape((own_rows, width), BF),
+        shape(swapped.shape, BF),
+        shape((2 * n_ctx, place_rows, features), BF),
+        shape((qkv.shape[1] // LANES * HEAD_SIZE, width), BF),
+    ]
+    ins = [dh_all, xn, qkv, attn, lse, cosine, sine, pos_rows, pos_columns, hidden, out_w, down_w, h1, swapped]
     scratch = [
-        pltpu.VMEM((n_outer - 1,) + g_out.shape[1:], BF),
-        pltpu.VMEM(g_out.shape[1:], BF),
+        pltpu.VMEM(xn.shape, BF),
+        pltpu.VMEM(qkv.shape, BF),
+        pltpu.VMEM(attn.shape, BF),
+        pltpu.VMEM(cosine.shape, F32),
+        pltpu.VMEM(sine.shape, F32),
+        pltpu.VMEM(pos_columns.shape, jnp.int32),
+        pltpu.VMEM((width, features), BF),
+        pltpu.VMEM((n_outer - 1, width // n_outer, features), BF),
+        pltpu.VMEM((2 * n_ctx, place_rows, features), BF),
         pltpu.SemaphoreType.DMA((n_outer - 1,)),
         pltpu.SemaphoreType.DMA((n_outer - 1,)),
         pltpu.VMEM((group, LANES), F32),
         pltpu.VMEM((group, LANES), F32),
-        pltpu.VMEM((weights.shape[0], pack, width), BF),
-        pltpu.VMEM((width, features), BF),
+        pltpu.VMEM(down_w.shape, BF),
+        pltpu.VMEM(out_w.shape, BF),
         pltpu.VMEM(dh_all.shape, BF),
         pltpu.SemaphoreType.DMA((1,)),
-        pltpu.SemaphoreType.DMA((n_loads,)),
-        pltpu.SemaphoreType.DMA((1,)),
+        pltpu.SemaphoreType.DMA((8,)),
     ]
     scratch += swap_sems(1, n_ctx) + swap_sems(1, n_ctx) + scatter_scratch(own_rows, width)
-    return remote_call(kernel, "attention_backward", number, ins, outs, scratch, any_ins=(0, 1, 10))
+    return remote_call(kernel, number, ins, outs, scratch, any_ins=(0, 1, 2, 3, 5, 6, 8, 10, 11))
 
 
 def attention_input(dproj, w, tokens, dh1, gain, gain_terms, n_outer, n_ctx, number):
@@ -963,7 +1149,7 @@
 
     outs = [shape((rows, width), F32), shape((8, LANES), F32)]
     ins = [dproj, w, tokens, dh1, gain, gain_terms]
-    n_loads = w.shape[0] * w.shape[1] // (HEAD_SIZE // 2)
+    n_loads = features // (LANES // 2)
     scratch = [pltpu.VMEM((features, width), BF), pltpu.SemaphoreType.DMA((n_loads,))]
     scratch += swap_sems(1, n_ctx)
     scratch += [
@@ -975,7 +1161,7 @@
         pltpu.SemaphoreType.DMA,
     ]
     scratch += scatter_scratch(rows, width)
-    return remote_call(kernel, "attention_input", number, ins, outs, scratch, any_ins=(1,))
+    return remote_call(kernel, number, ins, outs, scratch, any_ins=(1,))
 
 
 def make_shards(n_outer, n_inner, n_ctx):
@@ -983,75 +1169,64 @@
     moves = feature_moves(n_outer, n_plane)
     back = [(b, a) for a, b in moves]
 
-    def shards(tokens, norm_attn, w_qkv, w_out, norm_mlp, w_gate_up, w_down, cotangent, seq_lengths, block_slot):
-        rows, width = tokens.shape
+    def layer(tokens, norm_attn, w_qkv, w_out, norm_mlp, w_gate_up, w_down, cotangent, seq_lengths, block_slot):
+        _, width = tokens.shape
         gain_rows = norm_attn.shape[0]
-        feature_rows = w_qkv.shape[0]
         out_rows = w_out.shape[0]
         unit_rows = w_gate_up.shape[0]
         n_seqs, n_slots = seq_lengths.shape[1], block_slot.shape[1]
         units = FF // n_plane
+        qkv_w = z_ag(lax.ppermute(w_qkv, ALL, moves)).reshape(CHUNKS, -1, width)
         gain_part = jnp.pad(jnp.stack([norm_attn, norm_mlp]), ((0, 6), (0, LANES - gain_rows)))
         meta = jnp.concatenate([seq_lengths[0], block_slot[0]])
         meta = jnp.pad(meta[None], ((0, 7), (0, LANES - n_seqs - n_slots)))
-        moved_qkv = lax.ppermute(w_qkv, ALL, moves)
-        metas, gains = exchange(meta, gain_part, n_outer, n_ctx, 0)
-        gains = gains[:, :, :2, :gain_rows].transpose(2, 0, 1, 3).reshape(2, width)
-        moved_qkv, metas = lax.optimization_barrier((moved_qkv, metas))
-        qkv_w = z_ag(moved_qkv).reshape(CHUNKS, -1, width)
-        source = tokens.astype(F32)
-        xn1 = (source * inv_rms(source) * gains[0:1]).astype(BF)
-        out_parts = pad_heads(w_out, 1).reshape(out_rows, n_plane, -1).transpose(1, 0, 2)
+        out_parts = pad_heads(w_out, 1).reshape(out_rows, 2, n_plane // 2, -1).transpose(2, 1, 0, 3)
+        out_parts = out_parts.reshape(n_plane, out_rows, -1)
         down_parts = w_down.reshape(out_rows, n_outer // 2, n_plane, unit_rows).transpose(2, 0, 1, 3)
         down_parts = down_parts.reshape(n_plane, out_rows, units)
-        xn1, out_parts, down_parts, cosine, sine, pos_rows, pos_columns = prologue(
-            xn1, out_parts, down_parts, metas, n_seqs, n_ctx, 1
+        w_gate_up, out_parts, down_parts = lax.optimization_barrier((w_gate_up, out_parts, down_parts))
+        gate_up = z_ag(w_gate_up)
+        gate_up = gate_up.reshape(CHUNKS, -1, width)
+        x_all, out_parts, down_w, gains, cosine, sine, pos_rows, pos_columns = prologue(
+            tokens, out_parts, down_parts, gain_part, meta, n_seqs, n_outer, n_ctx, 1
         )
-        xn1 = xn1.reshape(-1, width)
-        features = out_parts.shape[-1]
-        out_pack = out_parts.reshape(width // features, -1, features).transpose(1, 0, 2).reshape(-1, width)
-        short = -(-(1 << 20) // (2 * width * n_outer * 16)) * 16 - out_pack.shape[0]
-        out_w = z_ag(jnp.pad(out_pack, ((0, max(short, 0)), (0, 0)))).reshape(n_outer, -1, width)
-        if n_outer != CHUNKS:
-            out_w = out_w[:, : out_pack.shape[0]].reshape(n_outer, -1, width // features, features).transpose(0, 2, 1, 3)
-            out_w = pack_down(out_w.reshape(width, features), CHUNKS)
-        down_pack = down_parts.reshape(width // units, -1, units).transpose(1, 0, 2).reshape(-1, width)
-        mlp_w = z_ag(jnp.concatenate([w_gate_up, down_pack], 0)).reshape(n_outer, -1, width)
-        mlp_w = in_chunks(mlp_w, unit_rows, units)
-        qkv, attn, lse, dy_all = attention_forward(xn1, qkv_w, cosine, sine, pos_rows, pos_columns, cotangent, n_ctx, 2)
+        x_all = x_all.reshape(-1, width)
+        gains = gains[:, :, :2, :gain_rows].transpose(2, 0, 1, 3).reshape(2, width)
+        down_w = z_ag(down_w.reshape(-1, units))
+        qkv, attn, lse, dy_all, xn1, out_w = attention_forward(
+            x_all, gains, qkv_w, cosine, sine, pos_rows, pos_columns, cotangent, out_parts, n_outer, n_ctx, 2
+        )
+        out_w = out_w.reshape(width, -1)
         h1, xn2 = output_projection(attn, out_w, tokens, gains, n_ctx, 3)
-        xn2_all = plane_gather(xn2, n_ctx, 4)
-        chunk_rows = 2 * units // CHUNKS
-        hidden, dgu = feed_forward(xn2_all, dy_all, mlp_w, chunk_rows, units)
-        g_down = tn(dy_all, hidden).astype(BF)
+        xn2_all, hidden, dgu, dgu_t, g_down = feed_forward(xn2, dy_all, gate_up, down_w, n_ctx, 4)
         dgu, g_down = lax.optimization_barrier((dgu, g_down))
-        g_gate_up = tn(dgu, xn2_all).astype(BF)
-        dgu, g_gate_up = lax.optimization_barrier((dgu, g_gate_up))
-        g_down, g_gate_up = z_rs(g_down), z_rs(g_gate_up)
-        dh1, dh1_bf, dgain_two = feed_forward_input(dgu, mlp_w, chunk_rows, h1, cotangent, gains, n_ctx, 5)
+        g_down = z_rs(g_down)
+        dh1, dh1_bf, dgain_two, g_gate_up = feed_forward_input(
+            dgu, gate_up, h1, cotangent, gains, xn2_all.reshape(-1, width), dgu_t, n_ctx, 5
+        )
+        g_gate_up = z_rs(g_gate_up)
         dh1_all = plane_gather(dh1_bf, n_ctx, 6)
-        dh1_all, g_gate_up, g_down = lax.optimization_barrier((dh1_all, g_gate_up, g_down))
+        dh1_all, g_down = lax.optimization_barrier((dh1_all, g_down))
         g_down = g_down.reshape(n_plane, out_rows, units)
-        g_out = tn(dh1_all, attn).astype(BF).reshape(n_outer, n_plane, out_rows, -1)
-        dproj, result, g_down, g_out = attention_backward(
-            dh1_all, out_w, qkv, attn, lse, cosine, sine, pos_rows, pos_columns, hidden, mlp_w, chunk_rows, h1, g_down, g_out, n_outer, n_ctx, 7
+        dproj, result, g_down, g_out, g_qkv = attention_backward(
+            dh1_all, xn1, qkv, attn, lse, cosine, sine, pos_rows, pos_columns, hidden, out_w, down_w, h1, g_down, n_outer, n_ctx, 7
         )
-        g_qkv = cut_heads(tn(dproj, xn1).astype(BF), 0)
         terms = jnp.sum(qkv_w.reshape(-1, width).astype(F32) * g_qkv.astype(F32), 0) / gains[0]
         terms = jnp.stack([terms, dgain_two[0]]).reshape(2, n_outer, n_plane, gain_rows).transpose(2, 1, 0, 3)
         terms = jnp.pad(terms, ((0, 0), (0, 0), (0, 6), (0, LANES - gain_rows)))
-        dproj, g_qkv = lax.optimization_barrier((dproj, g_qkv))
+        dproj, g_qkv, g_gate_up = lax.optimization_barrier((dproj, g_qkv, g_gate_up))
         g_qkv = z_rs(g_qkv)
         grad_input, g = attention_input(dproj, qkv_w, tokens, dh1, gains, terms, n_outer, n_ctx, 8)
         grad_input, g_qkv = lax.optimization_barrier((grad_input, g_qkv))
         grad_qkv = lax.ppermute(g_qkv, ALL, back).astype(F32)
-        grad_out = cut_heads(g_out.transpose(1, 0, 2).reshape(out_rows, -1), 1).astype(F32)
+        g_out = g_out.reshape(n_plane // 2, 2, out_rows, -1).transpose(2, 1, 0, 3)
+        grad_out = cut_heads(g_out.reshape(out_rows, -1), 1).astype(F32)
         grad_down = g_down.reshape(n_plane, out_rows, n_outer // 2, unit_rows).transpose(1, 2, 0, 3)
         grad_down = grad_down.reshape(out_rows, -1).astype(F32)
         g = g[:, :gain_rows]
         return (result, grad_input, g[0], grad_qkv, grad_out, g[1], g_gate_up.astype(F32), grad_down)
 
-    return shards
+    return layer
 
 
 def solution(mesh):

time: 458 us -> 437 us (0.954)
  matrix products: 31.9 us -> 0 us
  waiting for transfers between devices: 21.3 us -> 37.5 us
    dot_general x4 -> x0, matrix products: 31.9 us -> none  [tn(): lax.dot_general(a, b, (((0,), (0,)), ((), ())), preferred_element_type=F32)]
    all_gather x3, waiting for transfers between devices: 5.85 us -> 36.7 us  [z_ag(): return lax.all_gather(x, 'o', axis=0, tiled=True)]
    pallas_call x9 -> x8, Pallas kernels: 332 us -> 353 us  [remote_call(): pl.pallas_call(kernel, out_shape=outs, in_specs=[ANYWHERE if n in any_ins...]
    pallas_call x1 -> x0, Pallas kernels: 18.5 us -> none  [feed_forward(): pl.pallas_call(kernel, grid=(rows // block,), out_shape=[shape((rows, num...]
    ppermute x2, waiting for transfers between devices: 8.95 us -> 0.01 us  [the longest x1 0.01 us: layer(): qkv_w = z_ag(lax.ppermute(w_qkv, ALL, moves)).reshape(CHUNKS, -1, width)]
    reduce_scatter x3, waiting for transfers between devices: 6.37 us -> 0.06 us  [z_rs(): return lax.psum_scatter(x, 'o', scatter_dimension=0, tiled=True)]
  transfers between devices with their start and end apart: 8 -> 8, of which waited for: 3 -> 1; matrix products, arithmetic and copies ran while one was open for 7% -> 4% of each run, Pallas kernels for 62% -> 72%
where the time goes in v3:
time: 437 us; the launch traced here: 430 us
  Pallas kernels  353 us (81%)
  waiting for transfers between devices  37.5 us (9%)
  local copies, waits for them, and re-layouts  15.5 us (4%)
  between operations  14.6 us (3%)
  other arithmetic  4.62 us (1%)
    pallas_call x8, Pallas kernels, remote_call(): pl.pallas_call(kernel, out_shape=outs, in_specs=[ANYWHERE if n in any_ins...  353 us
    all_gather x3, waiting for transfers between devices, z_ag(): return lax.all_gather(x, 'o', axis=0, tiled=True)  36.7 us
  transfers between devices with their start and end apart: 8, of which 1 were waited for; matrix products, arithmetic and copies ran while one was open for 4% of the time, Pallas kernels for 72%

profile of v3, /device:TPU:2, one launch (start us, length us, event | category | flops | bytes accessed | tf_op | source)
XLA Modules:
  0.0 429.6 jit_solution(2487323580596262070)
XLA Ops:
  7.2 1.8 collective-permute-start
  9.8 1.3 reshape.78
  11.5 0.7 copy.23
  12.6 1.0 reshape.81.down_src
  14.9 54.6 %shard_map.179 = (bf16[8,256,1536]{2,1,0:T(8,128)(2,1)}, bf16[8,48,256]{2,1,0:T(8,128)(2,1)}, bf16[8,48,512]{2,1,0:T(8,128)(2,1)}, f32[4,8,8,128]{3,2,1,0:T(8,12...) custom-call(bf16[256,1536]{1,0:T(8,128)(2,1)} %x_ref.5, ...), custom_call_target="tpu_custom_call" | custom-call | tf_op jit(solution)/shard_map/pallas_call | solution.py:329
  70.5 0.9 slice_bitcast_fusion
  72.1 39.4 %shard_map.180 = (bf16[2048,512]{1,0:T(8,128)(2,1)}, bf16[2048,256]{1,0:T(8,128)(2,1)}, f32[8,2048]{1,0:T(8,128)}, bf16[8,256,1536]{2,1,0:T(8,128)(2,1)}, bf16[2...) custom-call(bf16[2048,1536]{1,0:T(8,128)(2,1)} %bitcast.47, f32[2,1536]{1,0:T(2,128)} %reshape.83.gain_ref, ...), custom_call_target="tpu_custom_call" | custom-call | tf_op jit(solution)/shard_map/pallas_call | solution.py:329
  111.5 37.0 %shard_map.181 = (f32[256,1536]{1,0:T(8,128)}, bf16[256,1536]{1,0:T(8,128)(2,1)}) custom-call(bf16[2048,256]{1,0:T(8,128)(2,1)} %get-tuple-element.61.attn_ref.attn_hbm, bf16[1536,256]{1,0:T(8,128)(2,1)} %bitcast.49, bf16[256,1536]{1,0:T(8,128)(2,1)} %x_ref.5, f32[2,1536]{1,0:T(2,128)} %reshape.83.gain_ref), custom_call_target="tpu_custom_call" | custom-call | tf_op jit(solution)/shard_map/pallas_call | solution.py:329
  148.6 36.6 %all-gather.6.cloned.1.call-done = bf16[1024,1536]{1,0:T(8,128)(2,1)} async-done(((bf16[256,1536]{1,0:T(8,128)(2,1)}), bf16[1024,1536]{1,0:T(8,128)(2,1)}) %all-gather.6.cloned.1.call-update) | async-done | bytes 3145744 | tf_op jit(solution)/shard_map/all_gather | solution.py:44
  185.3 44.8 %shard_map.182 = (bf16[8,256,1536]{2,1,0:T(8,128)(2,1)}, bf16[2048,512]{1,0:T(8,128)(2,1)}, bf16[2048,1024]{1,0:T(8,128)(2,1)}, bf16[1024,2048]{1,0:T(8,128)(2,1)}, bf16[1536,512]{1,0:T(8,128)(2,1)}) custom-call(bf16[256,1536]{1,0:T(8,128)(2,1)} %get-tuple-element.63.x_ref, bf16[2048,1536]{1,0:T(8,128)(2,1)} %bitcast.48, bf16[4,256,1536]{2,1,0:T(8,128)(2,1)} %bitcast.42, ...), custom_call_target="tpu_custom_call" | custom-call | tf_op jit(solution)/shard_map/pallas_call | solution.py:329
  230.1 43.0 %shard_map.183 = (f32[256,1536]{1,0:T(8,128)}, bf16[256,1536]{1,0:T(8,128)(2,1)}, f32[8,1536]{1,0:T(8,128)}, bf16[1024,1536]{1,0:T(8,128)(2,1)}) custom-call(bf16[2048,1024]{1,0:T(8,128)(2,1)} %get-tuple-element.69.dgu_ref, bf16[4,256,1536]{2,1,0:T(8,128)(2,1)} %bitcast.43, f32[256,1536]{1,0:T(8,128)} %get-tuple-element.70.h_ref, bf16[256,1536]{1,0:T(8,128)(2,1)} %dy_ref.3, ...), custom_call_target="tpu_custom_call" | custom-call | tf_op jit(solution)/shard_map/pallas_call | solution.py:329
  273.2 35.1 %shard_map.184 = bf16[8,256,1536]{2,1,0:T(8,128)(2,1)} custom-call(bf16[256,1536]{1,0:T(8,128)(2,1)} %get-tuple-element.73.src), custom_call_target="tpu_custom_call" | custom-call | tf_op jit(solution)/shard_map/pallas_call | solution.py:329
  308.4 57.4 %shard_map.185 = (bf16[2048,512]{1,0:T(8,128)(2,1)}, bf16[256,1536]{1,0:T(8,128)(2,1)}, bf16[8,48,512]{2,1,0:T(8,128)(2,1)}, bf16[8,48,256]{2,1,0:T(8,128)(2,1)}, bf16[384,1536]{1,0:T(8,128)(2,1)}) custom-call(bf16[2048,1536]{1,0:T(8,128)(2,1)} %bitcast.41, bf16[2048,1536]{1,0:T(8,128)(2,1)} %get-tuple-element.76.xn_hbm, ...), custom_call_target="tpu_custom_call" | custom-call | tf_op jit(solution)/shard_map/pallas_call | solution.py:329
  365.8 0.9 slice_reduce_fusion
  366.8 1.6 multiply_reduce_fusion
  369.6 42.0 %shard_map.186 = (f32[256,1536]{1,0:T(8,128)}, f32[8,128]{1,0:T(8,128)}) custom-call(bf16[2048,512]{1,0:T(8,128)(2,1)} %get-tuple-element.85.d_ref, bf16[4,96,1536]{2,1,0:T(8,128)(2,1)} %bitcast.45, bf16[256,1536]{1,0:T(8,128)(2,1)} %x_ref.5, f32[256,1536]{1,0:T(8,128)} %get-tuple-element.86.dh_ref, f32[2,1536]{1,0:T(2,128)} %reshape.83.gain_ref, ...), custom_call_target="tpu_custom_call" | custom-call | tf_op jit(solution)/shard_map/pallas_call | solution.py:329
  411.7 1.8 collective-permute-start.1
  413.5 1.2 reshape.93
  415.7 1.3 copy.32
  417.0 1.3 convert_element_type.41
  418.3 1.3 slice_bitcast_fusion.1
  419.6 0.9 convert_element_type.38
  420.5 0.9 copy.42
  421.3 1.1 copy.43
  (63 shorter events, 7.1 us)
Async XLA Ops:
  7.2 5.0 %copy-start.4 = (bf16[48,4096]{1,0:T(8,128)(2,1)S(1)}, bf16[48,4096]{1,0:T(8,128)(2,1)}, u32[]{:S(2)}) copy-start(bf16[48,4096]{1,0:T(8,128)(2,1)} %param.18) | copy-start | bytes 1179652
  7.2 64.9 %all-gather.4.cloned.1.call-start = ((), (), s32[]{:S(2)}) async-start(), calls=%async_computation.3 | async-start | bytes 1474560 | tf_op jit(solution)/shard_map/all_gather | solution.py:44
  7.2 1.8 collective-permute-start
  9.0 0.7 copy-start.6
  9.7 138.9 %all-gather.8.cloned.1.call-start = ((), (), s32[]{:S(2)}) async-start(), calls=%async_computation.5 | async-start | bytes 1966080 | tf_op jit(solution)/shard_map/all_gather | solution.py:44
  11.1 2.5 copy-start.10
  11.1 2.5 copy-start.11
  11.1 3.2 copy-start.8
  11.1 3.2 copy-start.9
  69.5 115.7 %all-gather.6.cloned.1.call-start = ((), (), s32[]{:S(2)}) async-start(), calls=%async_computation.4 | async-start | bytes 3932160 | tf_op jit(solution)/shard_map/all_gather | solution.py:44
  70.2 238.1 %reduce-scatter.4.cloned.1.call-start = ((), (), s32[]{:S(2)}) async-start(), calls=%async_computation.6 | async-start | bytes 1966080 | tf_op jit(solution)/shard_map/reduce_scatter | solution.py:48
  230.0 135.7 %reduce-scatter.6.cloned.1.call-start = ((), (), s32[]{:S(2)}) async-start(), calls=%async_computation.7 | async-start | bytes 3932160 | tf_op jit(solution)/shard_map/reduce_scatter | solution.py:48
  273.2 138.5 %reduce-scatter.8.cloned.1.call-start = ((), (), s32[]{:S(2)}) async-start(), calls=%async_computation.8 | async-start | bytes 1474560 | tf_op jit(solution)/shard_map/reduce_scatter | solution.py:48
  308.4 58.4 %copy-start = (bf16[384,1536]{1,0:T(8,128)(2,1)S(1)}, bf16[384,1536]{1,0:T(8,128)(2,1)}, u32[]{:S(2)}) copy-start(bf16[384,1536]{1,0:T(8,128)(2,1)} %all-gather.4.cloned.1.call-done) | copy-start | bytes 3538948
  365.7 2.7 copy-start.7
  411.6 3.1 copy-start.5
  411.7 7.9 %collective-permute-start.1 = (bf16[96,1536]{1,0:T(8,128)(2,1)}, bf16[96,1536]{1,0:T(8,128)(2,1)S(1)}, u32[]{:S(2)}, u32[]{:S(2)}) collective-permute-start(bf16[96,1536]{1,0:T(8,128)(2,1)} %reduce-scatter.8.cloned.1.call-done), channel_id=1, source_target_pairs={{0,0},{8,1},{2,2},{10,3},{4,4},{12,5},{6,6},{14,7},{1,8},{9,9},{3,... | collective-permute-start | bytes 884744 | tf_op jit(solution)/shard_map/ppermute | solution.py:1221
  414.7 2.3 copy-start.3
  415.6 4.8 %copy-start.2 = (bf16[256,1536]{1,0:T(8,128)(2,1)S(1)}, bf16[256,1536]{1,0:T(8,128)(2,1)}, u32[]{:S(2)}) copy-start(bf16[256,1536]{1,0:T(8,128)(2,1)} %get-tuple-element.106) | copy-start | bytes 2359300
  417.0 4.4 %copy-start.1 = (f32[256,1536]{1,0:T(8,128)S(1)}, f32[256,1536]{1,0:T(8,128)}, u32[]{:S(2)}) copy-start(f32[256,1536]{1,0:T(8,128)} %get-tuple-element.107) | copy-start | bytes 4718596
Sparse Core Ops, SparseCore 0:
  10.1 40.9 all-gather.3
  69.6 51.0 all-gather.7
  122.3 62.8 all-gather.5
  230.2 33.7 reduce-scatter.3
  273.3 58.6 reduce-scatter.5
  365.9 31.4 reduce-scatter.7

commit v4 on v3

--- a/solution.py
+++ b/solution.py
@@ -514,19 +514,6 @@
     return remote_call(kernel, number, ins, outs, scratch, any_outs=(0,))
 
 
-def plane_gather(x, n_ctx, number):
-    def kernel(src, out, *sems):
-        gather = Gather(n_ctx, src, out, *sems)
-        greet_neighbours(n_ctx)
-        gather.begin()
-        gather.middle()
-        gather.end()
-
-    outs = [shape((2 * n_ctx,) + x.shape, x.dtype)]
-    got = remote_call(kernel, number, [x], outs, GATHER_SEMS, any_outs=(0,))
-    return got[0].reshape(-1, x.shape[-1])
-
-
 def rotate(x, cosine, sine):
     return x * cosine + pltpu.roll(x, LANES // 2, 1) * sine
 
@@ -665,12 +652,12 @@
     return got[0], got[1], got[2], got[3].reshape(rows, width), got[4], got[5]
 
 
-def output_projection(attn, out_w, tokens, gain, n_ctx, number):
+def output_projection(attn, out_w, tokens, gain, down_part, n_outer, n_ctx, number):
     rows, width = tokens.shape
     tile = 256
 
 
-    def kernel(attn_ref, w_ref, x_ref, gain_ref, h_ref, xn_ref, *scratch):
+    def kernel(attn_ref, w_ref, x_ref, gain_ref, part_ref, h_ref, xn_ref, down_w, z_send, z_recv, z_local, *scratch):
         total = scratch[-1]
 
         def partial(slot, t):
@@ -678,7 +665,12 @@
             return nt(a, w_ref[pl.ds(pl.multiple_of(t * tile, tile), tile)])
 
         scatter = Scatter(n_ctx, partial, tile, *scratch)
-        greet_neighbours(n_ctx)
+        o, i, c, mate, far = places(n_ctx)
+        peers = outer_peers(n_outer)
+        greet([(o, i, mate), (o, 1 - i, c), (o, i, far)] + peers)
+        z_copies = [send(part_ref, down_w.at[o], z_send.at[k], z_recv.at[k], device) for k, device in enumerate(peers)]
+        own_part = pltpu.make_async_copy(part_ref, down_w.at[o], z_local)
+        own_part.start()
         scatter.to_mate()
         scatter.pairs()
         scatter.join()
@@ -690,9 +682,19 @@
             xn_ref[r] = (h * inv_rms(h) * gain_ref[1:2]).astype(BF)
 
         row_chunks(rows, 32, finish)
-
-    outs = [shape((rows, width), F32), shape((rows, width), BF)]
-    return remote_call(kernel, number, [attn, out_w, tokens, gain], outs, scatter_scratch(rows, width))
+        own_part.wait()
+        for copy in z_copies:
+            copy.wait_recv()
+            copy.wait_send()
+
+    outs = [shape((rows, width), F32), shape((rows, width), BF), shape((n_outer,) + down_part.shape, BF)]
+    sems = [
+        pltpu.SemaphoreType.DMA((n_outer - 1,)),
+        pltpu.SemaphoreType.DMA((n_outer - 1,)),
+        pltpu.SemaphoreType.DMA,
+    ]
+    ins = [attn, out_w, tokens, gain, down_part]
+    return remote_call(kernel, number, ins, outs, sems + scatter_scratch(rows, width), any_outs=(2,))
 
 
 def feed_forward(xn, dy, gate_up, down, n_ctx, number):
@@ -831,17 +833,20 @@
         xn_hbm,
         dgu_t_hbm,
         dh_ref,
-        dhb_ref,
+        dhb_all,
         dgain_ref,
         g_up_ref,
         w_ref,
         xn_ref,
         dgu_t_ref,
+        dhb_ref,
         w_sem,
         load_sem,
         *scratch,
     ):
+        gather_sems, scratch = scratch[:3], scratch[3:]
         total = scratch[-1]
+        gather = Gather(n_ctx, dhb_ref, dhb_all, *gather_sems)
         w_load = Load([(w_hbm, w_ref)], w_sem).begin()
         load = Load([(dgu_t_hbm, dgu_t_ref), (xn_hbm, xn_ref)], load_sem).begin()
 
@@ -871,7 +876,6 @@
         load.wait()
         up_gradient(0, units // part)
         scatter.join()
-        up_gradient(units // part, 2 * units // part)
         scatter.end()
         dgain_ref[...] = jnp.zeros_like(dgain_ref)
 
@@ -884,10 +888,15 @@
             dhb_ref[r] = dh.astype(BF)
 
         row_chunks(rows, 32, finish)
+        up_gradient(units // part, units // part + 1)
+        gather.begin()
+        up_gradient(units // part + 1, 2 * units // part)
+        gather.middle()
+        gather.end()
 
     outs = [
         shape((rows, width), F32),
-        shape((rows, width), BF),
+        shape((2 * n_ctx, rows, width), BF),
         shape((8, width), F32),
         shape((2 * units, width), BF),
     ]
@@ -895,6 +904,7 @@
         pltpu.VMEM((chunks, unit_rows, width), BF),
         pltpu.VMEM(xn_all.shape, BF),
         pltpu.VMEM(dgu_t.shape, BF),
+        pltpu.VMEM((rows, width), BF),
         pltpu.SemaphoreType.DMA((1,)),
         pltpu.SemaphoreType.DMA((2,)),
     ]
@@ -903,7 +913,8 @@
         number,
         [dgu, gate_up, h1, cotangent, gain, xn_all, dgu_t],
         outs,
-        scratch + scatter_scratch(rows, width),
+        scratch + GATHER_SEMS + scatter_scratch(rows, width),
+        any_outs=(1,),
         any_ins=(1, 5, 6),
     )
 
@@ -1187,25 +1198,25 @@
         w_gate_up, out_parts, down_parts = lax.optimization_barrier((w_gate_up, out_parts, down_parts))
         gate_up = z_ag(w_gate_up)
         gate_up = gate_up.reshape(CHUNKS, -1, width)
-        x_all, out_parts, down_w, gains, cosine, sine, pos_rows, pos_columns = prologue(
+        x_all, out_parts, down_parts, gains, cosine, sine, pos_rows, pos_columns = prologue(
             tokens, out_parts, down_parts, gain_part, meta, n_seqs, n_outer, n_ctx, 1
         )
         x_all = x_all.reshape(-1, width)
         gains = gains[:, :, :2, :gain_rows].transpose(2, 0, 1, 3).reshape(2, width)
-        down_w = z_ag(down_w.reshape(-1, units))
         qkv, attn, lse, dy_all, xn1, out_w = attention_forward(
             x_all, gains, qkv_w, cosine, sine, pos_rows, pos_columns, cotangent, out_parts, n_outer, n_ctx, 2
         )
         out_w = out_w.reshape(width, -1)
-        h1, xn2 = output_projection(attn, out_w, tokens, gains, n_ctx, 3)
+        h1, xn2, down_w = output_projection(attn, out_w, tokens, gains, down_parts, n_outer, n_ctx, 3)
+        down_w = down_w.reshape(-1, units)
         xn2_all, hidden, dgu, dgu_t, g_down = feed_forward(xn2, dy_all, gate_up, down_w, n_ctx, 4)
         dgu, g_down = lax.optimization_barrier((dgu, g_down))
         g_down = z_rs(g_down)
-        dh1, dh1_bf, dgain_two, g_gate_up = feed_forward_input(
+        dh1, dh1_all, dgain_two, g_gate_up = feed_forward_input(
             dgu, gate_up, h1, cotangent, gains, xn2_all.reshape(-1, width), dgu_t, n_ctx, 5
         )
         g_gate_up = z_rs(g_gate_up)
-        dh1_all = plane_gather(dh1_bf, n_ctx, 6)
+        dh1_all = dh1_all.reshape(-1, width)
         dh1_all, g_down = lax.optimization_barrier((dh1_all, g_down))
         g_down = g_down.reshape(n_plane, out_rows, units)
         dproj, result, g_down, g_out, g_qkv = attention_backward(

time: 437 us -> 457 us (1.046)
  the two profiles are of different devices: /device:TPU:2 before, /device:TPU:1 now
where the time goes in v4:
time: 457 us; the launch traced here: 448 us
  Pallas kernels  399 us (87%)
  local copies, waits for them, and re-layouts  15.5 us (3%)
  between operations  14.5 us (3%)
  starting transfers between devices  7.26 us (2%)
  waiting for transfers between devices  6.75 us (1%)
  other arithmetic  4.63 us (1%)
    pallas_call x7, Pallas kernels, remote_call(): pl.pallas_call(kernel, out_shape=outs, in_specs=[ANYWHERE if n in any_ins...  399 us
  transfers between devices with their start and end apart: 7, of which 2 were waited for; matrix products, arithmetic and copies ran while one was open for 4% of the time, Pallas kernels for 79%

profile of v4, /device:TPU:1, one launch (start us, length us, event | category | flops | bytes accessed | tf_op | source)
XLA Modules:
  0.0 448.0 jit_solution(2243497013692434929)
XLA Ops:
  7.2 4.7 %collective-permute-start = (bf16[96,1536]{1,0:T(8,128)(2,1)}, bf16[96,1536]{1,0:T(8,128)(2,1)S(1)}, u32[]{:S(2)}, u32[]{:S(2)}) collective-permute-start(bf16[96,1536]{1,0:T(8,128)(2,1)} %param.14), channel_id=1, source_target_pairs={{0,0},{1,8},{2,2},{3,10},{4,4},{5,12},{6,6},{7,14},{8,1},{9,9},{10... | collective-permute-start | bytes 884744 | tf_op jit(solution)/shard_map/ppermute | solution.py:1190
  11.9 4.6 %collective-permute-done = bf16[96,1536]{1,0:T(8,128)(2,1)S(1)} collective-permute-done((bf16[96,1536]{1,0:T(8,128)(2,1)}, bf16[96,1536]{1,0:T(8,128)(2,1)S(1)}, u32[]{:S(2)}, u32[]{:S(2)}) %collective-permute-start) | collective-permute-done | bytes 294944 | tf_op jit(solution)/shard_map/ppermute | solution.py:1190
  17.3 1.3 reshape.78
  19.1 0.7 copy.23
  20.2 1.0 reshape.81.down_src
  22.5 48.1 %shard_map.179 = (bf16[8,256,1536]{2,1,0:T(8,128)(2,1)}, bf16[8,48,256]{2,1,0:T(8,128)(2,1)}, bf16[8,48,512]{2,1,0:T(8,128)(2,1)}, f32[4,8,8,128]{3,2,1,0:T(8,12...) custom-call(bf16[256,1536]{1,0:T(8,128)(2,1)} %x_ref.5, ...), custom_call_target="tpu_custom_call" | custom-call | tf_op jit(solution)/shard_map/pallas_call | solution.py:329
  70.6 0.9 slice_bitcast_fusion
  72.3 40.5 %shard_map.180 = (bf16[2048,512]{1,0:T(8,128)(2,1)}, bf16[2048,256]{1,0:T(8,128)(2,1)}, f32[8,2048]{1,0:T(8,128)}, bf16[8,256,1536]{2,1,0:T(8,128)(2,1)}, bf16[2...) custom-call(bf16[2048,1536]{1,0:T(8,128)(2,1)} %bitcast.46, f32[2,1536]{1,0:T(2,128)} %reshape.83.gain_ref, ...), custom_call_target="tpu_custom_call" | custom-call | tf_op jit(solution)/shard_map/pallas_call | solution.py:329
  112.7 46.7 %shard_map.181 = (f32[256,1536]{1,0:T(8,128)}, bf16[256,1536]{1,0:T(8,128)(2,1)}, bf16[4,8,48,512]{3,2,1,0:T(8,128)(2,1)}) custom-call(bf16[2048,256]{1,0:T(8,128)(2,1)} %get-tuple-element.62.attn_ref.attn_hbm, bf16[1536,256]{1,0:T(8,128)(2,1)} %bitcast.51, bf16[256,1536]{1,0:T(8,128)(2,1)} %x_ref.5, f32[2,1536]{1,0:T(2,128)} %reshape.83.gain_ref, ...), custom_call_target="tpu_custom_call" | custom-call | tf_op jit(solution)/shard_map/pallas_call | solution.py:329
  159.4 45.4 %shard_map.182 = (bf16[8,256,1536]{2,1,0:T(8,128)(2,1)}, bf16[2048,512]{1,0:T(8,128)(2,1)}, bf16[2048,1024]{1,0:T(8,128)(2,1)}, bf16[1024,2048]{1,0:T(8,128)(2,1)}, bf16[1536,512]{1,0:T(8,128)(2,1)}) custom-call(bf16[256,1536]{1,0:T(8,128)(2,1)} %get-tuple-element.65.x_ref, bf16[2048,1536]{1,0:T(8,128)(2,1)} %bitcast.47, bf16[4,256,1536]{2,1,0:T(8,128)(2,1)} %bitcast.41, ...), custom_call_target="tpu_custom_call" | custom-call | tf_op jit(solution)/shard_map/pallas_call | solution.py:329
  204.9 89.2 %shard_map.183 = (f32[256,1536]{1,0:T(8,128)}, bf16[8,256,1536]{2,1,0:T(8,128)(2,1)}, f32[8,1536]{1,0:T(8,128)}, bf16[1024,1536]{1,0:T(8,128)(2,1)}) custom-call(bf16[2048,1024]{1,0:T(8,128)(2,1)} %get-tuple-element.71.dgu_ref, bf16[4,256,1536]{2,1,0:T(8,128)(2,1)} %bitcast.42, f32[256,1536]{1,0:T(8,128)} %get-tuple-element.72.h_ref, ...), custom_call_target="tpu_custom_call" | custom-call | tf_op jit(solution)/shard_map/pallas_call | solution.py:329
  294.2 76.1 %shard_map.184 = (bf16[2048,512]{1,0:T(8,128)(2,1)}, bf16[256,1536]{1,0:T(8,128)(2,1)}, bf16[8,48,512]{2,1,0:T(8,128)(2,1)}, bf16[8,48,256]{2,1,0:T(8,128)(2,1)}, bf16[384,1536]{1,0:T(8,128)(2,1)}) custom-call(bf16[2048,1536]{1,0:T(8,128)(2,1)} %bitcast.48, bf16[2048,1536]{1,0:T(8,128)(2,1)} %get-tuple-element.78.xn_hbm, ...), custom_call_target="tpu_custom_call" | custom-call | tf_op jit(solution)/shard_map/pallas_call | solution.py:329
  370.4 2.0 reduce-scatter.6.cloned.1.call-done
  372.4 0.8 slice_reduce_fusion
  373.3 1.6 multiply_reduce_fusion
  376.2 53.4 %shard_map.185 = (f32[256,1536]{1,0:T(8,128)}, f32[8,128]{1,0:T(8,128)}) custom-call(bf16[2048,512]{1,0:T(8,128)(2,1)} %get-tuple-element.87.d_ref, bf16[4,96,1536]{2,1,0:T(8,128)(2,1)} %bitcast.44, bf16[256,1536]{1,0:T(8,128)(2,1)} %x_ref.5, f32[256,1536]{1,0:T(8,128)} %get-tuple-element.88.dh_ref, f32[2,1536]{1,0:T(2,128)} %reshape.83.gain_ref, ...), custom_call_target="tpu_custom_call" | custom-call | tf_op jit(solution)/shard_map/pallas_call | solution.py:329
  429.6 2.3 collective-permute-start.1
  432.0 1.2 reshape.93
  434.2 1.3 copy.32
  435.5 1.3 convert_element_type.41
  436.8 1.3 slice_bitcast_fusion.1
  438.1 0.9 convert_element_type.38
  439.0 0.9 copy.42
  439.9 1.1 copy.43
  (59 shorter events, 6.1 us)
Async XLA Ops:
  7.2 12.6 %copy-start.4 = (bf16[48,4096]{1,0:T(8,128)(2,1)S(1)}, bf16[48,4096]{1,0:T(8,128)(2,1)}, u32[]{:S(2)}) copy-start(bf16[48,4096]{1,0:T(8,128)(2,1)} %param.18) | copy-start | bytes 1179652
  7.2 65.1 %all-gather.3.cloned.1.call-start = ((), (), s32[]{:S(2)}) async-start(), calls=%async_computation.3 | async-start | bytes 1474560 | tf_op jit(solution)/shard_map/all_gather | solution.py:44
  7.2 9.3 %collective-permute-start = (bf16[96,1536]{1,0:T(8,128)(2,1)}, bf16[96,1536]{1,0:T(8,128)(2,1)S(1)}, u32[]{:S(2)}, u32[]{:S(2)}) collective-permute-start(bf16[96,1536]{1,0:T(8,128)(2,1)} %param.14), channel_id=1, source_target_pairs={{0,0},{1,8},{2,2},{3,10},{4,4},{5,12},{6,6},{7,14},{8,1},{9,9},{10... | collective-permute-start | bytes 884744 | tf_op jit(solution)/shard_map/ppermute | solution.py:1190
  16.5 0.7 copy-start.6
  17.3 142.1 %all-gather.5.cloned.1.call-start = ((), (), s32[]{:S(2)}) async-start(), calls=%async_computation.4 | async-start | bytes 3932160 | tf_op jit(solution)/shard_map/all_gather | solution.py:44
  18.7 2.5 copy-start.10
  18.8 2.5 copy-start.11
  18.8 3.2 copy-start.8
  18.8 3.2 copy-start.9
  21.2 273.0 %reduce-scatter.4.cloned.1.call-start = ((), (), s32[]{:S(2)}) async-start(), calls=%async_computation.5 | async-start | bytes 1966080 | tf_op jit(solution)/shard_map/reduce_scatter | solution.py:48
  204.9 167.5 %reduce-scatter.6.cloned.1.call-start = ((), (), s32[]{:S(2)}) async-start(), calls=%async_computation.6 | async-start | bytes 3932160 | tf_op jit(solution)/shard_map/reduce_scatter | solution.py:48
  294.1 135.5 %reduce-scatter.8.cloned.1.call-start = ((), (), s32[]{:S(2)}) async-start(), calls=%async_computation.7 | async-start | bytes 1474560 | tf_op jit(solution)/shard_map/reduce_scatter | solution.py:48
  294.2 79.1 %copy-start = (bf16[384,1536]{1,0:T(8,128)(2,1)S(1)}, bf16[384,1536]{1,0:T(8,128)(2,1)}, u32[]{:S(2)}) copy-start(bf16[384,1536]{1,0:T(8,128)(2,1)} %all-gather.3.cloned.1.call-done) | copy-start | bytes 3538948
  370.4 4.7 %copy-start.7 = (bf16[8,48,256]{2,1,0:T(8,128)(2,1)S(1)}, bf16[8,48,256]{2,1,0:T(8,128)(2,1)}, u32[]{:S(2)}) copy-start(bf16[8,48,256]{2,1,0:T(8,128)(2,1)} %get-tuple-element.95) | copy-start | bytes 589828
  429.6 3.6 copy-start.5
  429.6 8.5 %collective-permute-start.1 = (bf16[96,1536]{1,0:T(8,128)(2,1)}, bf16[96,1536]{1,0:T(8,128)(2,1)S(1)}, u32[]{:S(2)}, u32[]{:S(2)}) collective-permute-start(bf16[96,1536]{1,0:T(8,128)(2,1)} %reduce-scatter.8.cloned.1.call-done), channel_id=1, source_target_pairs={{0,0},{8,1},{2,2},{10,3},{4,4},{12,5},{6,6},{14,7},{1,8},{9,9},{3,... | collective-permute-start | bytes 884744 | tf_op jit(solution)/shard_map/ppermute | solution.py:1232
  433.2 2.3 copy-start.3
  434.2 4.8 %copy-start.2 = (bf16[256,1536]{1,0:T(8,128)(2,1)S(1)}, bf16[256,1536]{1,0:T(8,128)(2,1)}, u32[]{:S(2)}) copy-start(bf16[256,1536]{1,0:T(8,128)(2,1)} %get-tuple-element.108) | copy-start | bytes 2359300
  435.5 4.4 copy-start.1
Sparse Core Ops, SparseCore 0:
  17.4 33.9 all-gather.2
  52.9 102.5 all-gather.4
  205.0 41.6 reduce-scatter.3
  294.2 78.0 reduce-scatter.5
  374.5 38.7 reduce-scatter.7

commit v5 on v3

--- a/solution.py
+++ b/solution.py
@@ -130,30 +130,37 @@
         self.mates_slots = [i * n_ctx + mate, j * n_ctx + mate, i * n_ctx + mate_far, j * n_ctx + mate_far]
         self.copies = {}
 
-    def go(self, kind, src, slot, device):
-        copy = send(src, self.out.at[slot], self.sems[0].at[kind], self.sems[1].at[kind], device)
-        self.copies[kind] = copy
+    def go(self, kind, part, src, slot, device):
+        rows = src.shape[0] // PARTS
+        at = pl.ds(part * rows, rows)
+        copy = send(src.at[at], self.out.at[slot, at], self.sems[0].at[kind, part], self.sems[1].at[kind, part], device)
+        self.copies[kind, part] = copy
 
     def begin(self):
-        self.go(1, self.src, self.me, self.x)
-        self.go(2, self.src, self.me, self.y)
-        self.go(0, self.src, self.me, self.mate)
+        for part in range(PARTS):
+            self.go(1, part, self.src, self.me, self.x)
+            self.go(2, part, self.src, self.me, self.y)
+        for part in range(PARTS):
+            self.go(0, part, self.src, self.me, self.mate)
         self.own = pltpu.make_async_copy(self.src, self.out.at[self.me], self.sems[2])
         self.own.start()
 
     def middle(self):
-        self.copies[1].wait_recv()
-        self.copies[2].wait_recv()
-        self.go(5, self.out.at[self.relayed], self.relayed, self.relay)
-        self.go(3, self.out.at[self.s_x], self.s_x, self.mate)
-        self.go(4, self.out.at[self.s_y], self.s_y, self.mate)
+        for part in range(PARTS):
+            self.copies[1, part].wait_recv()
+            self.copies[2, part].wait_recv()
+            self.go(5, part, self.out.at[self.relayed], self.relayed, self.relay)
+            self.go(3, part, self.out.at[self.s_x], self.s_x, self.mate)
+            self.go(4, part, self.out.at[self.s_y], self.s_y, self.mate)
 
     def corner(self):
-        self.copies[5].wait_recv()
-        self.go(6, self.out.at[self.s_d], self.s_d, self.mate)
+        for part in range(PARTS):
+            self.copies[5, part].wait_recv()
+            self.go(6, part, self.out.at[self.s_d], self.s_d, self.mate)
 
     def arrived(self, kind):
-        self.copies[kind].wait_recv()
+        for part in range(PARTS):
+            self.copies[kind, part].wait_recv()
 
     def sent(self):
         self.own.wait()
@@ -167,7 +174,8 @@
         self.sent()
 
 
-GATHER_SEMS = [pltpu.SemaphoreType.DMA((7,)), pltpu.SemaphoreType.DMA((7,)), pltpu.SemaphoreType.DMA]
+PARTS = 2
+GATHER_SEMS = [pltpu.SemaphoreType.DMA((7, PARTS)), pltpu.SemaphoreType.DMA((7, PARTS)), pltpu.SemaphoreType.DMA]
 
 
 class Scatter:
@@ -284,9 +292,6 @@
             self.each(part, rest)
         for copy in self.copies:
             copy.wait_send()
-
-
-PARTS = 2
 
 
 def scatter_scratch(rows, width):

time: 437 us -> 435 us (level)
  transfers between devices with their start and end apart: 8 -> 8, of which waited for: 1 -> 1; matrix products, arithmetic and copies ran while one was open for 4% -> 4% of each run, Pallas kernels for 72% -> 71%
where the time goes in v5:
time: 435 us; the launch traced here: 427 us
  Pallas kernels  350 us (80%)
  waiting for transfers between devices  37.5 us (9%)
  local copies, waits for them, and re-layouts  15.5 us (4%)
  between operations  14.6 us (3%)
  other arithmetic  4.62 us (1%)
    pallas_call x8, Pallas kernels, remote_call(): pl.pallas_call(kernel, out_shape=outs, in_specs=[ANYWHERE if n in any_ins...  350 us
    all_gather x3, waiting for transfers between devices, z_ag(): return lax.all_gather(x, 'o', axis=0, tiled=True)  36.7 us
  transfers between devices with their start and end apart: 8, of which 1 were waited for; matrix products, arithmetic and copies ran while one was open for 4% of the time, Pallas kernels for 71%

profile of v5, /device:TPU:2, one launch (start us, length us, event | category | flops | bytes accessed | tf_op | source)
XLA Modules:
  0.0 427.1 jit_solution(3765166476414878247)
XLA Ops:
  7.2 1.8 collective-permute-start
  9.8 1.3 reshape.78
  11.5 0.7 copy.23
  12.6 1.0 reshape.81.down_src
  14.9 54.2 %shard_map.179 = (bf16[8,256,1536]{2,1,0:T(8,128)(2,1)}, bf16[8,48,256]{2,1,0:T(8,128)(2,1)}, bf16[8,48,512]{2,1,0:T(8,128)(2,1)}, f32[4,8,8,128]{3,2,1,0:T(8,12...) custom-call(bf16[256,1536]{1,0:T(8,128)(2,1)} %x_ref.5, ...), custom_call_target="tpu_custom_call" | custom-call | tf_op jit(solution)/shard_map/pallas_call | solution.py:334
  70.0 0.9 slice_bitcast_fusion
  71.7 39.3 %shard_map.180 = (bf16[2048,512]{1,0:T(8,128)(2,1)}, bf16[2048,256]{1,0:T(8,128)(2,1)}, f32[8,2048]{1,0:T(8,128)}, bf16[8,256,1536]{2,1,0:T(8,128)(2,1)}, bf16[2...) custom-call(bf16[2048,1536]{1,0:T(8,128)(2,1)} %bitcast.47, f32[2,1536]{1,0:T(2,128)} %reshape.83.gain_ref, ...), custom_call_target="tpu_custom_call" | custom-call | tf_op jit(solution)/shard_map/pallas_call | solution.py:334
  111.0 37.6 %shard_map.181 = (f32[256,1536]{1,0:T(8,128)}, bf16[256,1536]{1,0:T(8,128)(2,1)}) custom-call(bf16[2048,256]{1,0:T(8,128)(2,1)} %get-tuple-element.61.attn_ref.attn_hbm, bf16[1536,256]{1,0:T(8,128)(2,1)} %bitcast.49, bf16[256,1536]{1,0:T(8,128)(2,1)} %x_ref.5, f32[2,1536]{1,0:T(2,128)} %reshape.83.gain_ref), custom_call_target="tpu_custom_call" | custom-call | tf_op jit(solution)/shard_map/pallas_call | solution.py:334
  148.7 36.7 %all-gather.6.cloned.1.call-done = bf16[1024,1536]{1,0:T(8,128)(2,1)} async-done(((bf16[256,1536]{1,0:T(8,128)(2,1)}), bf16[1024,1536]{1,0:T(8,128)(2,1)}) %all-gather.6.cloned.1.call-update) | async-done | bytes 3145744 | tf_op jit(solution)/shard_map/all_gather | solution.py:44
  185.3 45.1 %shard_map.182 = (bf16[8,256,1536]{2,1,0:T(8,128)(2,1)}, bf16[2048,512]{1,0:T(8,128)(2,1)}, bf16[2048,1024]{1,0:T(8,128)(2,1)}, bf16[1024,2048]{1,0:T(8,128)(2,1)}, bf16[1536,512]{1,0:T(8,128)(2,1)}) custom-call(bf16[256,1536]{1,0:T(8,128)(2,1)} %get-tuple-element.63.x_ref, bf16[2048,1536]{1,0:T(8,128)(2,1)} %bitcast.48, bf16[4,256,1536]{2,1,0:T(8,128)(2,1)} %bitcast.42, ...), custom_call_target="tpu_custom_call" | custom-call | tf_op jit(solution)/shard_map/pallas_call | solution.py:334
  230.5 43.5 %shard_map.183 = (f32[256,1536]{1,0:T(8,128)}, bf16[256,1536]{1,0:T(8,128)(2,1)}, f32[8,1536]{1,0:T(8,128)}, bf16[1024,1536]{1,0:T(8,128)(2,1)}) custom-call(bf16[2048,1024]{1,0:T(8,128)(2,1)} %get-tuple-element.69.dgu_ref, bf16[4,256,1536]{2,1,0:T(8,128)(2,1)} %bitcast.43, f32[256,1536]{1,0:T(8,128)} %get-tuple-element.70.h_ref, bf16[256,1536]{1,0:T(8,128)(2,1)} %dy_ref.3, ...), custom_call_target="tpu_custom_call" | custom-call | tf_op jit(solution)/shard_map/pallas_call | solution.py:334
  274.5 31.8 %shard_map.184 = bf16[8,256,1536]{2,1,0:T(8,128)(2,1)} custom-call(bf16[256,1536]{1,0:T(8,128)(2,1)} %get-tuple-element.73.src), custom_call_target="tpu_custom_call" | custom-call | tf_op jit(solution)/shard_map/pallas_call | solution.py:334
  306.4 56.5 %shard_map.185 = (bf16[2048,512]{1,0:T(8,128)(2,1)}, bf16[256,1536]{1,0:T(8,128)(2,1)}, bf16[8,48,512]{2,1,0:T(8,128)(2,1)}, bf16[8,48,256]{2,1,0:T(8,128)(2,1)}, bf16[384,1536]{1,0:T(8,128)(2,1)}) custom-call(bf16[2048,1536]{1,0:T(8,128)(2,1)} %bitcast.41, bf16[2048,1536]{1,0:T(8,128)(2,1)} %get-tuple-element.76.xn_hbm, ...), custom_call_target="tpu_custom_call" | custom-call | tf_op jit(solution)/shard_map/pallas_call | solution.py:334
  362.9 0.9 slice_reduce_fusion
  363.9 1.6 multiply_reduce_fusion
  366.7 42.4 %shard_map.186 = (f32[256,1536]{1,0:T(8,128)}, f32[8,128]{1,0:T(8,128)}) custom-call(bf16[2048,512]{1,0:T(8,128)(2,1)} %get-tuple-element.85.d_ref, bf16[4,96,1536]{2,1,0:T(8,128)(2,1)} %bitcast.45, bf16[256,1536]{1,0:T(8,128)(2,1)} %x_ref.5, f32[256,1536]{1,0:T(8,128)} %get-tuple-element.86.dh_ref, f32[2,1536]{1,0:T(2,128)} %reshape.83.gain_ref, ...), custom_call_target="tpu_custom_call" | custom-call | tf_op jit(solution)/shard_map/pallas_call | solution.py:334
  409.2 1.8 collective-permute-start.1
  411.0 1.2 reshape.93
  413.2 1.3 copy.32
  414.5 1.3 convert_element_type.41
  415.8 1.3 slice_bitcast_fusion.1
  417.1 0.9 convert_element_type.38
  418.0 0.9 copy.42
  418.8 1.1 copy.43
  (63 shorter events, 7.5 us)
Async XLA Ops:
  7.2 5.0 %copy-start.4 = (bf16[48,4096]{1,0:T(8,128)(2,1)S(1)}, bf16[48,4096]{1,0:T(8,128)(2,1)}, u32[]{:S(2)}) copy-start(bf16[48,4096]{1,0:T(8,128)(2,1)} %param.18) | copy-start | bytes 1179652
  7.2 64.5 %all-gather.4.cloned.1.call-start = ((), (), s32[]{:S(2)}) async-start(), calls=%async_computation.3 | async-start | bytes 1474560 | tf_op jit(solution)/shard_map/all_gather | solution.py:44
  7.2 1.8 collective-permute-start
  9.0 0.7 copy-start.6
  9.7 139.0 %all-gather.8.cloned.1.call-start = ((), (), s32[]{:S(2)}) async-start(), calls=%async_computation.5 | async-start | bytes 1966080 | tf_op jit(solution)/shard_map/all_gather | solution.py:44
  11.1 2.5 copy-start.10
  11.1 2.5 copy-start.11
  11.1 3.2 copy-start.8
  11.1 3.2 copy-start.9
  69.1 116.3 %all-gather.6.cloned.1.call-start = ((), (), s32[]{:S(2)}) async-start(), calls=%async_computation.4 | async-start | bytes 3932160 | tf_op jit(solution)/shard_map/all_gather | solution.py:44
  69.8 236.5 %reduce-scatter.4.cloned.1.call-start = ((), (), s32[]{:S(2)}) async-start(), calls=%async_computation.6 | async-start | bytes 1966080 | tf_op jit(solution)/shard_map/reduce_scatter | solution.py:48
  230.5 132.4 %reduce-scatter.6.cloned.1.call-start = ((), (), s32[]{:S(2)}) async-start(), calls=%async_computation.7 | async-start | bytes 3932160 | tf_op jit(solution)/shard_map/reduce_scatter | solution.py:48
  274.1 135.1 %reduce-scatter.8.cloned.1.call-start = ((), (), s32[]{:S(2)}) async-start(), calls=%async_computation.8 | async-start | bytes 1474560 | tf_op jit(solution)/shard_map/reduce_scatter | solution.py:48
  306.3 57.5 %copy-start = (bf16[384,1536]{1,0:T(8,128)(2,1)S(1)}, bf16[384,1536]{1,0:T(8,128)(2,1)}, u32[]{:S(2)}) copy-start(bf16[384,1536]{1,0:T(8,128)(2,1)} %all-gather.4.cloned.1.call-done) | copy-start | bytes 3538948
  362.8 2.7 copy-start.7
  409.1 3.1 copy-start.5
  409.2 7.9 %collective-permute-start.1 = (bf16[96,1536]{1,0:T(8,128)(2,1)}, bf16[96,1536]{1,0:T(8,128)(2,1)S(1)}, u32[]{:S(2)}, u32[]{:S(2)}) collective-permute-start(bf16[96,1536]{1,0:T(8,128)(2,1)} %reduce-scatter.8.cloned.1.call-done), channel_id=1, source_target_pairs={{0,0},{8,1},{2,2},{10,3},{4,4},{12,5},{6,6},{14,7},{1,8},{9,9},{3,... | collective-permute-start | bytes 884744 | tf_op jit(solution)/shard_map/ppermute | solution.py:1226
  412.2 2.3 copy-start.3
  413.1 4.8 %copy-start.2 = (bf16[256,1536]{1,0:T(8,128)(2,1)S(1)}, bf16[256,1536]{1,0:T(8,128)(2,1)}, u32[]{:S(2)}) copy-start(bf16[256,1536]{1,0:T(8,128)(2,1)} %get-tuple-element.106) | copy-start | bytes 2359300
  414.5 4.4 %copy-start.1 = (f32[256,1536]{1,0:T(8,128)S(1)}, f32[256,1536]{1,0:T(8,128)}, u32[]{:S(2)}) copy-start(f32[256,1536]{1,0:T(8,128)} %get-tuple-element.107) | copy-start | bytes 4718596
Sparse Core Ops, SparseCore 0:
  10.1 40.9 all-gather.3
  69.2 51.2 all-gather.7
  122.1 63.2 all-gather.5
  230.6 34.1 reduce-scatter.3
  274.2 58.4 reduce-scatter.5
  363.0 31.4 reduce-scatter.7

commit v6 on v5

--- a/solution.py
+++ b/solution.py
@@ -713,10 +713,14 @@
         up_hbm,
         down_hbm,
         xn_all,
+        hidden_out,
+        dgu_out,
+        dgu_t_out,
+        g_down_ref,
         hidden_ref,
         dgu_ref,
         dgu_t,
-        g_down_ref,
+        out_sem,
         raw,
         dy_ref,
         up_ref,
@@ -769,6 +773,14 @@
             copy.start()
             stores.append(copy)
 
+        flushes = []
+
+        def flush(slot):
+            both = pl.ds(pl.multiple_of((slot - core) * rows, 2 * rows), 2 * rows)
+            pairs = [(hidden_ref.at[both], hidden_out.at[both]), (dgu_ref.at[both], dgu_out.at[both])]
+            pairs.append((dgu_t.at[:, both], dgu_t_out.at[:, both]))
+            flushes.append(Load(pairs, out_sem.at[len(flushes)]).begin())
+
         load.wait()
         gather.arrived(0)
         gather.own.wait()
@@ -780,24 +792,28 @@
         store(gather.s_x)
         store(gather.mates_slots[1])
         chip(gather.s_x)
+        flush(gather.me)
         gather.arrived(4)
         store(gather.s_y)
         store(gather.mates_slots[2])
         chip(gather.s_y)
+        flush(gather.s_x)
         gather.corner()
         gather.arrived(6)
         store(gather.s_d)
         store(gather.mates_slots[3])
         chip(gather.s_d)
+        flush(gather.s_y)
 
         @pl.loop(0, width // tile)
         def _(t):
             lanes = pl.ds(pl.multiple_of(t * tile, tile), tile)
             g_down_ref[lanes] = jnp.transpose(g_acc[:, lanes]).astype(BF)
 
+        flush(gather.s_d)
         for copy in gather.copies.values():
             copy.wait_send()
-        for copy in stores:
+        for copy in stores + flushes:
             copy.wait()
 
     outs = [
@@ -808,6 +824,10 @@
         shape((width, units), BF),
     ]
     scratch = [
+        pltpu.VMEM((n * rows, units), BF),
+        pltpu.VMEM((n * rows, 2 * units), BF),
+        pltpu.VMEM((2 * units, n * rows), BF),
+        pltpu.SemaphoreType.DMA((4, 3)),
         pltpu.VMEM((n, rows, width), BF),
         pltpu.VMEM(dy.shape, BF),
         pltpu.VMEM(gate_up.shape, BF),
@@ -818,7 +838,7 @@
         pltpu.SemaphoreType.DMA((n,)),
     ]
     ins = [xn, dy, gate_up, down]
-    return remote_call(kernel, number, ins, outs, scratch + GATHER_SEMS, any_outs=(0,), any_ins=(1, 2, 3))
+    return remote_call(kernel, number, ins, outs, scratch + GATHER_SEMS, any_outs=(0, 1, 2, 3), any_ins=(1, 2, 3))
 
 
 def feed_forward_input(dgu, gate_up, h1, cotangent, gain, xn_all, dgu_t, n_ctx, number):
@@ -838,7 +858,9 @@
         dh_ref,
         dhb_ref,
         dgain_ref,
+        g_up_out,
         g_up_ref,
+        g_up_sem,
         w_ref,
         xn_ref,
         dgu_t_ref,
@@ -876,8 +898,10 @@
         load.wait()
         up_gradient(0, units // part)
         scatter.join()
+        flushes = [Load([(g_up_ref.at[pl.ds(0, units)], g_up_out.at[pl.ds(0, units)])], g_up_sem.at[0]).begin()]
         up_gradient(units // part, 2 * units // part)
         scatter.end()
+        flushes.append(Load([(g_up_ref.at[pl.ds(units, units)], g_up_out.at[pl.ds(units, units)])], g_up_sem.at[1]).begin())
         dgain_ref[...] = jnp.zeros_like(dgain_ref)
 
         def finish(r):
@@ -889,6 +913,8 @@
             dhb_ref[r] = dh.astype(BF)
 
         row_chunks(rows, 32, finish)
+        for copy in flushes:
+            copy.wait()
 
     outs = [
         shape((rows, width), F32),
@@ -897,6 +923,8 @@
         shape((2 * units, width), BF),
     ]
     scratch = [
+        pltpu.VMEM((2 * units, width), BF),
+        pltpu.SemaphoreType.DMA((2, 1)),
         pltpu.VMEM((chunks, unit_rows, width), BF),
         pltpu.VMEM(xn_all.shape, BF),
         pltpu.VMEM(dgu_t.shape, BF),
@@ -909,6 +937,7 @@
         [dgu, gate_up, h1, cotangent, gain, xn_all, dgu_t],
         outs,
         scratch + scatter_scratch(rows, width),
+        any_outs=(3,),
         any_ins=(1, 5, 6),
     )
 

time: 435 us -> 432 us (level)
  transfers between devices with their start and end apart: 8 -> 8, of which waited for: 1 -> 1; matrix products, arithmetic and copies ran while one was open for 4% -> 4% of each run, Pallas kernels for 71% -> 72%
where the time goes in v6:
time: 432 us; the launch traced here: 425 us
  Pallas kernels  348 us (81%)
  waiting for transfers between devices  37.5 us (9%)
  local copies, waits for them, and re-layouts  15.5 us (4%)
  between operations  14.6 us (3%)
  other arithmetic  4.62 us (1%)
  starting transfers between devices  4.32 us (1%)
    pallas_call x8, Pallas kernels, remote_call(): pl.pallas_call(kernel, out_shape=outs, in_specs=[ANYWHERE if n in any_ins...  348 us
    all_gather x3, waiting for transfers between devices, z_ag(): return lax.all_gather(x, 'o', axis=0, tiled=True)  36.7 us
  transfers between devices with their start and end apart: 8, of which 1 were waited for; matrix products, arithmetic and copies ran while one was open for 4% of the time, Pallas kernels for 72%

profile of v6, /device:TPU:2, one launch (start us, length us, event | category | flops | bytes accessed | tf_op | source)
XLA Modules:
  0.0 424.5 jit_solution(10470345956281467202)
XLA Ops:
  7.2 1.8 collective-permute-start
  9.8 1.3 reshape.78
  11.5 0.7 copy.23
  12.6 1.0 reshape.81.down_src
  14.9 54.2 %shard_map.179 = (bf16[8,256,1536]{2,1,0:T(8,128)(2,1)}, bf16[8,48,256]{2,1,0:T(8,128)(2,1)}, bf16[8,48,512]{2,1,0:T(8,128)(2,1)}, f32[4,8,8,128]{3,2,1,0:T(8,12...) custom-call(bf16[256,1536]{1,0:T(8,128)(2,1)} %x_ref.5, ...), custom_call_target="tpu_custom_call" | custom-call | tf_op jit(solution)/shard_map/pallas_call | solution.py:334
  70.0 0.9 slice_bitcast_fusion
  71.7 39.3 %shard_map.180 = (bf16[2048,512]{1,0:T(8,128)(2,1)}, bf16[2048,256]{1,0:T(8,128)(2,1)}, f32[8,2048]{1,0:T(8,128)}, bf16[8,256,1536]{2,1,0:T(8,128)(2,1)}, bf16[2...) custom-call(bf16[2048,1536]{1,0:T(8,128)(2,1)} %bitcast.47, f32[2,1536]{1,0:T(2,128)} %reshape.83.gain_ref, ...), custom_call_target="tpu_custom_call" | custom-call | tf_op jit(solution)/shard_map/pallas_call | solution.py:334
  111.0 37.6 %shard_map.181 = (f32[256,1536]{1,0:T(8,128)}, bf16[256,1536]{1,0:T(8,128)(2,1)}) custom-call(bf16[2048,256]{1,0:T(8,128)(2,1)} %get-tuple-element.61.attn_ref.attn_hbm, bf16[1536,256]{1,0:T(8,128)(2,1)} %bitcast.49, bf16[256,1536]{1,0:T(8,128)(2,1)} %x_ref.5, f32[2,1536]{1,0:T(2,128)} %reshape.83.gain_ref), custom_call_target="tpu_custom_call" | custom-call | tf_op jit(solution)/shard_map/pallas_call | solution.py:334
  148.7 36.7 %all-gather.6.cloned.1.call-done = bf16[1024,1536]{1,0:T(8,128)(2,1)} async-done(((bf16[256,1536]{1,0:T(8,128)(2,1)}), bf16[1024,1536]{1,0:T(8,128)(2,1)}) %all-gather.6.cloned.1.call-update) | async-done | bytes 3145744 | tf_op jit(solution)/shard_map/all_gather | solution.py:44
  185.3 43.3 %shard_map.182 = (bf16[8,256,1536]{2,1,0:T(8,128)(2,1)}, bf16[2048,512]{1,0:T(8,128)(2,1)}, bf16[2048,1024]{1,0:T(8,128)(2,1)}, bf16[1024,2048]{1,0:T(8,128)(2,1)}, bf16[1536,512]{1,0:T(8,128)(2,1)}) custom-call(bf16[256,1536]{1,0:T(8,128)(2,1)} %get-tuple-element.63.x_ref, bf16[2048,1536]{1,0:T(8,128)(2,1)} %bitcast.48, bf16[4,256,1536]{2,1,0:T(8,128)(2,1)} %bitcast.42, ...), custom_call_target="tpu_custom_call" | custom-call | tf_op jit(solution)/shard_map/pallas_call | solution.py:334
  228.7 42.8 %shard_map.183 = (f32[256,1536]{1,0:T(8,128)}, bf16[256,1536]{1,0:T(8,128)(2,1)}, f32[8,1536]{1,0:T(8,128)}, bf16[1024,1536]{1,0:T(8,128)(2,1)}) custom-call(bf16[2048,1024]{1,0:T(8,128)(2,1)} %get-tuple-element.69.dgu_ref, bf16[4,256,1536]{2,1,0:T(8,128)(2,1)} %bitcast.43, f32[256,1536]{1,0:T(8,128)} %get-tuple-element.70.h_ref, bf16[256,1536]{1,0:T(8,128)(2,1)} %dy_ref.3, ...), custom_call_target="tpu_custom_call" | custom-call | tf_op jit(solution)/shard_map/pallas_call | solution.py:334
  272.0 31.8 %shard_map.184 = bf16[8,256,1536]{2,1,0:T(8,128)(2,1)} custom-call(bf16[256,1536]{1,0:T(8,128)(2,1)} %get-tuple-element.73.src), custom_call_target="tpu_custom_call" | custom-call | tf_op jit(solution)/shard_map/pallas_call | solution.py:334
  303.8 56.5 %shard_map.185 = (bf16[2048,512]{1,0:T(8,128)(2,1)}, bf16[256,1536]{1,0:T(8,128)(2,1)}, bf16[8,48,512]{2,1,0:T(8,128)(2,1)}, bf16[8,48,256]{2,1,0:T(8,128)(2,1)}, bf16[384,1536]{1,0:T(8,128)(2,1)}) custom-call(bf16[2048,1536]{1,0:T(8,128)(2,1)} %bitcast.41, bf16[2048,1536]{1,0:T(8,128)(2,1)} %get-tuple-element.76.xn_hbm, ...), custom_call_target="tpu_custom_call" | custom-call | tf_op jit(solution)/shard_map/pallas_call | solution.py:334
  360.3 0.9 slice_reduce_fusion
  361.3 1.6 multiply_reduce_fusion
  364.1 42.5 %shard_map.186 = (f32[256,1536]{1,0:T(8,128)}, f32[8,128]{1,0:T(8,128)}) custom-call(bf16[2048,512]{1,0:T(8,128)(2,1)} %get-tuple-element.85.d_ref, bf16[4,96,1536]{2,1,0:T(8,128)(2,1)} %bitcast.45, bf16[256,1536]{1,0:T(8,128)(2,1)} %x_ref.5, f32[256,1536]{1,0:T(8,128)} %get-tuple-element.86.dh_ref, f32[2,1536]{1,0:T(2,128)} %reshape.83.gain_ref, ...), custom_call_target="tpu_custom_call" | custom-call | tf_op jit(solution)/shard_map/pallas_call | solution.py:334
  406.7 1.8 collective-permute-start.1
  408.5 1.2 reshape.93
  410.6 1.3 copy.32
  412.0 1.3 convert_element_type.41
  413.3 1.3 slice_bitcast_fusion.1
  414.6 0.9 convert_element_type.38
  415.4 0.9 copy.42
  416.3 1.1 copy.43
  (63 shorter events, 7.5 us)
Async XLA Ops:
  7.2 5.0 %copy-start.4 = (bf16[48,4096]{1,0:T(8,128)(2,1)S(1)}, bf16[48,4096]{1,0:T(8,128)(2,1)}, u32[]{:S(2)}) copy-start(bf16[48,4096]{1,0:T(8,128)(2,1)} %param.18) | copy-start | bytes 1179652
  7.2 64.5 %all-gather.4.cloned.1.call-start = ((), (), s32[]{:S(2)}) async-start(), calls=%async_computation.3 | async-start | bytes 1474560 | tf_op jit(solution)/shard_map/all_gather | solution.py:44
  7.2 1.8 collective-permute-start
  9.0 0.7 copy-start.6
  9.7 139.0 %all-gather.8.cloned.1.call-start = ((), (), s32[]{:S(2)}) async-start(), calls=%async_computation.5 | async-start | bytes 1966080 | tf_op jit(solution)/shard_map/all_gather | solution.py:44
  11.1 2.5 copy-start.10
  11.1 2.5 copy-start.11
  11.1 3.2 copy-start.8
  11.1 3.2 copy-start.9
  69.1 116.3 %all-gather.6.cloned.1.call-start = ((), (), s32[]{:S(2)}) async-start(), calls=%async_computation.4 | async-start | bytes 3932160 | tf_op jit(solution)/shard_map/all_gather | solution.py:44
  69.8 233.9 %reduce-scatter.4.cloned.1.call-start = ((), (), s32[]{:S(2)}) async-start(), calls=%async_computation.6 | async-start | bytes 1966080 | tf_op jit(solution)/shard_map/reduce_scatter | solution.py:48
  228.7 131.7 %reduce-scatter.6.cloned.1.call-start = ((), (), s32[]{:S(2)}) async-start(), calls=%async_computation.7 | async-start | bytes 3932160 | tf_op jit(solution)/shard_map/reduce_scatter | solution.py:48
  271.5 135.1 %reduce-scatter.8.cloned.1.call-start = ((), (), s32[]{:S(2)}) async-start(), calls=%async_computation.8 | async-start | bytes 1474560 | tf_op jit(solution)/shard_map/reduce_scatter | solution.py:48
  303.8 57.5 %copy-start = (bf16[384,1536]{1,0:T(8,128)(2,1)S(1)}, bf16[384,1536]{1,0:T(8,128)(2,1)}, u32[]{:S(2)}) copy-start(bf16[384,1536]{1,0:T(8,128)(2,1)} %all-gather.4.cloned.1.call-done) | copy-start | bytes 3538948
  360.3 2.7 copy-start.7
  406.6 3.1 copy-start.5
  406.7 7.9 %collective-permute-start.1 = (bf16[96,1536]{1,0:T(8,128)(2,1)}, bf16[96,1536]{1,0:T(8,128)(2,1)S(1)}, u32[]{:S(2)}, u32[]{:S(2)}) collective-permute-start(bf16[96,1536]{1,0:T(8,128)(2,1)} %reduce-scatter.8.cloned.1.call-done), channel_id=1, source_target_pairs={{0,0},{8,1},{2,2},{10,3},{4,4},{12,5},{6,6},{14,7},{1,8},{9,9},{3,... | collective-permute-start | bytes 884744 | tf_op jit(solution)/shard_map/ppermute | solution.py:1255
  409.7 2.3 copy-start.3
  410.6 4.8 %copy-start.2 = (bf16[256,1536]{1,0:T(8,128)(2,1)S(1)}, bf16[256,1536]{1,0:T(8,128)(2,1)}, u32[]{:S(2)}) copy-start(bf16[256,1536]{1,0:T(8,128)(2,1)} %get-tuple-element.106) | copy-start | bytes 2359300
  412.0 4.4 %copy-start.1 = (f32[256,1536]{1,0:T(8,128)S(1)}, f32[256,1536]{1,0:T(8,128)}, u32[]{:S(2)}) copy-start(f32[256,1536]{1,0:T(8,128)} %get-tuple-element.107) | copy-start | bytes 4718596
Sparse Core Ops, SparseCore 0:
  10.1 40.9 all-gather.3
  69.2 51.2 all-gather.7
  122.1 63.2 all-gather.5
  228.8 34.1 reduce-scatter.3
  271.6 58.4 reduce-scatter.5
  360.5 31.5 reduce-scatter.7
